TPU v7x, 256 devices: a whole 4x4x8 slice. The times are simulated.
256 devices in a mesh: gx: 8 (over z_lo, core), gy: 4 (over y), gz: 8 (over z_hi, x).
Axes of the slice: x: 4, y: 4, z: 8 (z_hi: 2, z_lo: 4; z = z_hi * 4 + z_lo), core: 2. Of those that a mesh axis runs over, the one named last changes fastest.
Arguments:
- raw_weight: float32 [128, 27, 128], P(('gx', 'gy')), may hold values from -6 to 6
- inputs: bfloat16 [64, 64, 128, 128], P('gx', 'gy', 'gz'), may hold values from -6 to 6
- cotangent: bfloat16 [64, 64, 128, 128], P('gx', 'gy', 'gz'), may hold values from -0.099609375 to 0.099609375
Outputs:
- input_grad: bfloat16 [64, 64, 128, 128], P('gx', 'gy', 'gz')
- weight_grad: float32 [128, 27, 128], P(('gx', 'gy'))
All inputs are finite; a program needn't handle non-finite values.
Results may differ from a plain program's by a relative error of at most 0.0049.
Values may be sent and summed in bfloat16 or wider, within the bound.
No kernel may reach another device: no remote copies, remote signals or barrier semaphores. Data moves between devices by JAX's collectives and lax.ppermute only.
A program may use at most 64 MiB of HBM per device.

v0:
```python
import jax
import jax.numpy as jnp
from jax import lax
from jax.experimental import pallas as pl
from jax.experimental.pallas import tpu as pltpu
from jax.sharding import PartitionSpec as P


var_eps = 1e-05
norm_eps = 1e-06
clip_norm = 600.0
AXES = ("gx", "gy", "gz")
CORES = 2
TAPS = 27
MIB = 1024 * 1024


def call(kernel, out_shape, args, scalars=0, vmem=8, flops=1_000_000_000):
    spaces = [pltpu.SMEM] * scalars + [pltpu.VMEM] * (len(args) - scalars)
    many = isinstance(out_shape, tuple)
    return pl.pallas_call(
        kernel,
        out_shape=out_shape,
        in_specs=[pl.BlockSpec(memory_space=s) for s in spaces],
        out_specs=tuple(pl.BlockSpec(memory_space=pltpu.VMEM) for _ in out_shape)
        if many
        else pl.BlockSpec(memory_space=pltpu.VMEM),
        compiler_params=pltpu.CompilerParams(vmem_limit_bytes=vmem * MIB),
        cost_estimate=pl.CostEstimate(flops=flops, bytes_accessed=1_000_000, transcendentals=0),
    )(*args)


def of(shape, dtype):
    return jax.ShapeDtypeStruct(shape, dtype)


class Layout:
    def __init__(self, mesh):
        self.gx, self.gy, self.gz = (mesh.shape[a] for a in AXES)
        self.zl = self.gx // CORES
        self.x = self.zl
        self.zh = self.gz // self.x

    def spots(self):
        for zl in range(self.zl):
            for core in range(CORES):
                for y in range(self.gy):
                    for zh in range(self.zh):
                        for x in range(self.x):
                            yield dict(zl=zl, core=core, y=y, zh=zh, x=x)

    def index(self, s):
        return ((s["zl"] * CORES + s["core"]) * self.gy + s["y"]) * self.gz + s["zh"] * self.x + s["x"]

    def send(self, array, target):
        pairs = []
        for s in self.spots():
            t = dict(s)
            t.update(target(s))
            pairs.append((self.index(s), self.index(t)))
        return lax.ppermute(array, AXES, pairs)

    def exchange(self, array, fixed, order):
        groups = {}
        for s in self.spots():
            groups.setdefault(tuple(s[k] for k in fixed), []).append((order(s), self.index(s)))
        groups = [[i for _, i in sorted(g)] for g in groups.values()]
        return lax.all_to_all(array, AXES, 0, 0, tiled=True, axis_index_groups=groups)


def shift(array, axis, step):
    count = lax.axis_size(axis)
    if step > 0:
        pairs = [(i, i + 1) for i in range(count - 1)]
    else:
        pairs = [(i + 1, i) for i in range(count - 1)]
    return lax.ppermute(array, axis, pairs)


def wide(row, taps=TAPS):
    return jnp.concatenate([row] * taps, axis=1)


def fold(values, ch):
    total = values[:, 0:ch]
    for t in range(1, values.shape[1] // ch):
        total = total + values[:, t * ch : (t + 1) * ch]
    return jnp.sum(total, axis=0, keepdims=True)


def base_kernel(raw_ref, held_ref):
    taps, rows, ch = raw_ref.shape
    base = jnp.sum(jnp.sum(raw_ref[...], axis=0), axis=0, keepdims=True) / (taps * rows)
    high = base.astype(jnp.bfloat16)
    low = (base - high.astype(jnp.float32)).astype(jnp.bfloat16)
    base = high.astype(jnp.float32) + low.astype(jnp.float32)
    for t in range(taps):
        held_ref[0, :, t * ch : (t + 1) * ch] = (raw_ref[t] - base).astype(jnp.bfloat16)
    place = lax.broadcasted_iota(jnp.int32, (rows, ch), 0)
    both = jnp.where(place == 0, high.astype(jnp.float32), low.astype(jnp.float32))
    held_ref[0, :, taps * ch :] = both.astype(jnp.bfloat16)


def filter_kernel(core_ref, mid_ref, xl_ref, xh_ref, yl_ref, yh_ref, zl_ref, zh_ref, in_ref, taps_ref, keep_ref, send_ref):
    nx, ny, nz, ch = mid_ref.shape

    def fill(k, rows, j, n):
        mid = rows.astype(jnp.float32)
        low = zl_ref[k, j : j + n].astype(jnp.float32)[:, None, :]
        high = zh_ref[k, j : j + n].astype(jnp.float32)[:, None, :]
        up = jnp.concatenate([mid[:, 1:], high], axis=1)
        down = jnp.concatenate([low, mid[:, :-1]], axis=1)
        taps_ref[k, j : j + n, :, 0:ch] = up.astype(jnp.bfloat16)
        taps_ref[k, j : j + n, :, ch : 2 * ch] = rows
        taps_ref[k, j : j + n, :, 2 * ch : 3 * ch] = down.astype(jnp.bfloat16)

    def plane(k, carry):
        fill(k, yl_ref[k][None], 0, 1)
        fill(k, yh_ref[k][None], ny + 1, 1)
        return carry

    def middle(k, carry):
        fill(k + 1, mid_ref[k], 1, ny)
        return carry

    lax.fori_loop(0, nx, middle, 0)
    fill(0, xl_ref[0], 1, ny)
    fill(nx + 1, xh_ref[0], 1, ny)
    lax.fori_loop(0, nx + 2, plane, 0)
    cells = nx * ny * nz
    flat = in_ref[...].T
    core = core_ref[0]
    for a in range(3):
        for b in range(3):
            view = taps_ref[2 - a : 2 - a + nx, 2 - b : 2 - b + ny].reshape(cells, 3 * ch)
            res = jnp.dot(flat, view, preferred_element_type=jnp.float32)
            lanes = pl.ds((a * 3 + b) * 3 * ch, 3 * ch)
            for g in range(ch // 32):
                first = res[g * 32 : g * 32 + 16]
                second = res[g * 32 + 16 : g * 32 + 32]
                keep_ref[g * 16 : g * 16 + 16, lanes] = jnp.where(core == 0, first, second)
                send_ref[g * 16 : g * 16 + 16, lanes] = jnp.where(core == 0, second, first).astype(jnp.bfloat16)


def pair_kernel(keep_ref, other_ref, out_ref):
    rows = out_ref.shape[1]
    for g in range(keep_ref.shape[0] // 16):
        total = keep_ref[g * 16 : g * 16 + 16] + other_ref[g * 16 : g * 16 + 16].astype(jnp.float32)
        for r in range(16 // rows):
            out_ref[g * (16 // rows) + r] = total[r * rows : (r + 1) * rows].astype(jnp.bfloat16)


def peers_kernel(parts_ref, out_ref):
    total = jnp.sum(parts_ref[...].astype(jnp.float32), axis=0).astype(jnp.bfloat16)
    for k in range(out_ref.shape[0]):
        out_ref[k] = total


def block_kernel(parts_ref, std_ref, grad_ref, sums_ref):
    ch = sums_ref.shape[2] // 3
    total = jnp.sum(parts_ref[...].astype(jnp.float32), axis=0)
    grad_ref[...] = total
    three = jnp.concatenate([fold(total, ch), fold(total * std_ref[...], ch), fold(total * total, ch)], axis=1)
    for k in range(sums_ref.shape[0]):
        sums_ref[k] = three


def input_kernel(taps_ref, std_ref, out_ref):
    nx, ny, nz, ch = out_ref.shape
    planes = 2
    std = std_ref[...]
    for x in range(0, nx, planes):
        rows = jnp.concatenate(
            [
                taps_ref[x + 2 - a : x + 2 - a + planes, 2 - b : 2 - b + ny].reshape(planes * ny * nz, 3 * ch)
                for a in range(3)
                for b in range(3)
            ],
            axis=1,
        )
        res = lax.dot_general(rows, std, (((1,), (1,)), ((), ())), preferred_element_type=jnp.float32)
        out_ref[x : x + planes] = res.astype(jnp.bfloat16).reshape(planes, ny, nz, ch)


def std_kernel(spot_ref, near_ref, far_ref, std_ref, mean_ref, inv_ref, block_ref):
    slots, rows, held = near_ref.shape
    ch = inv_ref.shape[1]
    width = held - ch
    taps = width // ch
    y, zl, core, x = spot_ref[0], spot_ref[1], spot_ref[2], spot_ref[3]
    blocks = [(b // 8, (b // 4) % 2, b % 4) for b in range(2 * slots)]
    count = float(2 * slots * rows * taps)

    def parts(zl_b, core_b, y_b):
        slot = (y_b ^ y) + 4 * (zl_b ^ zl)
        data = jnp.where(core_b == core, near_ref[slot], far_ref[slot]).astype(jnp.float32)
        return data[:, :width], data[0:1, width:] + data[1:2, width:]

    total = jnp.zeros((1, ch), jnp.float32)
    for b in blocks:
        values, base = parts(*b)
        total = total + (fold(values, ch) + float(rows * taps) * base)
    mean = total / count
    square = jnp.zeros((1, ch), jnp.float32)
    for b in blocks:
        values, base = parts(*b)
        first = values + wide(base - mean)
        square = square + fold(first * first, ch)
    inv = lax.rsqrt(square / count + var_eps)
    mean_ref[...] = mean
    inv_ref[...] = inv
    inv_wide = wide(inv)
    for n, b in enumerate(blocks):
        values, base = parts(*b)
        std_ref[n * rows : (n + 1) * rows, :] = ((values + wide(base - mean)) * inv_wide).astype(jnp.bfloat16)
    values, base = parts(x, core, y)
    block_ref[...] = (values + wide(base - mean)) * inv_wide


def last_kernel(fan_count, grad_ref, raw_ref, mean_ref, inv_ref, sums_ref, out_ref):
    taps, _, ch = raw_ref.shape
    sums = jnp.sum(sums_ref[...], axis=0)
    sum_grad, sum_cross, sum_square = sums[:, :ch], sums[:, ch : 2 * ch], sums[:, 2 * ch :]
    mean, inv = mean_ref[...], inv_ref[...]
    mean_grad = sum_grad / fan_count
    mean_cross = sum_cross / fan_count
    shrink = 1.0 - var_eps * inv * inv
    per_output = sum_square - 2.0 * mean_grad * sum_grad - 2.0 * mean_cross * sum_cross
    per_output = per_output + fan_count * mean_grad * mean_grad + fan_count * mean_cross * mean_cross * shrink
    square_sum = jnp.sum(inv * inv * per_output, axis=1, keepdims=True)
    scale = jnp.minimum(1.0, clip_norm * lax.rsqrt(square_sum + norm_eps))
    factor = inv * scale
    for t in range(taps):
        std = (raw_ref[t] - mean) * inv
        out_ref[t] = factor * (grad_ref[:, t * ch : (t + 1) * ch] - mean_grad - std * mean_cross)


def on_device(where, raw_weight, inputs, cotangent):
    nx, ny, nz, ch = inputs.shape
    rows, taps = raw_weight.shape[:2]
    width = taps * ch
    bf16, f32 = jnp.bfloat16, jnp.float32
    gx, gy, gz = (lax.axis_index(a).astype(jnp.int32) for a in AXES)
    core, zl, x = gx & 1, gx >> 1, gz & (where.x - 1)
    spot = jnp.stack([gy, zl, core, x])
    raw = jnp.transpose(raw_weight, (1, 0, 2))

    x_low = shift(cotangent[-1:], "gx", 1)
    x_high = shift(cotangent[:1], "gx", -1)
    held = call(base_kernel, of((1, rows, width + ch), bf16), (raw,))
    held = jnp.concatenate([held, where.send(held, lambda s: dict(y=s["y"] ^ 1))], 0)
    y_low = shift(jnp.concatenate([a[:, -1] for a in (x_low, cotangent, x_high)], 0), "gy", 1)
    y_high = shift(jnp.concatenate([a[:, 0] for a in (x_low, cotangent, x_high)], 0), "gy", -1)
    held = jnp.concatenate([held, where.send(held, lambda s: dict(y=s["y"] ^ 2))], 0)

    def face(k):
        deep = jnp.concatenate([a[:, :, k] for a in (x_low, cotangent, x_high)], 0)
        return jnp.concatenate([y_low[:, None, k], deep, y_high[:, None, k]], 1)

    z_low = shift(face(nz - 1), "gz", 1)
    z_high = shift(face(0), "gz", -1)
    held = jnp.concatenate([held, where.send(held, lambda s: dict(zl=s["zl"] ^ 1))], 0)

    flops = 2 * nx * ny * nz * ch * width
    tap_views, keep, send = call(
        filter_kernel,
        (of((nx + 2, ny + 2, nz, 3 * ch), bf16), of((ch // 2, width), f32), of((ch // 2, width), bf16)),
        (core[None], cotangent, x_low, x_high, y_low, y_high, z_low, z_high, inputs.reshape(-1, ch)),
        scalars=1,
        vmem=16,
        flops=2 * flops,
    )
    other = where.send(send, lambda s: dict(core=1 - s["core"]))
    held = jnp.concatenate([held, where.send(held, lambda s: dict(zl=s["zl"] ^ 2))], 0)
    peers = where.x * where.gy
    half = call(pair_kernel, of((peers, rows, width), bf16), (keep, other))
    parts = where.exchange(half, ("core", "zl", "zh"), lambda s: (s["x"], s["y"]))
    far = where.send(held, lambda s: dict(core=1 - s["core"]))
    copies = call(peers_kernel, of((where.zl * where.zh, rows, width), bf16), (parts,))
    parts = where.exchange(copies, ("core", "x", "y"), lambda s: (s["zh"], s["zl"]))

    std_half, mean_out, inv_std, block_std = call(
        std_kernel,
        (of((ch, width), bf16), of((1, ch), f32), of((1, ch), f32), of((rows, width), f32)),
        (spot, held, far),
        scalars=1,
        flops=3_000_000_000,
    )
    everyone = CORES * where.x * where.gy
    block_grad, local = call(block_kernel, (of((rows, width), f32), of((everyone, 1, 3 * ch), f32)), (parts, block_std))
    filter_grad = where.send(block_grad, lambda s: dict(x=s["zl"], zl=s["x"]))
    sums = where.exchange(local, ("zl", "zh"), lambda s: (s["core"], s["x"], s["y"]))
    input_grad = call(input_kernel, of(inputs.shape, bf16), (tap_views, std_half), vmem=16, flops=2 * flops)

    def last(*refs):
        last_kernel(float(ch * taps), *refs)

    grad = call(last, of((taps, rows, ch), f32), (filter_grad, raw, mean_out, inv_std, sums))
    return (input_grad, jnp.transpose(grad, (1, 0, 2)))


def solution(mesh):
    where = Layout(mesh)
    in_specs = (P(("gx", "gy"), None, None), P("gx", "gy", "gz", None), P("gx", "gy", "gz", None))
    out_specs = (P("gx", "gy", "gz", None), P(("gx", "gy"), None, None))

    def body(raw_weight, inputs, cotangent):
        return on_device(where, raw_weight, inputs, cotangent)

    return jax.shard_map(body, mesh=mesh, in_specs=in_specs, out_specs=out_specs, check_vma=False)
```

profile of v0, /device:TPU:1, one launch (start us, length us, event | category | flops | bytes accessed | tf_op | source)
XLA Modules:
  0.0 100.1 jit_solution(14681647774651804731)
XLA Ops:
  0.6 0.9 fusion.1
  1.6 4.9 %collective-permute-start = (bf16[1,16,16,128]{3,2,1,0:T(8,128)(2,1)S(1)}, bf16[1,16,16,128]{3,2,1,0:T(8,128)(2,1)S(1)}, u32[]{:S(2)}, u32[]{:S(2)}) collective-permute-start(bf16[1,16,16,128]{3,2,1,0:T(8,128)(2,1)S(1)} %get-tuple-element.25), channel_id=1, source_target_pairs={{0,32},{32,64},{64,96},{96,128},{128,160},{160,192},{192,224},{1,3... | collective-permute-start | bytes 196616 | tf_op jit(solution)/shard_map/ppermute | solution.py:77
  6.5 1.9 %collective-permute-start.1 = (bf16[1,16,16,128]{3,2,1,0:T(8,128)(2,1)S(1)}, bf16[1,16,16,128]{3,2,1,0:T(8,128)(2,1)S(1)}, u32[]{:S(2)}, u32[]{:S(2)}) collective-permute-start(bf16[1,16,16,128]{3,2,1,0:T(8,128)(2,1)S(1)} %get-tuple-element.24), channel_id=1, source_target_pairs={{32,0},{64,32},{96,64},{128,96},{160,128},{192,160},{224,192},{33,... | collective-permute-start | bytes 196616 | tf_op jit(solution)/shard_map/ppermute | solution.py:77
  8.4 0.0 copy-start.2
  8.5 0.8 copy-done.2
  9.3 0.1 shard_map.51
  9.3 1.4 %collective-permute-start.6 = (bf16[1,4,3584]{2,1,0:T(4,128)(2,1)S(1)}, bf16[1,4,3584]{2,1,0:T(4,128)(2,1)S(1)}, u32[]{:S(2)}, u32[]{:S(2)}) collective-permute-start(bf16[1,4,3584]{2,1,0:T(4,128)(2,1)S(1)} %shard_map.51), channel_id=1, source_target_pairs={{0,8},{1,9},{2,10},{3,11},{4,12},{5,13},{6,14},{7,15},{8,0},{9,1},... | collective-permute-start | bytes 86024 | tf_op jit(solution)/shard_map/ppermute | solution.py:61
  10.7 0.1 fusion
  10.9 1.2 %collective-permute-done.6 = bf16[1,4,3584]{2,1,0:T(4,128)(2,1)S(1)} collective-permute-done((bf16[1,4,3584]{2,1,0:T(4,128)(2,1)S(1)}, bf16[1,4,3584]{2,1,0:T(4,128)(2,1)S(1)}, u32[]{:S(2)}, u32[]{:S(2)}) %collective-permute-start.6) | collective-permute-done | bytes 28704 | tf_op jit(solution)/shard_map/ppermute | solution.py:61
  12.2 3.0 %collective-permute-start.7 = (bf16[2,4,3584]{2,1,0:T(4,128)(2,1)S(1)}, bf16[2,4,3584]{2,1,0:T(4,128)(2,1)S(1)}, u32[]{:S(2)}, u32[]{:S(2)}) collective-permute-start(bf16[2,4,3584]{2,1,0:T(4,128)(2,1)S(1)} %pad_maximum_fusion.4), channel_id=1, source_target_pairs={{0,16},{1,17},{2,18},{3,19},{4,20},{5,21},{6,22},{7,23},{8,24},{9,... | collective-permute-start | bytes 172040 | tf_op jit(solution)/shard_map/ppermute | solution.py:61
  15.2 0.0 collective-permute-done.xl_ref
  15.2 0.0 collective-permute-done.1.xh_ref
  15.3 1.3 %collective-permute-start.3 = (bf16[10,16,128]{2,1,0:T(8,128)(2,1)S(1)}, bf16[10,16,128]{2,1,0:T(8,128)(2,1)S(1)}, u32[]{:S(2)}, u32[]{:S(2)}) collective-permute-start(bf16[10,16,128]{2,1,0:T(8,128)(2,1)S(1)} %pad_maximum_fusion.6), channel_id=1, source_target_pairs={{8,0},{16,8},{24,16},{9,1},{17,9},{25,17},{10,2},{18,10},{26,18},{... | collective-permute-start | bytes 122888 | tf_op jit(solution)/shard_map/ppermute | solution.py:77
  16.6 4.0 %collective-permute-start.2 = (bf16[10,16,128]{2,1,0:T(8,128)(2,1)S(1)}, bf16[10,16,128]{2,1,0:T(8,128)(2,1)S(1)}, u32[]{:S(2)}, u32[]{:S(2)}) collective-permute-start(bf16[10,16,128]{2,1,0:T(8,128)(2,1)S(1)} %pad_maximum_fusion.5), channel_id=1, source_target_pairs={{0,8},{8,16},{16,24},{1,9},{9,17},{17,25},{2,10},{10,18},{18,26},{... | collective-permute-start | bytes 122888 | tf_op jit(solution)/shard_map/ppermute | solution.py:77
  20.6 0.0 collective-permute-done.7
  20.7 0.1 pad_maximum_fusion.1
  20.7 1.7 %collective-permute-start.8 = (bf16[4,4,3584]{2,1,0:T(4,128)(2,1)S(1)}, bf16[4,4,3584]{2,1,0:T(4,128)(2,1)S(1)}, u32[]{:S(2)}, u32[]{:S(2)}) collective-permute-start(bf16[4,4,3584]{2,1,0:T(4,128)(2,1)S(1)} %pad_maximum_fusion.1), channel_id=1, source_target_pairs={{0,64},{1,65},{2,66},{3,67},{4,68},{5,69},{6,70},{7,71},{8,72},{9,... | collective-permute-start | bytes 344072 | tf_op jit(solution)/shard_map/ppermute | solution.py:61
  22.5 0.0 collective-permute-done.3.yh_ref
  22.6 1.3 %collective-permute-start.5 = (bf16[10,18,128]{2,1,0:T(8,128)(2,1)S(1)}, bf16[10,18,128]{2,1,0:T(8,128)(2,1)S(1)}, u32[]{:S(2)}, u32[]{:S(2)}) collective-permute-start(bf16[10,18,128]{2,1,0:T(8,128)(2,1)S(1)} %pad_maximum_fusion.3), channel_id=1, source_target_pairs={{1,0},{2,1},{3,2},{4,3},{5,4},{6,5},{7,6},{9,8},{10,9},{11,10},{12... | collective-permute-start | bytes 138248 | tf_op jit(solution)/shard_map/ppermute | solution.py:77
  23.9 4.0 %collective-permute-start.4 = (bf16[10,18,128]{2,1,0:T(8,128)(2,1)S(1)}, bf16[10,18,128]{2,1,0:T(8,128)(2,1)S(1)}, u32[]{:S(2)}, u32[]{:S(2)}) collective-permute-start(bf16[10,18,128]{2,1,0:T(8,128)(2,1)S(1)} %pad_maximum_fusion.2), channel_id=1, source_target_pairs={{0,1},{1,2},{2,3},{3,4},{4,5},{5,6},{6,7},{8,9},{9,10},{10,11},{11... | collective-permute-start | bytes 138248 | tf_op jit(solution)/shard_map/ppermute | solution.py:77
  27.9 0.0 collective-permute-done.5.zh_ref
  27.9 1.2 %collective-permute-done.4.zl_ref = bf16[10,18,128]{2,1,0:T(8,128)(2,1)S(1)} collective-permute-done((bf16[10,18,128]{2,1,0:T(8,128)(2,1)S(1)}, bf16[10,18,128]{2,1,0:T(8,128)(2,1)S(1)}, u32[]{:S(2)}, u32[]{:S(2)}) %collective-permute-start.4) | collective-permute-done | bytes 46112 | tf_op jit(solution)/shard_map/ppermute | solution.py:77
  29.2 3.3 %shard_map.50 = (bf16[10,18,16,384]{3,2,1,0:T(8,128)(2,1)S(1)}, f32[64,3456]{1,0:T(8,128)S(1)}, bf16[64,3456]{1,0:T(8,128)(2,1)S(1)}) custom-call(s32[1]{0:T(128)} %bitcast.core_ref, bf16[8,16,16,128]{3,2,1,0:T(8,128)(2,1)S(1)} %copy-done, bf16[1,16,16,128]{3,2,1,0:T(8,128)(2,1)S(1)} %collective-permute-done.xl_ref, ...), custom_call_target="tpu_custom_call" | custom-call | flops 3623878656 | bytes 1000000 | tf_op jit(solution)/shard_map/pallas_call | solution.py:21
  32.5 1.4 %copy-done.4 = bf16[10,18,16,384]{3,2,1,0:T(8,128)(2,1)} copy-done((bf16[10,18,16,384]{3,2,1,0:T(8,128)(2,1)}, bf16[10,18,16,384]{3,2,1,0:T(8,128)(2,1)S(1)}, u32[]{:S(2)}) %copy-start.4) | copy-done | bytes 2211864
  33.9 3.6 %collective-permute-start.11 = (bf16[64,3456]{1,0:T(8,128)(2,1)S(1)}, bf16[64,3456]{1,0:T(8,128)(2,1)S(1)}, u32[]{:S(2)}, u32[]{:S(2)}) collective-permute-start(bf16[64,3456]{1,0:T(8,128)(2,1)S(1)} %get-tuple-element.14), channel_id=1, source_target_pairs={{0,32},{1,33},{2,34},{3,35},{4,36},{5,37},{6,38},{7,39},{8,40},{9,... | collective-permute-start | bytes 1327112 | tf_op jit(solution)/shard_map/ppermute | solution.py:61
  37.5 0.0 collective-permute-done.8
  37.5 0.2 pad_maximum_fusion
  37.7 3.1 %collective-permute-start.9 = (bf16[8,4,3584]{2,1,0:T(4,128)(2,1)S(1)}, bf16[8,4,3584]{2,1,0:T(4,128)(2,1)S(1)}, u32[]{:S(2)}, u32[]{:S(2)}) collective-permute-start(bf16[8,4,3584]{2,1,0:T(4,128)(2,1)S(1)} %pad_maximum_fusion), channel_id=1, source_target_pairs={{0,128},{1,129},{2,130},{3,131},{4,132},{5,133},{6,134},{7,135},{8... | collective-permute-start | bytes 688136 | tf_op jit(solution)/shard_map/ppermute | solution.py:61
  40.8 0.1 constant_dynamic-update-slice_fusion.1
  40.8 0.9 shard_map.54
  41.7 11.8 %all-to-all-start = ((bf16[16,4,3456]{2,1,0:T(4,128)(2,1)}), bf16[16,4,3456]{2,1,0:T(4,128)(2,1)S(1)}, u32[]{:S(2)}, u32[]{:S(2)}) async-start(bf16[16,4,3456]{2,1,0:T(4,128)(2,1)} %shard_map.54), calls=%async_computation | async-start | bytes 884736 | tf_op jit(solution)/shard_map/all_to_all | solution.py:68
  53.5 0.0 collective-permute-done.9
  53.5 0.1 constant_dynamic-update-slice_fusion.near_ref
  53.6 0.7 collective-permute-start.10
  54.3 9.0 %all-to-all-done.parts_ref = bf16[16,4,3456]{2,1,0:T(4,128)(2,1)S(1)} async-done(((bf16[16,4,3456]{2,1,0:T(4,128)(2,1)}), bf16[16,4,3456]{2,1,0:T(4,128)(2,1)S(1)}, u32[]{:S(2)}, u32[]{:S(2)}) %all-to-all-start) | async-done | bytes 442400 | tf_op jit(solution)/shard_map/all_to_all | solution.py:68
  63.3 0.9 shard_map.55
  64.2 8.0 %all-to-all-start.1 = ((bf16[8,4,3456]{2,1,0:T(4,128)(2,1)}), bf16[8,4,3456]{2,1,0:T(4,128)(2,1)S(1)}, u32[]{:S(2)}, u32[]{:S(2)}) async-start(bf16[8,4,3456]{2,1,0:T(4,128)(2,1)} %shard_map.55), calls=%async_computation.1 | async-start | bytes 442368 | tf_op jit(solution)/shard_map/all_to_all | solution.py:68
  72.2 0.1 pad_add_fusion.spot_ref
  72.2 1.6 %shard_map.52 = (bf16[128,3456]{1,0:T(8,128)(2,1)S(1)}, f32[1,128]{1,0:T(1,128)S(1)}, f32[1,128]{1,0:T(1,128)S(1)}, f32[4,3456]{1,0:T(4,128)S(1)}) custom-call(s32[4]{0:T(128)S(1)} %pad_add_fusion.spot_ref, bf16[16,4,3584]{2,1,0:T(4,128)(2,1)S(1)} %constant_dynamic-update-slice_fusion.near_ref, bf16[16,4,3584]{2,1,0:T(4,128)(2,1)S(1)} %collective-permute-done.10.far_ref), custom_call_target="tpu_custom_call" | custom-call | flops 3000000000 | bytes 1000000 | tf_op jit(solution)/shard_map/pallas_call | solution.py:21
  73.9 7.1 %all-to-all-done.1.parts_ref = bf16[8,4,3456]{2,1,0:T(4,128)(2,1)S(1)} async-done(((bf16[8,4,3456]{2,1,0:T(4,128)(2,1)}), bf16[8,4,3456]{2,1,0:T(4,128)(2,1)S(1)}, u32[]{:S(2)}, u32[]{:S(2)}) %all-to-all-start.1) | async-done | bytes 221216 | tf_op jit(solution)/shard_map/all_to_all | solution.py:68
  81.0 0.8 shard_map.56
  81.7 0.7 collective-permute-start.12
  82.4 9.8 %all-to-all-start.2 = ((f32[32,1,384]{2,1,0:T(1,128)}), f32[32,1,384]{2,1,0:T(1,128)S(1)}, u32[]{:S(2)}, u32[]{:S(2)}) async-start(f32[32,1,384]{2,1,0:T(1,128)} %get-tuple-element.19), calls=%async_computation.2 | async-start | bytes 98304 | tf_op jit(solution)/shard_map/all_to_all | solution.py:68
  92.2 0.0 copy-start.3
  92.2 4.6 %shard_map.53 = bf16[8,16,16,128]{3,2,1,0:T(8,128)(2,1)} custom-call(bf16[10,18,16,384]{3,2,1,0:T(8,128)(2,1)S(1)} %copy-done.5, bf16[128,3456]{1,0:T(8,128)(2,1)S(1)} %get-tuple-element.12.std_ref), custom_call_target="tpu_custom_call" | custom-call | flops 3623878656 | bytes 1000000 | tf_op jit(solution)/shard_map/pallas_call | solution.py:21
  96.8 2.4 %all-to-all-done.2.refs_4_ = f32[32,1,384]{2,1,0:T(1,128)S(1)} async-done(((f32[32,1,384]{2,1,0:T(1,128)}), f32[32,1,384]{2,1,0:T(1,128)S(1)}, u32[]{:S(2)}, u32[]{:S(2)}) %all-to-all-start.2) | async-done | bytes 49184 | tf_op jit(solution)/shard_map/all_to_all | solution.py:68
  99.3 0.0 collective-permute-done.12.refs_0_
  99.3 0.8 shard_map.57
  (30 shorter events, 0.3 us)
Async XLA Ops:
  0.6 10.1 %copy-start = (bf16[8,16,16,128]{3,2,1,0:T(8,128)(2,1)S(1)}, bf16[8,16,16,128]{3,2,1,0:T(8,128)(2,1)}, u32[]{:S(2)}) copy-start(bf16[8,16,16,128]{3,2,1,0:T(8,128)(2,1)} %mid_ref.1) | copy-start | bytes 1572868
  1.6 13.6 %collective-permute-start = (bf16[1,16,16,128]{3,2,1,0:T(8,128)(2,1)S(1)}, bf16[1,16,16,128]{3,2,1,0:T(8,128)(2,1)S(1)}, u32[]{:S(2)}, u32[]{:S(2)}) collective-permute-start(bf16[1,16,16,128]{3,2,1,0:T(8,128)(2,1)S(1)} %get-tuple-element.25), channel_id=1, source_target_pairs={{0,32},{32,64},{64,96},{96,128},{128,160},{160,192},{192,224},{1,3... | collective-permute-start | bytes 196616 | tf_op jit(solution)/shard_map/ppermute | solution.py:77
  6.5 8.7 %collective-permute-start.1 = (bf16[1,16,16,128]{3,2,1,0:T(8,128)(2,1)S(1)}, bf16[1,16,16,128]{3,2,1,0:T(8,128)(2,1)S(1)}, u32[]{:S(2)}, u32[]{:S(2)}) collective-permute-start(bf16[1,16,16,128]{3,2,1,0:T(8,128)(2,1)S(1)} %get-tuple-element.24), channel_id=1, source_target_pairs={{32,0},{64,32},{96,64},{128,96},{160,128},{192,160},{224,192},{33,... | collective-permute-start | bytes 196616 | tf_op jit(solution)/shard_map/ppermute | solution.py:77
  8.4 0.8 copy-start.2
  9.3 19.9 %copy-start.1 = (bf16[8,16,16,128]{3,2,1,0:T(8,128)(2,1)S(1)}, bf16[8,16,16,128]{3,2,1,0:T(8,128)(2,1)}, u32[]{:S(2)}) copy-start(bf16[8,16,16,128]{3,2,1,0:T(8,128)(2,1)} %param.4) | copy-start | bytes 1572868
  9.3 2.8 %collective-permute-start.6 = (bf16[1,4,3584]{2,1,0:T(4,128)(2,1)S(1)}, bf16[1,4,3584]{2,1,0:T(4,128)(2,1)S(1)}, u32[]{:S(2)}, u32[]{:S(2)}) collective-permute-start(bf16[1,4,3584]{2,1,0:T(4,128)(2,1)S(1)} %shard_map.51), channel_id=1, source_target_pairs={{0,8},{1,9},{2,10},{3,11},{4,12},{5,13},{6,14},{7,15},{8,0},{9,1},... | collective-permute-start | bytes 86024 | tf_op jit(solution)/shard_map/ppermute | solution.py:61
  12.2 8.5 %collective-permute-start.7 = (bf16[2,4,3584]{2,1,0:T(4,128)(2,1)S(1)}, bf16[2,4,3584]{2,1,0:T(4,128)(2,1)S(1)}, u32[]{:S(2)}, u32[]{:S(2)}) collective-permute-start(bf16[2,4,3584]{2,1,0:T(4,128)(2,1)S(1)} %pad_maximum_fusion.4), channel_id=1, source_target_pairs={{0,16},{1,17},{2,18},{3,19},{4,20},{5,21},{6,22},{7,23},{8,24},{9,... | collective-permute-start | bytes 172040 | tf_op jit(solution)/shard_map/ppermute | solution.py:61
  15.3 7.2 %collective-permute-start.3 = (bf16[10,16,128]{2,1,0:T(8,128)(2,1)S(1)}, bf16[10,16,128]{2,1,0:T(8,128)(2,1)S(1)}, u32[]{:S(2)}, u32[]{:S(2)}) collective-permute-start(bf16[10,16,128]{2,1,0:T(8,128)(2,1)S(1)} %pad_maximum_fusion.6), channel_id=1, source_target_pairs={{8,0},{16,8},{24,16},{9,1},{17,9},{25,17},{10,2},{18,10},{26,18},{... | collective-permute-start | bytes 122888 | tf_op jit(solution)/shard_map/ppermute | solution.py:77
  16.6 5.9 %collective-permute-start.2 = (bf16[10,16,128]{2,1,0:T(8,128)(2,1)S(1)}, bf16[10,16,128]{2,1,0:T(8,128)(2,1)S(1)}, u32[]{:S(2)}, u32[]{:S(2)}) collective-permute-start(bf16[10,16,128]{2,1,0:T(8,128)(2,1)S(1)} %pad_maximum_fusion.5), channel_id=1, source_target_pairs={{0,8},{8,16},{16,24},{1,9},{9,17},{17,25},{2,10},{10,18},{18,26},{... | collective-permute-start | bytes 122888 | tf_op jit(solution)/shard_map/ppermute | solution.py:77
  20.7 16.8 %collective-permute-start.8 = (bf16[4,4,3584]{2,1,0:T(4,128)(2,1)S(1)}, bf16[4,4,3584]{2,1,0:T(4,128)(2,1)S(1)}, u32[]{:S(2)}, u32[]{:S(2)}) collective-permute-start(bf16[4,4,3584]{2,1,0:T(4,128)(2,1)S(1)} %pad_maximum_fusion.1), channel_id=1, source_target_pairs={{0,64},{1,65},{2,66},{3,67},{4,68},{5,69},{6,70},{7,71},{8,72},{9,... | collective-permute-start | bytes 344072 | tf_op jit(solution)/shard_map/ppermute | solution.py:61
  22.6 5.4 %collective-permute-start.5 = (bf16[10,18,128]{2,1,0:T(8,128)(2,1)S(1)}, bf16[10,18,128]{2,1,0:T(8,128)(2,1)S(1)}, u32[]{:S(2)}, u32[]{:S(2)}) collective-permute-start(bf16[10,18,128]{2,1,0:T(8,128)(2,1)S(1)} %pad_maximum_fusion.3), channel_id=1, source_target_pairs={{1,0},{2,1},{3,2},{4,3},{5,4},{6,5},{7,6},{9,8},{10,9},{11,10},{12... | collective-permute-start | bytes 138248 | tf_op jit(solution)/shard_map/ppermute | solution.py:77
  23.9 5.3 %collective-permute-start.4 = (bf16[10,18,128]{2,1,0:T(8,128)(2,1)S(1)}, bf16[10,18,128]{2,1,0:T(8,128)(2,1)S(1)}, u32[]{:S(2)}, u32[]{:S(2)}) collective-permute-start(bf16[10,18,128]{2,1,0:T(8,128)(2,1)S(1)} %pad_maximum_fusion.2), channel_id=1, source_target_pairs={{0,1},{1,2},{2,3},{3,4},{4,5},{5,6},{6,7},{8,9},{9,10},{10,11},{11... | collective-permute-start | bytes 138248 | tf_op jit(solution)/shard_map/ppermute | solution.py:77
  32.5 1.4 %copy-start.4 = (bf16[10,18,16,384]{3,2,1,0:T(8,128)(2,1)}, bf16[10,18,16,384]{3,2,1,0:T(8,128)(2,1)S(1)}, u32[]{:S(2)}) copy-start(bf16[10,18,16,384]{3,2,1,0:T(8,128)(2,1)S(1)} %get-tuple-element.11.taps_ref) | copy-start | bytes 6635524
  33.9 6.9 %collective-permute-start.11 = (bf16[64,3456]{1,0:T(8,128)(2,1)S(1)}, bf16[64,3456]{1,0:T(8,128)(2,1)S(1)}, u32[]{:S(2)}, u32[]{:S(2)}) collective-permute-start(bf16[64,3456]{1,0:T(8,128)(2,1)S(1)} %get-tuple-element.14), channel_id=1, source_target_pairs={{0,32},{1,33},{2,34},{3,35},{4,36},{5,37},{6,38},{7,39},{8,40},{9,... | collective-permute-start | bytes 1327112 | tf_op jit(solution)/shard_map/ppermute | solution.py:61
  37.7 15.8 %collective-permute-start.9 = (bf16[8,4,3584]{2,1,0:T(4,128)(2,1)S(1)}, bf16[8,4,3584]{2,1,0:T(4,128)(2,1)S(1)}, u32[]{:S(2)}, u32[]{:S(2)}) collective-permute-start(bf16[8,4,3584]{2,1,0:T(4,128)(2,1)S(1)} %pad_maximum_fusion), channel_id=1, source_target_pairs={{0,128},{1,129},{2,130},{3,131},{4,132},{5,133},{6,134},{7,135},{8... | collective-permute-start | bytes 688136 | tf_op jit(solution)/shard_map/ppermute | solution.py:61
  41.7 21.6 %all-to-all-start = ((bf16[16,4,3456]{2,1,0:T(4,128)(2,1)}), bf16[16,4,3456]{2,1,0:T(4,128)(2,1)S(1)}, u32[]{:S(2)}, u32[]{:S(2)}) async-start(bf16[16,4,3456]{2,1,0:T(4,128)(2,1)} %shard_map.54), calls=%async_computation | async-start | bytes 884736 | tf_op jit(solution)/shard_map/all_to_all | solution.py:68
  53.6 18.6 %collective-permute-start.10 = (bf16[16,4,3584]{2,1,0:T(4,128)(2,1)S(1)}, bf16[16,4,3584]{2,1,0:T(4,128)(2,1)S(1)}, u32[]{:S(2)}, u32[]{:S(2)}) collective-permute-start(bf16[16,4,3584]{2,1,0:T(4,128)(2,1)S(1)} %constant_dynamic-update-slice_fusion.near_ref), channel_id=1, source_target_pairs={{0,32},{1,33},{2,34},{3,35},{4,36},{5,37},{6,38},{7,39},{8,40},{9,... | collective-permute-start | bytes 1376264 | tf_op jit(solution)/shard_map/ppermute | solution.py:61
  64.2 16.8 %all-to-all-start.1 = ((bf16[8,4,3456]{2,1,0:T(4,128)(2,1)}), bf16[8,4,3456]{2,1,0:T(4,128)(2,1)S(1)}, u32[]{:S(2)}, u32[]{:S(2)}) async-start(bf16[8,4,3456]{2,1,0:T(4,128)(2,1)} %shard_map.55), calls=%async_computation.1 | async-start | bytes 442368 | tf_op jit(solution)/shard_map/all_to_all | solution.py:68
  73.9 18.4 %copy-start.5 = (bf16[10,18,16,384]{3,2,1,0:T(8,128)(2,1)S(1)}, bf16[10,18,16,384]{3,2,1,0:T(8,128)(2,1)}, u32[]{:S(2)}) copy-start(bf16[10,18,16,384]{3,2,1,0:T(8,128)(2,1)} %copy-done.4) | copy-start | bytes 6635524
  81.7 17.6 %collective-permute-start.12 = (f32[4,3456]{1,0:T(4,128)S(1)}, f32[4,3456]{1,0:T(4,128)S(1)}, u32[]{:S(2)}, u32[]{:S(2)}) collective-permute-start(f32[4,3456]{1,0:T(4,128)S(1)} %get-tuple-element.16), channel_id=1, source_target_pairs={{0,0},{1,64},{2,128},{3,192},{4,4},{5,68},{6,132},{7,196},{8,8},{9... | collective-permute-start | bytes 165896 | tf_op jit(solution)/shard_map/ppermute | solution.py:61
  82.4 16.9 %all-to-all-start.2 = ((f32[32,1,384]{2,1,0:T(1,128)}), f32[32,1,384]{2,1,0:T(1,128)S(1)}, u32[]{:S(2)}, u32[]{:S(2)}) async-start(f32[32,1,384]{2,1,0:T(1,128)} %get-tuple-element.19), calls=%async_computation.2 | async-start | bytes 98304 | tf_op jit(solution)/shard_map/all_to_all | solution.py:68
  92.2 7.1 %copy-start.3 = (f32[4,27,128]{2,0,1:T(4,128)S(1)}, f32[4,27,128]{2,0,1:T(4,128)}, u32[]{:S(2)}) copy-start(f32[4,27,128]{2,0,1:T(4,128)} %param.3) | copy-start | bytes 165892
where the time goes:
time: 101 us; the launch traced here: 100 us
  starting transfers between devices  61.1 us (60%)
  waiting for transfers between devices  21 us (21%)
  Pallas kernels  12.9 us (13%)
  local copies, waits for them, and re-layouts  3.57 us (4%)
    all_to_all x3, starting transfers between devices, exchange(): lax.all_to_all(array, AXES, 0, 0, tiled=True, axis_index_groups=groups)  29.6 us
    all_to_all x3, waiting for transfers between devices, exchange(): lax.all_to_all(array, AXES, 0, 0, tiled=True, axis_index_groups=groups)  18.5 us
    ppermute x6, starting transfers between devices, shift(): return lax.ppermute(array, axis, pairs)  17.4 us
    ppermute x7, starting transfers between devices, send(): return lax.ppermute(array, AXES, pairs)  14.1 us
    pallas_call x8, Pallas kernels, call(): pl.pallas_call(kernel, out_shape=out_shape, in_specs=[pl.BlockSpec(memory...  12.9 us
    unnamed x20, local copies, waits for them, and re-layouts  2.36 us
  transfers between devices with their start and end apart: 16, of which 5 were waited for; matrix products, arithmetic and copies ran while one was open for 1% of the time, Pallas kernels for 11%

commit v1 on v0

--- a/solution.py
+++ b/solution.py
@@ -1,3 +1,5 @@
+import functools
+
 import jax
 import jax.numpy as jnp
 from jax import lax
@@ -15,13 +17,12 @@
 MIB = 1024 * 1024
 
 
-def call(kernel, out_shape, args, scalars=0, vmem=8, flops=1_000_000_000):
-    spaces = [pltpu.SMEM] * scalars + [pltpu.VMEM] * (len(args) - scalars)
+def call(kernel, out_shape, args, vmem=8, flops=1_000_000_000):
     many = isinstance(out_shape, tuple)
     return pl.pallas_call(
         kernel,
         out_shape=out_shape,
-        in_specs=[pl.BlockSpec(memory_space=s) for s in spaces],
+        in_specs=[pl.BlockSpec(memory_space=pltpu.VMEM) for _ in args],
         out_specs=tuple(pl.BlockSpec(memory_space=pltpu.VMEM) for _ in out_shape)
         if many
         else pl.BlockSpec(memory_space=pltpu.VMEM),
@@ -101,7 +102,7 @@
     held_ref[0, :, taps * ch :] = both.astype(jnp.bfloat16)
 
 
-def filter_kernel(core_ref, mid_ref, xl_ref, xh_ref, yl_ref, yh_ref, zl_ref, zh_ref, in_ref, taps_ref, keep_ref, send_ref):
+def filter_kernel(mid_ref, xl_ref, xh_ref, yl_ref, yh_ref, zl_ref, zh_ref, in_ref, taps_ref, keep_ref, send_ref):
     nx, ny, nz, ch = mid_ref.shape
 
     def fill(k, rows, j, n):
@@ -129,7 +130,7 @@
     lax.fori_loop(0, nx + 2, plane, 0)
     cells = nx * ny * nz
     flat = in_ref[...].T
-    core = core_ref[0]
+    core = lax.axis_index("gx") % CORES
     for a in range(3):
         for b in range(3):
             view = taps_ref[2 - a : 2 - a + nx, 2 - b : 2 - b + ny].reshape(cells, 3 * ch)
@@ -182,12 +183,13 @@
         out_ref[x : x + planes] = res.astype(jnp.bfloat16).reshape(planes, ny, nz, ch)
 
 
-def std_kernel(spot_ref, near_ref, far_ref, std_ref, mean_ref, inv_ref, block_ref):
+def std_kernel(x_count, near_ref, far_ref, std_ref, mean_ref, inv_ref, block_ref):
     slots, rows, held = near_ref.shape
     ch = inv_ref.shape[1]
     width = held - ch
     taps = width // ch
-    y, zl, core, x = spot_ref[0], spot_ref[1], spot_ref[2], spot_ref[3]
+    gx, y, x = lax.axis_index("gx"), lax.axis_index("gy"), lax.axis_index("gz") % x_count
+    zl, core = gx // CORES, gx % CORES
     blocks = [(b // 8, (b // 4) % 2, b % 4) for b in range(2 * slots)]
     count = float(2 * slots * rows * taps)
 
@@ -240,18 +242,18 @@
     rows, taps = raw_weight.shape[:2]
     width = taps * ch
     bf16, f32 = jnp.bfloat16, jnp.float32
-    gx, gy, gz = (lax.axis_index(a).astype(jnp.int32) for a in AXES)
-    core, zl, x = gx & 1, gx >> 1, gz & (where.x - 1)
-    spot = jnp.stack([gy, zl, core, x])
     raw = jnp.transpose(raw_weight, (1, 0, 2))
+
+    def joined(held, got):
+        return jnp.concatenate([held, got], 0)
 
     x_low = shift(cotangent[-1:], "gx", 1)
     x_high = shift(cotangent[:1], "gx", -1)
     held = call(base_kernel, of((1, rows, width + ch), bf16), (raw,))
-    held = jnp.concatenate([held, where.send(held, lambda s: dict(y=s["y"] ^ 1))], 0)
+    held = joined(held, where.send(held, lambda s: dict(y=s["y"] ^ 1)))
     y_low = shift(jnp.concatenate([a[:, -1] for a in (x_low, cotangent, x_high)], 0), "gy", 1)
     y_high = shift(jnp.concatenate([a[:, 0] for a in (x_low, cotangent, x_high)], 0), "gy", -1)
-    held = jnp.concatenate([held, where.send(held, lambda s: dict(y=s["y"] ^ 2))], 0)
+    held = joined(held, where.send(held, lambda s: dict(y=s["y"] ^ 2)))
 
     def face(k):
         deep = jnp.concatenate([a[:, :, k] for a in (x_low, cotangent, x_high)], 0)
@@ -259,43 +261,39 @@
 
     z_low = shift(face(nz - 1), "gz", 1)
     z_high = shift(face(0), "gz", -1)
-    held = jnp.concatenate([held, where.send(held, lambda s: dict(zl=s["zl"] ^ 1))], 0)
+    held = joined(held, where.send(held, lambda s: dict(zl=s["zl"] ^ 1)))
 
     flops = 2 * nx * ny * nz * ch * width
     tap_views, keep, send = call(
         filter_kernel,
         (of((nx + 2, ny + 2, nz, 3 * ch), bf16), of((ch // 2, width), f32), of((ch // 2, width), bf16)),
-        (core[None], cotangent, x_low, x_high, y_low, y_high, z_low, z_high, inputs.reshape(-1, ch)),
-        scalars=1,
+        (cotangent, x_low, x_high, y_low, y_high, z_low, z_high, inputs.reshape(-1, ch)),
         vmem=16,
         flops=2 * flops,
     )
     other = where.send(send, lambda s: dict(core=1 - s["core"]))
-    held = jnp.concatenate([held, where.send(held, lambda s: dict(zl=s["zl"] ^ 2))], 0)
+    held = joined(held, where.send(held, lambda s: dict(zl=s["zl"] ^ 2)))
     peers = where.x * where.gy
     half = call(pair_kernel, of((peers, rows, width), bf16), (keep, other))
     parts = where.exchange(half, ("core", "zl", "zh"), lambda s: (s["x"], s["y"]))
     far = where.send(held, lambda s: dict(core=1 - s["core"]))
+    std_half, mean_out, inv_std, block_std = call(
+        functools.partial(std_kernel, where.x),
+        (of((ch, width), bf16), of((1, ch), f32), of((1, ch), f32), of((rows, width), f32)),
+        (held, far),
+        flops=3_000_000_000,
+    )
+    parts, inv_std = lax.optimization_barrier((parts, inv_std))
     copies = call(peers_kernel, of((where.zl * where.zh, rows, width), bf16), (parts,))
     parts = where.exchange(copies, ("core", "x", "y"), lambda s: (s["zh"], s["zl"]))
-
-    std_half, mean_out, inv_std, block_std = call(
-        std_kernel,
-        (of((ch, width), bf16), of((1, ch), f32), of((1, ch), f32), of((rows, width), f32)),
-        (spot, held, far),
-        scalars=1,
-        flops=3_000_000_000,
-    )
+    input_grad = call(input_kernel, of(inputs.shape, bf16), (tap_views, std_half), vmem=16, flops=2 * flops)
+    parts, input_grad = lax.optimization_barrier((parts, input_grad))
     everyone = CORES * where.x * where.gy
     block_grad, local = call(block_kernel, (of((rows, width), f32), of((everyone, 1, 3 * ch), f32)), (parts, block_std))
     filter_grad = where.send(block_grad, lambda s: dict(x=s["zl"], zl=s["x"]))
     sums = where.exchange(local, ("zl", "zh"), lambda s: (s["core"], s["x"], s["y"]))
-    input_grad = call(input_kernel, of(inputs.shape, bf16), (tap_views, std_half), vmem=16, flops=2 * flops)
-
-    def last(*refs):
-        last_kernel(float(ch * taps), *refs)
-
-    grad = call(last, of((taps, rows, ch), f32), (filter_grad, raw, mean_out, inv_std, sums))
+
+    grad = call(functools.partial(last_kernel, float(ch * taps)), of((taps, rows, ch), f32), (filter_grad, raw, mean_out, inv_std, sums))
     return (input_grad, jnp.transpose(grad, (1, 0, 2)))
 
 

time: 101 us -> 114 us (1.13)
  blocking collectives: 0 us -> 17.4 us
  starting transfers between devices: 61.1 us -> 47.8 us
  waiting for transfers between devices: 21 us -> 30.4 us
  Pallas kernels: 12.9 us -> 11.7 us
    all_to_all x0 -> x1, blocking collectives: none -> 17.4 us  [exchange(): lax.all_to_all(array, AXES, 0, 0, tiled=True, axis_index_groups=groups)]
    ppermute x7, waiting for transfers between devices: 1.25 us -> 12.8 us  [send(): return lax.ppermute(array, AXES, pairs)]
    all_to_all x3 -> x2, starting transfers between devices: 29.6 us -> 18.4 us  [exchange(): lax.all_to_all(array, AXES, 0, 0, tiled=True, axis_index_groups=groups)]
    all_to_all x3 -> x2, waiting for transfers between devices: 18.5 us -> 12.1 us  [exchange(): lax.all_to_all(array, AXES, 0, 0, tiled=True, axis_index_groups=groups)]
    ppermute x6, waiting for transfers between devices: 1.24 us -> 5.61 us  [shift(): return lax.ppermute(array, axis, pairs)]
    ppermute x6, starting transfers between devices: 17.4 us -> 14.9 us  [shift(): return lax.ppermute(array, axis, pairs)]
    pallas_call x8, Pallas kernels: 12.9 us -> 11.7 us  [call(): pl.pallas_call(kernel, out_shape=out_shape, in_specs=[pl.BlockSpec(memory...]
    unnamed x20 -> x24, local copies, waits for them, and re-layouts: 2.36 us -> 2.97 us
  transfers between devices with their start and end apart: 16 -> 15, of which waited for: 5 -> 6; matrix products, arithmetic and copies ran while one was open for 1% -> 1% of each run, Pallas kernels for 11% -> 9%
where the time goes in v1:
time: 114 us; the launch traced here: 113 us
  starting transfers between devices  47.8 us (42%)
  waiting for transfers between devices  30.4 us (27%)
  blocking collectives  17.4 us (15%)
  Pallas kernels  11.7 us (10%)
  local copies, waits for them, and re-layouts  4.19 us (4%)
    all_to_all x2, starting transfers between devices, exchange(): lax.all_to_all(array, AXES, 0, 0, tiled=True, axis_index_groups=groups)  18.4 us
    all_to_all x1, blocking collectives, exchange(): lax.all_to_all(array, AXES, 0, 0, tiled=True, axis_index_groups=groups)  17.4 us
    ppermute x6, starting transfers between devices, shift(): return lax.ppermute(array, axis, pairs)  14.9 us
    ppermute x7, starting transfers between devices, send(): return lax.ppermute(array, AXES, pairs)  14.6 us
    ppermute x7, waiting for transfers between devices, send(): return lax.ppermute(array, AXES, pairs)  12.8 us
    all_to_all x2, waiting for transfers between devices, exchange(): lax.all_to_all(array, AXES, 0, 0, tiled=True, axis_index_groups=groups)  12.1 us
    pallas_call x8, Pallas kernels, call(): pl.pallas_call(kernel, out_shape=out_shape, in_specs=[pl.BlockSpec(memory...  11.7 us
    ppermute x6, waiting for transfers between devices, shift(): return lax.ppermute(array, axis, pairs)  5.61 us
  transfers between devices with their start and end apart: 15, of which 6 were waited for; matrix products, arithmetic and copies ran while one was open for 1% of the time, Pallas kernels for 9%

profile of v1, /device:TPU:1, one launch (start us, length us, event | category | flops | bytes accessed | tf_op | source)
XLA Modules:
  0.0 112.9 jit_solution(1787834130262230058)
XLA Ops:
  0.6 0.9 fusion.1
  1.6 4.9 %collective-permute-start = (bf16[1,16,16,128]{3,2,1,0:T(8,128)(2,1)S(1)}, bf16[1,16,16,128]{3,2,1,0:T(8,128)(2,1)S(1)}, u32[]{:S(2)}, u32[]{:S(2)}) collective-permute-start(bf16[1,16,16,128]{3,2,1,0:T(8,128)(2,1)S(1)} %get-tuple-element.33), channel_id=1, source_target_pairs={{0,32},{32,64},{64,96},{96,128},{128,160},{160,192},{192,224},{1,3... | collective-permute-start | bytes 196616 | tf_op jit(solution)/shard_map/ppermute | solution.py:78
  6.5 1.9 %collective-permute-start.1 = (bf16[1,16,16,128]{3,2,1,0:T(8,128)(2,1)S(1)}, bf16[1,16,16,128]{3,2,1,0:T(8,128)(2,1)S(1)}, u32[]{:S(2)}, u32[]{:S(2)}) collective-permute-start(bf16[1,16,16,128]{3,2,1,0:T(8,128)(2,1)S(1)} %get-tuple-element.32), channel_id=1, source_target_pairs={{32,0},{64,32},{96,64},{128,96},{160,128},{192,160},{224,192},{33,... | collective-permute-start | bytes 196616 | tf_op jit(solution)/shard_map/ppermute | solution.py:78
  8.4 0.0 copy-start.2
  8.5 0.8 copy-done.2
  9.3 0.1 shard_map.52
  9.3 1.4 %collective-permute-start.7 = (bf16[1,4,3584]{2,1,0:T(4,128)(2,1)S(1)}, bf16[1,4,3584]{2,1,0:T(4,128)(2,1)S(1)}, u32[]{:S(2)}, u32[]{:S(2)}) collective-permute-start(bf16[1,4,3584]{2,1,0:T(4,128)(2,1)S(1)} %shard_map.52), channel_id=1, source_target_pairs={{0,8},{1,9},{2,10},{3,11},{4,12},{5,13},{6,14},{7,15},{8,0},{9,1},... | collective-permute-start | bytes 86024 | tf_op jit(solution)/shard_map/ppermute | solution.py:62
  10.7 0.1 fusion
  10.9 1.2 %collective-permute-done.7 = bf16[1,4,3584]{2,1,0:T(4,128)(2,1)S(1)} collective-permute-done((bf16[1,4,3584]{2,1,0:T(4,128)(2,1)S(1)}, bf16[1,4,3584]{2,1,0:T(4,128)(2,1)S(1)}, u32[]{:S(2)}, u32[]{:S(2)}) %collective-permute-start.7) | collective-permute-done | bytes 28704 | tf_op jit(solution)/shard_map/ppermute | solution.py:62
  12.2 3.0 %collective-permute-start.8 = (bf16[2,4,3584]{2,1,0:T(4,128)(2,1)S(1)}, bf16[2,4,3584]{2,1,0:T(4,128)(2,1)S(1)}, u32[]{:S(2)}, u32[]{:S(2)}) collective-permute-start(bf16[2,4,3584]{2,1,0:T(4,128)(2,1)S(1)} %pad_maximum_fusion.4), channel_id=1, source_target_pairs={{0,16},{1,17},{2,18},{3,19},{4,20},{5,21},{6,22},{7,23},{8,24},{9,... | collective-permute-start | bytes 172040 | tf_op jit(solution)/shard_map/ppermute | solution.py:62
  15.2 0.0 collective-permute-done.1.xh_ref
  15.2 0.0 collective-permute-done.xl_ref
  15.3 2.3 %collective-permute-start.2 = (bf16[10,16,128]{2,1,0:T(8,128)(2,1)S(1)}, bf16[10,16,128]{2,1,0:T(8,128)(2,1)S(1)}, u32[]{:S(2)}, u32[]{:S(2)}) collective-permute-start(bf16[10,16,128]{2,1,0:T(8,128)(2,1)S(1)} %pad_maximum_fusion.5), channel_id=1, source_target_pairs={{0,8},{8,16},{16,24},{1,9},{9,17},{17,25},{2,10},{10,18},{18,26},{... | collective-permute-start | bytes 122888 | tf_op jit(solution)/shard_map/ppermute | solution.py:78
  17.6 1.3 %collective-permute-start.3 = (bf16[10,16,128]{2,1,0:T(8,128)(2,1)S(1)}, bf16[10,16,128]{2,1,0:T(8,128)(2,1)S(1)}, u32[]{:S(2)}, u32[]{:S(2)}) collective-permute-start(bf16[10,16,128]{2,1,0:T(8,128)(2,1)S(1)} %pad_maximum_fusion.6), channel_id=1, source_target_pairs={{8,0},{16,8},{24,16},{9,1},{17,9},{25,17},{10,2},{18,10},{26,18},{... | collective-permute-start | bytes 122888 | tf_op jit(solution)/shard_map/ppermute | solution.py:78
  19.0 0.0 collective-permute-done.8
  19.0 0.1 pad_maximum_fusion.1
  19.1 1.7 %collective-permute-start.9 = (bf16[4,4,3584]{2,1,0:T(4,128)(2,1)S(1)}, bf16[4,4,3584]{2,1,0:T(4,128)(2,1)S(1)}, u32[]{:S(2)}, u32[]{:S(2)}) collective-permute-start(bf16[4,4,3584]{2,1,0:T(4,128)(2,1)S(1)} %pad_maximum_fusion.1), channel_id=1, source_target_pairs={{0,64},{1,65},{2,66},{3,67},{4,68},{5,69},{6,70},{7,71},{8,72},{9,... | collective-permute-start | bytes 344072 | tf_op jit(solution)/shard_map/ppermute | solution.py:62
  20.8 2.0 %collective-permute-done.3.yh_ref = bf16[10,16,128]{2,1,0:T(8,128)(2,1)S(1)} collective-permute-done((bf16[10,16,128]{2,1,0:T(8,128)(2,1)S(1)}, bf16[10,16,128]{2,1,0:T(8,128)(2,1)S(1)}, u32[]{:S(2)}, u32[]{:S(2)}) %collective-permute-start.3) | collective-permute-done | bytes 40992 | tf_op jit(solution)/shard_map/ppermute | solution.py:78
  22.8 0.0 collective-permute-done.2.yl_ref
  22.9 3.1 %collective-permute-start.4 = (bf16[10,18,128]{2,1,0:T(8,128)(2,1)S(1)}, bf16[10,18,128]{2,1,0:T(8,128)(2,1)S(1)}, u32[]{:S(2)}, u32[]{:S(2)}) collective-permute-start(bf16[10,18,128]{2,1,0:T(8,128)(2,1)S(1)} %pad_maximum_fusion.2), channel_id=1, source_target_pairs={{0,1},{1,2},{2,3},{3,4},{4,5},{5,6},{6,7},{8,9},{9,10},{10,11},{11... | collective-permute-start | bytes 138248 | tf_op jit(solution)/shard_map/ppermute | solution.py:78
  26.0 1.3 %collective-permute-start.5 = (bf16[10,18,128]{2,1,0:T(8,128)(2,1)S(1)}, bf16[10,18,128]{2,1,0:T(8,128)(2,1)S(1)}, u32[]{:S(2)}, u32[]{:S(2)}) collective-permute-start(bf16[10,18,128]{2,1,0:T(8,128)(2,1)S(1)} %pad_maximum_fusion.3), channel_id=1, source_target_pairs={{1,0},{2,1},{3,2},{4,3},{5,4},{6,5},{7,6},{9,8},{10,9},{11,10},{12... | collective-permute-start | bytes 138248 | tf_op jit(solution)/shard_map/ppermute | solution.py:78
  27.4 0.0 collective-permute-done.4.zl_ref
  27.4 3.6 %collective-permute-done.5.zh_ref = bf16[10,18,128]{2,1,0:T(8,128)(2,1)S(1)} collective-permute-done((bf16[10,18,128]{2,1,0:T(8,128)(2,1)S(1)}, bf16[10,18,128]{2,1,0:T(8,128)(2,1)S(1)}, u32[]{:S(2)}, u32[]{:S(2)}) %collective-permute-start.5) | collective-permute-done | bytes 46112 | tf_op jit(solution)/shard_map/ppermute | solution.py:78
  31.0 3.3 %shard_map.50 = (bf16[10,18,16,384]{3,2,1,0:T(8,128)(2,1)S(1)}, f32[64,3456]{1,0:T(8,128)S(1)}, bf16[64,3456]{1,0:T(8,128)(2,1)S(1)}) custom-call(bf16[8,16,16,128]{3,2,1,0:T(8,128)(2,1)S(1)} %copy-done, bf16[1,16,16,128]{3,2,1,0:T(8,128)(2,1)S(1)} %collective-permute-done.xl_ref, bf16[1,16,16,128]{3,2,1,0:T(8,128)(2,1)S(1)} %collective-permute-done.1.xh_ref, ...), custom_call_target="tpu_custom_call" | custom-call | flops 3623878656 | bytes 1000000 | tf_op jit(solution)/shard_map/pallas_call | solution.py:22
  34.3 1.4 %copy-done.4 = bf16[10,18,16,384]{3,2,1,0:T(8,128)(2,1)} copy-done((bf16[10,18,16,384]{3,2,1,0:T(8,128)(2,1)}, bf16[10,18,16,384]{3,2,1,0:T(8,128)(2,1)S(1)}, u32[]{:S(2)}) %copy-start.4) | copy-done | bytes 2211864
  35.7 1.8 %collective-permute-start.6 = (bf16[64,3456]{1,0:T(8,128)(2,1)S(1)}, bf16[64,3456]{1,0:T(8,128)(2,1)S(1)}, u32[]{:S(2)}, u32[]{:S(2)}) collective-permute-start(bf16[64,3456]{1,0:T(8,128)(2,1)S(1)} %get-tuple-element.16), channel_id=1, source_target_pairs={{0,32},{1,33},{2,34},{3,35},{4,36},{5,37},{6,38},{7,39},{8,40},{9,... | collective-permute-start | bytes 1327112 | tf_op jit(solution)/shard_map/ppermute | solution.py:62
  37.5 0.2 pad_maximum_fusion
  37.7 5.3 %collective-permute-start.10 = (bf16[8,4,3584]{2,1,0:T(4,128)(2,1)S(1)}, bf16[8,4,3584]{2,1,0:T(4,128)(2,1)S(1)}, u32[]{:S(2)}, u32[]{:S(2)}) collective-permute-start(bf16[8,4,3584]{2,1,0:T(4,128)(2,1)S(1)} %pad_maximum_fusion), channel_id=1, source_target_pairs={{0,128},{1,129},{2,130},{3,131},{4,132},{5,133},{6,134},{7,135},{8... | collective-permute-start | bytes 688136 | tf_op jit(solution)/shard_map/ppermute | solution.py:62
  43.0 0.1 constant_dynamic-update-slice_fusion.1
  43.1 11.5 %collective-permute-done.10 = bf16[8,4,3584]{2,1,0:T(4,128)(2,1)S(1)} collective-permute-done((bf16[8,4,3584]{2,1,0:T(4,128)(2,1)S(1)}, bf16[8,4,3584]{2,1,0:T(4,128)(2,1)S(1)}, u32[]{:S(2)}, u32[]{:S(2)}) %collective-permute-start.10) | collective-permute-done | bytes 229408 | tf_op jit(solution)/shard_map/ppermute | solution.py:62
  54.6 0.1 constant_dynamic-update-slice_fusion.near_ref
  54.7 0.7 collective-permute-start.11
  55.4 0.0 collective-permute-done.6.other_ref
  55.4 0.9 shard_map.51
  56.2 14.5 %all-to-all-start = ((bf16[16,4,3456]{2,1,0:T(4,128)(2,1)}), bf16[16,4,3456]{2,1,0:T(4,128)(2,1)S(1)}, u32[]{:S(2)}, u32[]{:S(2)}) async-start(bf16[16,4,3456]{2,1,0:T(4,128)(2,1)} %shard_map.51), calls=%async_computation | async-start | bytes 884736 | tf_op jit(solution)/shard_map/all_to_all | solution.py:69
  70.7 1.1 shard_map.53
  71.8 0.0 copy-start.6
  71.8 0.6 copy-done.6
  72.5 7.7 %all-to-all-done.parts_ref = bf16[16,4,3456]{2,1,0:T(4,128)(2,1)S(1)} async-done(((bf16[16,4,3456]{2,1,0:T(4,128)(2,1)}), bf16[16,4,3456]{2,1,0:T(4,128)(2,1)S(1)}, u32[]{:S(2)}, u32[]{:S(2)}) %all-to-all-start) | async-done | bytes 442400 | tf_op jit(solution)/shard_map/all_to_all | solution.py:69
  80.1 0.9 shard_map.54
  81.0 3.9 %all-to-all-start.1 = ((bf16[8,4,3456]{2,1,0:T(4,128)(2,1)}), bf16[8,4,3456]{2,1,0:T(4,128)(2,1)S(1)}, u32[]{:S(2)}, u32[]{:S(2)}) async-start(bf16[8,4,3456]{2,1,0:T(4,128)(2,1)} %shard_map.54), calls=%async_computation.1 | async-start | bytes 442368 | tf_op jit(solution)/shard_map/all_to_all | solution.py:69
  85.0 0.0 copy-start.7
  85.0 4.6 %shard_map.55 = bf16[8,16,16,128]{3,2,1,0:T(8,128)(2,1)} custom-call(bf16[10,18,16,384]{3,2,1,0:T(8,128)(2,1)S(1)} %copy-done.5, bf16[128,3456]{1,0:T(8,128)(2,1)S(1)} %get-tuple-element.20.std_ref), custom_call_target="tpu_custom_call" | custom-call | flops 3623878656 | bytes 1000000 | tf_op jit(solution)/shard_map/pallas_call | solution.py:22
  89.6 4.4 %all-to-all-done.1.parts_ref = bf16[8,4,3456]{2,1,0:T(4,128)(2,1)S(1)} async-done(((bf16[8,4,3456]{2,1,0:T(4,128)(2,1)}), bf16[8,4,3456]{2,1,0:T(4,128)(2,1)S(1)}, u32[]{:S(2)}, u32[]{:S(2)}) %all-to-all-start.1) | async-done | bytes 221216 | tf_op jit(solution)/shard_map/all_to_all | solution.py:69
  93.9 0.1 shard_map.56
  94.1 0.7 collective-permute-start.12
  94.7 17.4 %all_to_all.15.sums_ref = f32[32,1,384]{2,1,0:T(1,128)S(1)} all-to-all(f32[32,1,384]{2,1,0:T(1,128)S(1)} %get-tuple-element.27), channel_id=1, replica_groups={{0,8,16,24,1,9,17,25,2,10,18,26,3,11,19,27,32,40,48,56,33,41,49,57,34,4..., dimensions={0} | all-to-all | bytes 98304 | tf_op jit(solution)/shard_map/all_to_all | solution.py:69
  112.1 0.8 shard_map.57
  (32 shorter events, 0.3 us)
Async XLA Ops:
  0.6 10.1 %copy-start = (bf16[8,16,16,128]{3,2,1,0:T(8,128)(2,1)S(1)}, bf16[8,16,16,128]{3,2,1,0:T(8,128)(2,1)}, u32[]{:S(2)}) copy-start(bf16[8,16,16,128]{3,2,1,0:T(8,128)(2,1)} %mid_ref.1) | copy-start | bytes 1572868
  1.6 13.6 %collective-permute-start = (bf16[1,16,16,128]{3,2,1,0:T(8,128)(2,1)S(1)}, bf16[1,16,16,128]{3,2,1,0:T(8,128)(2,1)S(1)}, u32[]{:S(2)}, u32[]{:S(2)}) collective-permute-start(bf16[1,16,16,128]{3,2,1,0:T(8,128)(2,1)S(1)} %get-tuple-element.33), channel_id=1, source_target_pairs={{0,32},{32,64},{64,96},{96,128},{128,160},{160,192},{192,224},{1,3... | collective-permute-start | bytes 196616 | tf_op jit(solution)/shard_map/ppermute | solution.py:78
  6.5 8.7 %collective-permute-start.1 = (bf16[1,16,16,128]{3,2,1,0:T(8,128)(2,1)S(1)}, bf16[1,16,16,128]{3,2,1,0:T(8,128)(2,1)S(1)}, u32[]{:S(2)}, u32[]{:S(2)}) collective-permute-start(bf16[1,16,16,128]{3,2,1,0:T(8,128)(2,1)S(1)} %get-tuple-element.32), channel_id=1, source_target_pairs={{32,0},{64,32},{96,64},{128,96},{160,128},{192,160},{224,192},{33,... | collective-permute-start | bytes 196616 | tf_op jit(solution)/shard_map/ppermute | solution.py:78
  8.4 0.8 copy-start.2
  9.3 21.7 %copy-start.1 = (bf16[8,16,16,128]{3,2,1,0:T(8,128)(2,1)S(1)}, bf16[8,16,16,128]{3,2,1,0:T(8,128)(2,1)}, u32[]{:S(2)}) copy-start(bf16[8,16,16,128]{3,2,1,0:T(8,128)(2,1)} %param.4) | copy-start | bytes 1572868
  9.3 2.8 %collective-permute-start.7 = (bf16[1,4,3584]{2,1,0:T(4,128)(2,1)S(1)}, bf16[1,4,3584]{2,1,0:T(4,128)(2,1)S(1)}, u32[]{:S(2)}, u32[]{:S(2)}) collective-permute-start(bf16[1,4,3584]{2,1,0:T(4,128)(2,1)S(1)} %shard_map.52), channel_id=1, source_target_pairs={{0,8},{1,9},{2,10},{3,11},{4,12},{5,13},{6,14},{7,15},{8,0},{9,1},... | collective-permute-start | bytes 86024 | tf_op jit(solution)/shard_map/ppermute | solution.py:62
  12.2 6.8 %collective-permute-start.8 = (bf16[2,4,3584]{2,1,0:T(4,128)(2,1)S(1)}, bf16[2,4,3584]{2,1,0:T(4,128)(2,1)S(1)}, u32[]{:S(2)}, u32[]{:S(2)}) collective-permute-start(bf16[2,4,3584]{2,1,0:T(4,128)(2,1)S(1)} %pad_maximum_fusion.4), channel_id=1, source_target_pairs={{0,16},{1,17},{2,18},{3,19},{4,20},{5,21},{6,22},{7,23},{8,24},{9,... | collective-permute-start | bytes 172040 | tf_op jit(solution)/shard_map/ppermute | solution.py:62
  15.3 7.5 %collective-permute-start.2 = (bf16[10,16,128]{2,1,0:T(8,128)(2,1)S(1)}, bf16[10,16,128]{2,1,0:T(8,128)(2,1)S(1)}, u32[]{:S(2)}, u32[]{:S(2)}) collective-permute-start(bf16[10,16,128]{2,1,0:T(8,128)(2,1)S(1)} %pad_maximum_fusion.5), channel_id=1, source_target_pairs={{0,8},{8,16},{16,24},{1,9},{9,17},{17,25},{2,10},{10,18},{18,26},{... | collective-permute-start | bytes 122888 | tf_op jit(solution)/shard_map/ppermute | solution.py:78
  17.6 5.2 %collective-permute-start.3 = (bf16[10,16,128]{2,1,0:T(8,128)(2,1)S(1)}, bf16[10,16,128]{2,1,0:T(8,128)(2,1)S(1)}, u32[]{:S(2)}, u32[]{:S(2)}) collective-permute-start(bf16[10,16,128]{2,1,0:T(8,128)(2,1)S(1)} %pad_maximum_fusion.6), channel_id=1, source_target_pairs={{8,0},{16,8},{24,16},{9,1},{17,9},{25,17},{10,2},{18,10},{26,18},{... | collective-permute-start | bytes 122888 | tf_op jit(solution)/shard_map/ppermute | solution.py:78
  19.1 18.5 %collective-permute-start.9 = (bf16[4,4,3584]{2,1,0:T(4,128)(2,1)S(1)}, bf16[4,4,3584]{2,1,0:T(4,128)(2,1)S(1)}, u32[]{:S(2)}, u32[]{:S(2)}) collective-permute-start(bf16[4,4,3584]{2,1,0:T(4,128)(2,1)S(1)} %pad_maximum_fusion.1), channel_id=1, source_target_pairs={{0,64},{1,65},{2,66},{3,67},{4,68},{5,69},{6,70},{7,71},{8,72},{9,... | collective-permute-start | bytes 344072 | tf_op jit(solution)/shard_map/ppermute | solution.py:62
  22.9 4.5 %collective-permute-start.4 = (bf16[10,18,128]{2,1,0:T(8,128)(2,1)S(1)}, bf16[10,18,128]{2,1,0:T(8,128)(2,1)S(1)}, u32[]{:S(2)}, u32[]{:S(2)}) collective-permute-start(bf16[10,18,128]{2,1,0:T(8,128)(2,1)S(1)} %pad_maximum_fusion.2), channel_id=1, source_target_pairs={{0,1},{1,2},{2,3},{3,4},{4,5},{5,6},{6,7},{8,9},{9,10},{10,11},{11... | collective-permute-start | bytes 138248 | tf_op jit(solution)/shard_map/ppermute | solution.py:78
  26.0 5.0 %collective-permute-start.5 = (bf16[10,18,128]{2,1,0:T(8,128)(2,1)S(1)}, bf16[10,18,128]{2,1,0:T(8,128)(2,1)S(1)}, u32[]{:S(2)}, u32[]{:S(2)}) collective-permute-start(bf16[10,18,128]{2,1,0:T(8,128)(2,1)S(1)} %pad_maximum_fusion.3), channel_id=1, source_target_pairs={{1,0},{2,1},{3,2},{4,3},{5,4},{6,5},{7,6},{9,8},{10,9},{11,10},{12... | collective-permute-start | bytes 138248 | tf_op jit(solution)/shard_map/ppermute | solution.py:78
  34.3 1.4 %copy-start.4 = (bf16[10,18,16,384]{3,2,1,0:T(8,128)(2,1)}, bf16[10,18,16,384]{3,2,1,0:T(8,128)(2,1)S(1)}, u32[]{:S(2)}) copy-start(bf16[10,18,16,384]{3,2,1,0:T(8,128)(2,1)S(1)} %get-tuple-element.19.taps_ref) | copy-start | bytes 6635524
  35.7 19.6 %collective-permute-start.6 = (bf16[64,3456]{1,0:T(8,128)(2,1)S(1)}, bf16[64,3456]{1,0:T(8,128)(2,1)S(1)}, u32[]{:S(2)}, u32[]{:S(2)}) collective-permute-start(bf16[64,3456]{1,0:T(8,128)(2,1)S(1)} %get-tuple-element.16), channel_id=1, source_target_pairs={{0,32},{1,33},{2,34},{3,35},{4,36},{5,37},{6,38},{7,39},{8,40},{9,... | collective-permute-start | bytes 1327112 | tf_op jit(solution)/shard_map/ppermute | solution.py:62
  37.7 16.9 %collective-permute-start.10 = (bf16[8,4,3584]{2,1,0:T(4,128)(2,1)S(1)}, bf16[8,4,3584]{2,1,0:T(4,128)(2,1)S(1)}, u32[]{:S(2)}, u32[]{:S(2)}) collective-permute-start(bf16[8,4,3584]{2,1,0:T(4,128)(2,1)S(1)} %pad_maximum_fusion), channel_id=1, source_target_pairs={{0,128},{1,129},{2,130},{3,131},{4,132},{5,133},{6,134},{7,135},{8... | collective-permute-start | bytes 688136 | tf_op jit(solution)/shard_map/ppermute | solution.py:62
  54.7 16.0 %collective-permute-start.11 = (bf16[16,4,3584]{2,1,0:T(4,128)(2,1)S(1)}, bf16[16,4,3584]{2,1,0:T(4,128)(2,1)S(1)}, u32[]{:S(2)}, u32[]{:S(2)}) collective-permute-start(bf16[16,4,3584]{2,1,0:T(4,128)(2,1)S(1)} %constant_dynamic-update-slice_fusion.near_ref), channel_id=1, source_target_pairs={{0,32},{1,33},{2,34},{3,35},{4,36},{5,37},{6,38},{7,39},{8,40},{9,... | collective-permute-start | bytes 1376264 | tf_op jit(solution)/shard_map/ppermute | solution.py:62
  56.2 23.9 %all-to-all-start = ((bf16[16,4,3456]{2,1,0:T(4,128)(2,1)}), bf16[16,4,3456]{2,1,0:T(4,128)(2,1)S(1)}, u32[]{:S(2)}, u32[]{:S(2)}) async-start(bf16[16,4,3456]{2,1,0:T(4,128)(2,1)} %shard_map.51), calls=%async_computation | async-start | bytes 884736 | tf_op jit(solution)/shard_map/all_to_all | solution.py:69
  71.8 0.6 copy-start.6
  72.5 12.5 %copy-start.5 = (bf16[10,18,16,384]{3,2,1,0:T(8,128)(2,1)S(1)}, bf16[10,18,16,384]{3,2,1,0:T(8,128)(2,1)}, u32[]{:S(2)}) copy-start(bf16[10,18,16,384]{3,2,1,0:T(8,128)(2,1)} %copy-done.4) | copy-start | bytes 6635524
  81.0 12.9 %all-to-all-start.1 = ((bf16[8,4,3456]{2,1,0:T(4,128)(2,1)}), bf16[8,4,3456]{2,1,0:T(4,128)(2,1)S(1)}, u32[]{:S(2)}, u32[]{:S(2)}) async-start(bf16[8,4,3456]{2,1,0:T(4,128)(2,1)} %shard_map.54), calls=%async_computation.1 | async-start | bytes 442368 | tf_op jit(solution)/shard_map/all_to_all | solution.py:69
  85.0 9.0 %copy-start.7 = (f32[4,3456]{1,0:T(4,128)S(1)}, f32[4,3456]{1,0:T(4,128)}, u32[]{:S(2)}) copy-start(f32[4,3456]{1,0:T(4,128)} %copy-done.6) | copy-start | bytes 165892
  89.6 22.6 %copy-start.3 = (f32[4,27,128]{2,0,1:T(4,128)S(1)}, f32[4,27,128]{2,0,1:T(4,128)}, u32[]{:S(2)}) copy-start(f32[4,27,128]{2,0,1:T(4,128)} %param.3) | copy-start | bytes 165892
  94.1 18.1 %collective-permute-start.12 = (f32[4,3456]{1,0:T(4,128)S(1)}, f32[4,3456]{1,0:T(4,128)S(1)}, u32[]{:S(2)}, u32[]{:S(2)}) collective-permute-start(f32[4,3456]{1,0:T(4,128)S(1)} %get-tuple-element.24), channel_id=1, source_target_pairs={{0,0},{1,64},{2,128},{3,192},{4,4},{5,68},{6,132},{7,196},{8,8},{9... | collective-permute-start | bytes 165896 | tf_op jit(solution)/shard_map/ppermute | solution.py:62

commit v2 on v1

--- a/solution.py
+++ b/solution.py
@@ -69,13 +69,18 @@
         return lax.all_to_all(array, AXES, 0, 0, tiled=True, axis_index_groups=groups)
 
 
-def shift(array, axis, step):
+def swapped(first, second, axis):
     count = lax.axis_size(axis)
-    if step > 0:
-        pairs = [(i, i + 1) for i in range(count - 1)]
-    else:
-        pairs = [(i + 1, i) for i in range(count - 1)]
-    return lax.ppermute(array, axis, pairs)
+
+    def pairs(start):
+        ends = [(i, i + 1) for i in range(start, count - 1, 2)]
+        return ends + [(j, i) for i, j in ends]
+
+    return lax.ppermute(first, axis, pairs(0)), lax.ppermute(second, axis, pairs(1))
+
+
+def is_odd(axis):
+    return lax.axis_index(axis) % 2 == 1
 
 
 def wide(row, taps=TAPS):
@@ -89,7 +94,14 @@
     return jnp.sum(total, axis=0, keepdims=True)
 
 
-def base_kernel(raw_ref, held_ref):
+def faces_kernel(mid_ref, first_ref, second_ref):
+    last = mid_ref.shape[0] - 1
+    odd = is_odd("gx")
+    first_ref[0] = mid_ref[jnp.where(odd, 0, last)]
+    second_ref[0] = mid_ref[jnp.where(odd, last, 0)]
+
+
+def base_kernel(raw_ref, mid_ref, held_ref, zl_ref, zh_ref):
     taps, rows, ch = raw_ref.shape
     base = jnp.sum(jnp.sum(raw_ref[...], axis=0), axis=0, keepdims=True) / (taps * rows)
     high = base.astype(jnp.bfloat16)
@@ -100,15 +112,52 @@
     place = lax.broadcasted_iota(jnp.int32, (rows, ch), 0)
     both = jnp.where(place == 0, high.astype(jnp.float32), low.astype(jnp.float32))
     held_ref[0, :, taps * ch :] = both.astype(jnp.bfloat16)
-
-
-def filter_kernel(mid_ref, xl_ref, xh_ref, yl_ref, yh_ref, zl_ref, zh_ref, in_ref, taps_ref, keep_ref, send_ref):
+    nz = mid_ref.shape[2]
+    for k in range(mid_ref.shape[0]):
+        mid = mid_ref[k].astype(jnp.float32)
+        zl_ref[k] = mid[:, 0].astype(jnp.bfloat16)
+        zh_ref[k] = mid[:, nz - 1].astype(jnp.bfloat16)
+
+
+def picked(odd, first, second):
+    return jnp.where(odd, first, second), jnp.where(odd, second, first)
+
+
+def height_kernel(mid_ref, xa_ref, xb_ref, first_ref, second_ref):
+    nx, ny = mid_ref.shape[:2]
+    x_odd, odd = is_odd("gx"), is_odd("gy")
+    for out_ref, j in ((first_ref, jnp.where(odd, 0, ny - 1)), (second_ref, jnp.where(odd, ny - 1, 0))):
+        low, high = picked(x_odd, xa_ref[0, j], xb_ref[0, j])
+        out_ref[0] = low
+        out_ref[nx + 1] = high
+        for k in range(nx):
+            out_ref[k + 1] = mid_ref[k, j]
+
+
+def width_kernel(zl_ref, zh_ref, xa_ref, xb_ref, ya_ref, yb_ref, first_ref, second_ref):
+    nz = ya_ref.shape[1]
+    x_odd, y_odd, odd = is_odd("gx"), is_odd("gy"), is_odd("gz")
+
+    def face(k, own):
+        x_low, x_high = picked(x_odd, xa_ref[0].astype(jnp.float32)[:, k], xb_ref[0].astype(jnp.float32)[:, k])
+        y_low, y_high = picked(y_odd, ya_ref[...].astype(jnp.float32)[:, k], yb_ref[...].astype(jnp.float32)[:, k])
+        deep = jnp.concatenate([x_low[None], own.astype(jnp.float32), x_high[None]], axis=0)
+        return jnp.concatenate([y_low[:, None], deep, y_high[:, None]], axis=1)
+
+    low, high = face(0, zl_ref[...]), face(nz - 1, zh_ref[...])
+    first_ref[...] = jnp.where(odd, low, high).astype(jnp.bfloat16)
+    second_ref[...] = jnp.where(odd, high, low).astype(jnp.bfloat16)
+
+
+def filter_kernel(mid_ref, xa_ref, xb_ref, ya_ref, yb_ref, za_ref, zb_ref, in_ref, taps_ref, keep_ref, send_ref):
     nx, ny, nz, ch = mid_ref.shape
+    x_odd, y_odd, z_odd = is_odd("gx"), is_odd("gy"), is_odd("gz")
 
     def fill(k, rows, j, n):
         mid = rows.astype(jnp.float32)
-        low = zl_ref[k, j : j + n].astype(jnp.float32)[:, None, :]
-        high = zh_ref[k, j : j + n].astype(jnp.float32)[:, None, :]
+        low, high = picked(z_odd, za_ref[k, j : j + n], zb_ref[k, j : j + n])
+        low = low.astype(jnp.float32)[:, None, :]
+        high = high.astype(jnp.float32)[:, None, :]
         up = jnp.concatenate([mid[:, 1:], high], axis=1)
         down = jnp.concatenate([low, mid[:, :-1]], axis=1)
         taps_ref[k, j : j + n, :, 0:ch] = up.astype(jnp.bfloat16)
@@ -116,8 +165,9 @@
         taps_ref[k, j : j + n, :, 2 * ch : 3 * ch] = down.astype(jnp.bfloat16)
 
     def plane(k, carry):
-        fill(k, yl_ref[k][None], 0, 1)
-        fill(k, yh_ref[k][None], ny + 1, 1)
+        low, high = picked(y_odd, ya_ref[k], yb_ref[k])
+        fill(k, low[None], 0, 1)
+        fill(k, high[None], ny + 1, 1)
         return carry
 
     def middle(k, carry):
@@ -125,8 +175,9 @@
         return carry
 
     lax.fori_loop(0, nx, middle, 0)
-    fill(0, xl_ref[0], 1, ny)
-    fill(nx + 1, xh_ref[0], 1, ny)
+    low, high = picked(x_odd, xa_ref[0], xb_ref[0])
+    fill(0, low, 1, ny)
+    fill(nx + 1, high, 1, ny)
     lax.fori_loop(0, nx + 2, plane, 0)
     cells = nx * ny * nz
     flat = in_ref[...].T
@@ -247,27 +298,25 @@
     def joined(held, got):
         return jnp.concatenate([held, got], 0)
 
-    x_low = shift(cotangent[-1:], "gx", 1)
-    x_high = shift(cotangent[:1], "gx", -1)
-    held = call(base_kernel, of((1, rows, width + ch), bf16), (raw,))
+    def both(shape):
+        return (of(shape, bf16), of(shape, bf16))
+
+    faces = call(faces_kernel, both((1, ny, nz, ch)), (cotangent,))
+    x_halo = swapped(*faces, "gx")
+    held, *width_faces = call(base_kernel, (of((1, rows, width + ch), bf16), *both((nx, ny, ch))), (raw, cotangent))
     held = joined(held, where.send(held, lambda s: dict(y=s["y"] ^ 1)))
-    y_low = shift(jnp.concatenate([a[:, -1] for a in (x_low, cotangent, x_high)], 0), "gy", 1)
-    y_high = shift(jnp.concatenate([a[:, 0] for a in (x_low, cotangent, x_high)], 0), "gy", -1)
+    faces = call(height_kernel, both((nx + 2, nz, ch)), (cotangent, *x_halo))
+    y_halo = swapped(*faces, "gy")
     held = joined(held, where.send(held, lambda s: dict(y=s["y"] ^ 2)))
-
-    def face(k):
-        deep = jnp.concatenate([a[:, :, k] for a in (x_low, cotangent, x_high)], 0)
-        return jnp.concatenate([y_low[:, None, k], deep, y_high[:, None, k]], 1)
-
-    z_low = shift(face(nz - 1), "gz", 1)
-    z_high = shift(face(0), "gz", -1)
+    faces = call(width_kernel, both((nx + 2, ny + 2, ch)), (*width_faces, *x_halo, *y_halo))
+    z_halo = swapped(*faces, "gz")
     held = joined(held, where.send(held, lambda s: dict(zl=s["zl"] ^ 1)))
 
     flops = 2 * nx * ny * nz * ch * width
     tap_views, keep, send = call(
         filter_kernel,
         (of((nx + 2, ny + 2, nz, 3 * ch), bf16), of((ch // 2, width), f32), of((ch // 2, width), bf16)),
-        (cotangent, x_low, x_high, y_low, y_high, z_low, z_high, inputs.reshape(-1, ch)),
+        (cotangent, *x_halo, *y_halo, *z_halo, inputs.reshape(-1, ch)),
         vmem=16,
         flops=2 * flops,
     )

time: 114 us -> 103 us (0.904)
  starting transfers between devices: 47.8 us -> 41.9 us
  waiting for transfers between devices: 30.4 us -> 26.2 us
    ppermute x6, starting transfers between devices: 14.9 us -> 9.04 us  [the longest x3 5.82 us: swapped(): lax.ppermute(first, axis, pairs(0))]
    ppermute x6, waiting for transfers between devices: 5.61 us -> 0.93 us  [the longest x3 0.92 us: swapped(): lax.ppermute(first, axis, pairs(0))]
    ppermute x7, starting transfers between devices: 14.6 us -> 11.6 us  [send(): return lax.ppermute(array, AXES, pairs)]
    all_to_all x2, starting transfers between devices: 18.4 us -> 21.2 us  [exchange(): lax.all_to_all(array, AXES, 0, 0, tiled=True, axis_index_groups=groups)]
    ppermute x7, waiting for transfers between devices: 12.8 us -> 14.2 us  [send(): return lax.ppermute(array, AXES, pairs)]
    unnamed x24 -> x16, local copies, waits for them, and re-layouts: 2.97 us -> 4.17 us
    pallas_call x8 -> x11, Pallas kernels: 11.7 us -> 12 us  [call(): pl.pallas_call(kernel, out_shape=out_shape, in_specs=[pl.BlockSpec(memory...]
  transfers between devices with their start and end apart: 15 -> 15, of which waited for: 6 -> 6; matrix products, arithmetic and copies ran while one was open for 1% -> 0% of each run, Pallas kernels for 9% -> 10%
where the time goes in v2:
time: 103 us
  starting transfers between devices  41.9 us (41%)
  waiting for transfers between devices  26.2 us (25%)
  blocking collectives  17.4 us (17%)
  Pallas kernels  12 us (12%)
  local copies, waits for them, and re-layouts  4.26 us (4%)
    all_to_all x2, starting transfers between devices, exchange(): lax.all_to_all(array, AXES, 0, 0, tiled=True, axis_index_groups=groups)  21.2 us
    all_to_all x1, blocking collectives, exchange(): lax.all_to_all(array, AXES, 0, 0, tiled=True, axis_index_groups=groups)  17.4 us
    ppermute x7, waiting for transfers between devices, send(): return lax.ppermute(array, AXES, pairs)  14.2 us
    pallas_call x11, Pallas kernels, call(): pl.pallas_call(kernel, out_shape=out_shape, in_specs=[pl.BlockSpec(memory...  12 us
    ppermute x7, starting transfers between devices, send(): return lax.ppermute(array, AXES, pairs)  11.6 us
    all_to_all x2, waiting for transfers between devices, exchange(): lax.all_to_all(array, AXES, 0, 0, tiled=True, axis_index_groups=groups)  11.1 us
    ppermute x3, starting transfers between devices, swapped(): lax.ppermute(first, axis, pairs(0))  5.82 us
    unnamed x16, local copies, waits for them, and re-layouts  4.17 us
  transfers between devices with their start and end apart: 15, of which 6 were waited for; matrix products, arithmetic and copies ran while one was open for 0% of the time, Pallas kernels for 10%

profile of v2, /device:TPU:1, one launch (start us, length us, event | category | flops | bytes accessed | tf_op | source)
XLA Modules:
  0.0 102.8 jit_solution(1692724722996453247)
XLA Ops:
  0.6 0.0 copy-start
  0.6 1.0 %copy-done = bf16[8,16,16,128]{3,2,1,0:T(8,128)(2,1)S(1)} copy-done((bf16[8,16,16,128]{3,2,1,0:T(8,128)(2,1)S(1)}, bf16[8,16,16,128]{3,2,1,0:T(8,128)(2,1)}, u32[]{:S(2)}) %copy-start) | copy-done | bytes 524312
  1.7 0.0 copy-start.1
  1.7 3.3 %collective-permute-start = (bf16[1,16,16,128]{3,2,1,0:T(8,128)(2,1)S(1)}, bf16[1,16,16,128]{3,2,1,0:T(8,128)(2,1)S(1)}, u32[]{:S(2)}, u32[]{:S(2)}) collective-permute-start(bf16[1,16,16,128]{3,2,1,0:T(8,128)(2,1)S(1)} %get-tuple-element.24), channel_id=1, source_target_pairs={{0,32},{64,96},{128,160},{192,224},{32,0},{96,64},{160,128},{224,1... | collective-permute-start | bytes 196616 | tf_op jit(solution)/shard_map/ppermute | solution.py:79
  5.0 1.9 %collective-permute-start.1 = (bf16[1,16,16,128]{3,2,1,0:T(8,128)(2,1)S(1)}, bf16[1,16,16,128]{3,2,1,0:T(8,128)(2,1)S(1)}, u32[]{:S(2)}, u32[]{:S(2)}) collective-permute-start(bf16[1,16,16,128]{3,2,1,0:T(8,128)(2,1)S(1)} %get-tuple-element.25), channel_id=1, source_target_pairs={{32,64},{96,128},{160,192},{64,32},{128,96},{192,160},{33,65},{97,... | collective-permute-start | bytes 196616 | tf_op jit(solution)/shard_map/ppermute | solution.py:79
  6.9 0.1 shard_map.52
  7.0 1.3 %collective-permute-start.7 = (bf16[1,4,3584]{2,1,0:T(4,128)(2,1)S(1)}, bf16[1,4,3584]{2,1,0:T(4,128)(2,1)S(1)}, u32[]{:S(2)}, u32[]{:S(2)}) collective-permute-start(bf16[1,4,3584]{2,1,0:T(4,128)(2,1)S(1)} %get-tuple-element.34), channel_id=1, source_target_pairs={{0,8},{1,9},{2,10},{3,11},{4,12},{5,13},{6,14},{7,15},{8,0},{9,1},... | collective-permute-start | bytes 86024 | tf_op jit(solution)/shard_map/ppermute | solution.py:62
  8.4 1.4 %collective-permute-done.7 = bf16[1,4,3584]{2,1,0:T(4,128)(2,1)S(1)} collective-permute-done((bf16[1,4,3584]{2,1,0:T(4,128)(2,1)S(1)}, bf16[1,4,3584]{2,1,0:T(4,128)(2,1)S(1)}, u32[]{:S(2)}, u32[]{:S(2)}) %collective-permute-start.7) | collective-permute-done | bytes 28704 | tf_op jit(solution)/shard_map/ppermute | solution.py:62
  9.9 3.0 %collective-permute-start.8 = (bf16[2,4,3584]{2,1,0:T(4,128)(2,1)S(1)}, bf16[2,4,3584]{2,1,0:T(4,128)(2,1)S(1)}, u32[]{:S(2)}, u32[]{:S(2)}) collective-permute-start(bf16[2,4,3584]{2,1,0:T(4,128)(2,1)S(1)} %pad_maximum_fusion.2), channel_id=1, source_target_pairs={{0,16},{1,17},{2,18},{3,19},{4,20},{5,21},{6,22},{7,23},{8,24},{9,... | collective-permute-start | bytes 172040 | tf_op jit(solution)/shard_map/ppermute | solution.py:62
  12.9 0.0 collective-permute-done.xa_ref
  13.0 0.0 copy-start.2
  13.0 0.5 collective-permute-start.2
  13.5 0.7 collective-permute-start.3
  14.1 0.8 collective-permute-done.8
  14.9 0.1 pad_maximum_fusion.1
  15.0 1.3 %collective-permute-start.9 = (bf16[4,4,3584]{2,1,0:T(4,128)(2,1)S(1)}, bf16[4,4,3584]{2,1,0:T(4,128)(2,1)S(1)}, u32[]{:S(2)}, u32[]{:S(2)}) collective-permute-start(bf16[4,4,3584]{2,1,0:T(4,128)(2,1)S(1)} %pad_maximum_fusion.1), channel_id=1, source_target_pairs={{0,64},{1,65},{2,66},{3,67},{4,68},{5,69},{6,70},{7,71},{8,72},{9,... | collective-permute-start | bytes 344072 | tf_op jit(solution)/shard_map/ppermute | solution.py:62
  16.3 0.0 collective-permute-done.2.ya_ref
  16.3 0.0 collective-permute-done.3.yb_ref
  16.3 0.1 shard_map.53
  16.4 2.1 %collective-permute-start.4 = (bf16[10,18,128]{2,1,0:T(8,128)(2,1)S(1)}, bf16[10,18,128]{2,1,0:T(8,128)(2,1)S(1)}, u32[]{:S(2)}, u32[]{:S(2)}) collective-permute-start(bf16[10,18,128]{2,1,0:T(8,128)(2,1)S(1)} %get-tuple-element.30), channel_id=1, source_target_pairs={{0,1},{2,3},{4,5},{6,7},{1,0},{3,2},{5,4},{7,6},{8,9},{10,11},{12,... | collective-permute-start | bytes 138248 | tf_op jit(solution)/shard_map/ppermute | solution.py:79
  18.5 0.7 collective-permute-start.5
  19.2 0.9 collective-permute-done.4.za_ref
  20.1 0.0 collective-permute-done.5.zb_ref
  20.1 3.4 %shard_map.54 = (bf16[10,18,16,384]{3,2,1,0:T(8,128)(2,1)S(1)}, f32[64,3456]{1,0:T(8,128)S(1)}, bf16[64,3456]{1,0:T(8,128)(2,1)S(1)}) custom-call(bf16[8,16,16,128]{3,2,1,0:T(8,128)(2,1)S(1)} %copy-done.1, bf16[1,16,16,128]{3,2,1,0:T(8,128)(2,1)S(1)} %collective-permute-done.xa_ref, bf16[1,16,16,128]{3,2,1,0:T(8,128)(2,1)S(1)} %collective-permute-done.1.xb_ref, ...), custom_call_target="tpu_custom_call" | custom-call | flops 3623878656 | bytes 1000000 | tf_op jit(solution)/shard_map/pallas_call | solution.py:22
  23.5 1.4 %copy-done.4 = bf16[10,18,16,384]{3,2,1,0:T(8,128)(2,1)} copy-done((bf16[10,18,16,384]{3,2,1,0:T(8,128)(2,1)}, bf16[10,18,16,384]{3,2,1,0:T(8,128)(2,1)S(1)}, u32[]{:S(2)}) %copy-start.4) | copy-done | bytes 2211864
  24.9 3.9 %collective-permute-start.6 = (bf16[64,3456]{1,0:T(8,128)(2,1)S(1)}, bf16[64,3456]{1,0:T(8,128)(2,1)S(1)}, u32[]{:S(2)}, u32[]{:S(2)}) collective-permute-start(bf16[64,3456]{1,0:T(8,128)(2,1)S(1)} %get-tuple-element.33), channel_id=1, source_target_pairs={{0,32},{1,33},{2,34},{3,35},{4,36},{5,37},{6,38},{7,39},{8,40},{9,... | collective-permute-start | bytes 1327112 | tf_op jit(solution)/shard_map/ppermute | solution.py:62
  28.7 0.0 collective-permute-done.9
  28.7 0.2 pad_maximum_fusion
  28.9 1.0 collective-permute-start.10
  29.9 0.1 constant_dynamic-update-slice_fusion.1
  29.9 11.9 %collective-permute-done.10 = bf16[8,4,3584]{2,1,0:T(4,128)(2,1)S(1)} collective-permute-done((bf16[8,4,3584]{2,1,0:T(4,128)(2,1)S(1)}, bf16[8,4,3584]{2,1,0:T(4,128)(2,1)S(1)}, u32[]{:S(2)}, u32[]{:S(2)}) %collective-permute-start.10) | collective-permute-done | bytes 229408 | tf_op jit(solution)/shard_map/ppermute | solution.py:62
  41.9 0.1 constant_dynamic-update-slice_fusion.near_ref
  42.0 0.5 collective-permute-start.11
  42.5 0.0 collective-permute-done.6.other_ref
  42.5 0.9 shard_map.55
  43.4 15.1 %all-to-all-start = ((bf16[16,4,3456]{2,1,0:T(4,128)(2,1)}), bf16[16,4,3456]{2,1,0:T(4,128)(2,1)S(1)}, u32[]{:S(2)}, u32[]{:S(2)}) async-start(bf16[16,4,3456]{2,1,0:T(4,128)(2,1)} %shard_map.55), calls=%async_computation | async-start | bytes 884736 | tf_op jit(solution)/shard_map/all_to_all | solution.py:69
  58.5 0.0 collective-permute-done.11.far_ref
  58.5 1.1 %shard_map.56 = (bf16[128,3456]{1,0:T(8,128)(2,1)S(1)}, f32[1,128]{1,0:T(1,128)S(1)}, f32[1,128]{1,0:T(1,128)S(1)}, f32[4,3456]{1,0:T(4,128)S(1)}) custom-call(bf16[16,4,3584]{2,1,0:T(4,128)(2,1)S(1)} %constant_dynamic-update-slice_fusion.near_ref, bf16[16,4,3584]{2,1,0:T(4,128)(2,1)S(1)} %collective-permute-done.11.far_ref), custom_call_target="tpu_custom_call" | custom-call | flops 3000000000 | bytes 1000000 | tf_op jit(solution)/shard_map/pallas_call | solution.py:22
  59.6 8.3 %all-to-all-done.parts_ref = bf16[16,4,3456]{2,1,0:T(4,128)(2,1)S(1)} async-done(((bf16[16,4,3456]{2,1,0:T(4,128)(2,1)}), bf16[16,4,3456]{2,1,0:T(4,128)(2,1)S(1)}, u32[]{:S(2)}, u32[]{:S(2)}) %all-to-all-start) | async-done | bytes 442400 | tf_op jit(solution)/shard_map/all_to_all | solution.py:69
  67.9 0.9 shard_map.57
  68.8 6.1 %all-to-all-start.1 = ((bf16[8,4,3456]{2,1,0:T(4,128)(2,1)}), bf16[8,4,3456]{2,1,0:T(4,128)(2,1)S(1)}, u32[]{:S(2)}, u32[]{:S(2)}) async-start(bf16[8,4,3456]{2,1,0:T(4,128)(2,1)} %shard_map.57), calls=%async_computation.1 | async-start | bytes 442368 | tf_op jit(solution)/shard_map/all_to_all | solution.py:69
  74.9 1.6 %copy-done.5 = bf16[10,18,16,384]{3,2,1,0:T(8,128)(2,1)S(1)} copy-done((bf16[10,18,16,384]{3,2,1,0:T(8,128)(2,1)S(1)}, bf16[10,18,16,384]{3,2,1,0:T(8,128)(2,1)}, u32[]{:S(2)}) %copy-start.5) | copy-done | bytes 2211864
  76.5 4.6 %shard_map.58 = bf16[8,16,16,128]{3,2,1,0:T(8,128)(2,1)} custom-call(bf16[10,18,16,384]{3,2,1,0:T(8,128)(2,1)S(1)} %copy-done.5, bf16[128,3456]{1,0:T(8,128)(2,1)S(1)} %get-tuple-element.38.std_ref), custom_call_target="tpu_custom_call" | custom-call | flops 3623878656 | bytes 1000000 | tf_op jit(solution)/shard_map/pallas_call | solution.py:22
  81.1 2.8 %all-to-all-done.1.parts_ref = bf16[8,4,3456]{2,1,0:T(4,128)(2,1)S(1)} async-done(((bf16[8,4,3456]{2,1,0:T(4,128)(2,1)}), bf16[8,4,3456]{2,1,0:T(4,128)(2,1)S(1)}, u32[]{:S(2)}, u32[]{:S(2)}) %all-to-all-start.1) | async-done | bytes 221216 | tf_op jit(solution)/shard_map/all_to_all | solution.py:69
  83.9 0.1 shard_map.59
  84.0 0.7 collective-permute-start.12
  84.7 17.4 %all_to_all.15.sums_ref = f32[32,1,384]{2,1,0:T(1,128)S(1)} all-to-all(f32[32,1,384]{2,1,0:T(1,128)S(1)} %get-tuple-element.45), channel_id=1, replica_groups={{0,8,16,24,1,9,17,25,2,10,18,26,3,11,19,27,32,40,48,56,33,41,49,57,34,4..., dimensions={0} | all-to-all | bytes 98304 | tf_op jit(solution)/shard_map/all_to_all | solution.py:69
  102.1 0.8 shard_map.60
  (14 shorter events, 0.2 us)
Async XLA Ops:
  0.6 1.0 %copy-start = (bf16[8,16,16,128]{3,2,1,0:T(8,128)(2,1)S(1)}, bf16[8,16,16,128]{3,2,1,0:T(8,128)(2,1)}, u32[]{:S(2)}) copy-start(bf16[8,16,16,128]{3,2,1,0:T(8,128)(2,1)} %mid_ref.7) | copy-start | bytes 1572868
  1.7 5.2 %copy-start.3 = (f32[4,27,128]{2,0,1:T(4,128)S(1)}, f32[4,27,128]{2,0,1:T(4,128)}, u32[]{:S(2)}) copy-start(f32[4,27,128]{2,0,1:T(4,128)} %param.3) | copy-start | bytes 165892
  1.7 11.2 %copy-start.1 = (bf16[8,16,16,128]{3,2,1,0:T(8,128)(2,1)S(1)}, bf16[8,16,16,128]{3,2,1,0:T(8,128)(2,1)}, u32[]{:S(2)}) copy-start(bf16[8,16,16,128]{3,2,1,0:T(8,128)(2,1)} %mid_ref.7) | copy-start | bytes 1572868
  1.7 11.2 %collective-permute-start = (bf16[1,16,16,128]{3,2,1,0:T(8,128)(2,1)S(1)}, bf16[1,16,16,128]{3,2,1,0:T(8,128)(2,1)S(1)}, u32[]{:S(2)}, u32[]{:S(2)}) collective-permute-start(bf16[1,16,16,128]{3,2,1,0:T(8,128)(2,1)S(1)} %get-tuple-element.24), channel_id=1, source_target_pairs={{0,32},{64,96},{128,160},{192,224},{32,0},{96,64},{160,128},{224,1... | collective-permute-start | bytes 196616 | tf_op jit(solution)/shard_map/ppermute | solution.py:79
  5.0 7.9 %collective-permute-start.1 = (bf16[1,16,16,128]{3,2,1,0:T(8,128)(2,1)S(1)}, bf16[1,16,16,128]{3,2,1,0:T(8,128)(2,1)S(1)}, u32[]{:S(2)}, u32[]{:S(2)}) collective-permute-start(bf16[1,16,16,128]{3,2,1,0:T(8,128)(2,1)S(1)} %get-tuple-element.25), channel_id=1, source_target_pairs={{32,64},{96,128},{160,192},{64,32},{128,96},{192,160},{33,65},{97,... | collective-permute-start | bytes 196616 | tf_op jit(solution)/shard_map/ppermute | solution.py:79
  7.0 2.8 %collective-permute-start.7 = (bf16[1,4,3584]{2,1,0:T(4,128)(2,1)S(1)}, bf16[1,4,3584]{2,1,0:T(4,128)(2,1)S(1)}, u32[]{:S(2)}, u32[]{:S(2)}) collective-permute-start(bf16[1,4,3584]{2,1,0:T(4,128)(2,1)S(1)} %get-tuple-element.34), channel_id=1, source_target_pairs={{0,8},{1,9},{2,10},{3,11},{4,12},{5,13},{6,14},{7,15},{8,0},{9,1},... | collective-permute-start | bytes 86024 | tf_op jit(solution)/shard_map/ppermute | solution.py:62
  9.9 5.0 %collective-permute-start.8 = (bf16[2,4,3584]{2,1,0:T(4,128)(2,1)S(1)}, bf16[2,4,3584]{2,1,0:T(4,128)(2,1)S(1)}, u32[]{:S(2)}, u32[]{:S(2)}) collective-permute-start(bf16[2,4,3584]{2,1,0:T(4,128)(2,1)S(1)} %pad_maximum_fusion.2), channel_id=1, source_target_pairs={{0,16},{1,17},{2,18},{3,19},{4,20},{5,21},{6,22},{7,23},{8,24},{9,... | collective-permute-start | bytes 172040 | tf_op jit(solution)/shard_map/ppermute | solution.py:62
  13.0 7.1 %copy-start.2 = (bf16[8,16,16,128]{3,2,1,0:T(8,128)(2,1)S(1)}, bf16[8,16,16,128]{3,2,1,0:T(8,128)(2,1)}, u32[]{:S(2)}) copy-start(bf16[8,16,16,128]{3,2,1,0:T(8,128)(2,1)} %param.4) | copy-start | bytes 1572868
  13.0 3.3 %collective-permute-start.2 = (bf16[10,16,128]{2,1,0:T(8,128)(2,1)S(1)}, bf16[10,16,128]{2,1,0:T(8,128)(2,1)S(1)}, u32[]{:S(2)}, u32[]{:S(2)}) collective-permute-start(bf16[10,16,128]{2,1,0:T(8,128)(2,1)S(1)} %get-tuple-element.26), channel_id=1, source_target_pairs={{0,8},{16,24},{8,0},{24,16},{1,9},{17,25},{9,1},{25,17},{2,10},{18... | collective-permute-start | bytes 122888 | tf_op jit(solution)/shard_map/ppermute | solution.py:79
  13.5 2.8 %collective-permute-start.3 = (bf16[10,16,128]{2,1,0:T(8,128)(2,1)S(1)}, bf16[10,16,128]{2,1,0:T(8,128)(2,1)S(1)}, u32[]{:S(2)}, u32[]{:S(2)}) collective-permute-start(bf16[10,16,128]{2,1,0:T(8,128)(2,1)S(1)} %get-tuple-element.27), channel_id=1, source_target_pairs={{8,16},{16,8},{9,17},{17,9},{10,18},{18,10},{11,19},{19,11},{12,20... | collective-permute-start | bytes 122888 | tf_op jit(solution)/shard_map/ppermute | solution.py:79
  15.0 13.7 %collective-permute-start.9 = (bf16[4,4,3584]{2,1,0:T(4,128)(2,1)S(1)}, bf16[4,4,3584]{2,1,0:T(4,128)(2,1)S(1)}, u32[]{:S(2)}, u32[]{:S(2)}) collective-permute-start(bf16[4,4,3584]{2,1,0:T(4,128)(2,1)S(1)} %pad_maximum_fusion.1), channel_id=1, source_target_pairs={{0,64},{1,65},{2,66},{3,67},{4,68},{5,69},{6,70},{7,71},{8,72},{9,... | collective-permute-start | bytes 344072 | tf_op jit(solution)/shard_map/ppermute | solution.py:62
  16.4 3.7 %collective-permute-start.4 = (bf16[10,18,128]{2,1,0:T(8,128)(2,1)S(1)}, bf16[10,18,128]{2,1,0:T(8,128)(2,1)S(1)}, u32[]{:S(2)}, u32[]{:S(2)}) collective-permute-start(bf16[10,18,128]{2,1,0:T(8,128)(2,1)S(1)} %get-tuple-element.30), channel_id=1, source_target_pairs={{0,1},{2,3},{4,5},{6,7},{1,0},{3,2},{5,4},{7,6},{8,9},{10,11},{12,... | collective-permute-start | bytes 138248 | tf_op jit(solution)/shard_map/ppermute | solution.py:79
  18.5 1.6 %collective-permute-start.5 = (bf16[10,18,128]{2,1,0:T(8,128)(2,1)S(1)}, bf16[10,18,128]{2,1,0:T(8,128)(2,1)S(1)}, u32[]{:S(2)}, u32[]{:S(2)}) collective-permute-start(bf16[10,18,128]{2,1,0:T(8,128)(2,1)S(1)} %get-tuple-element.31), channel_id=1, source_target_pairs={{1,2},{3,4},{5,6},{2,1},{4,3},{6,5},{9,10},{11,12},{13,14},{10,9},... | collective-permute-start | bytes 138248 | tf_op jit(solution)/shard_map/ppermute | solution.py:79
  23.5 1.4 %copy-start.4 = (bf16[10,18,16,384]{3,2,1,0:T(8,128)(2,1)}, bf16[10,18,16,384]{3,2,1,0:T(8,128)(2,1)S(1)}, u32[]{:S(2)}) copy-start(bf16[10,18,16,384]{3,2,1,0:T(8,128)(2,1)S(1)} %get-tuple-element.37.taps_ref) | copy-start | bytes 6635524
  24.9 17.6 %collective-permute-start.6 = (bf16[64,3456]{1,0:T(8,128)(2,1)S(1)}, bf16[64,3456]{1,0:T(8,128)(2,1)S(1)}, u32[]{:S(2)}, u32[]{:S(2)}) collective-permute-start(bf16[64,3456]{1,0:T(8,128)(2,1)S(1)} %get-tuple-element.33), channel_id=1, source_target_pairs={{0,32},{1,33},{2,34},{3,35},{4,36},{5,37},{6,38},{7,39},{8,40},{9,... | collective-permute-start | bytes 1327112 | tf_op jit(solution)/shard_map/ppermute | solution.py:62
  28.9 13.0 %collective-permute-start.10 = (bf16[8,4,3584]{2,1,0:T(4,128)(2,1)S(1)}, bf16[8,4,3584]{2,1,0:T(4,128)(2,1)S(1)}, u32[]{:S(2)}, u32[]{:S(2)}) collective-permute-start(bf16[8,4,3584]{2,1,0:T(4,128)(2,1)S(1)} %pad_maximum_fusion), channel_id=1, source_target_pairs={{0,128},{1,129},{2,130},{3,131},{4,132},{5,133},{6,134},{7,135},{8... | collective-permute-start | bytes 688136 | tf_op jit(solution)/shard_map/ppermute | solution.py:62
  42.0 16.5 %collective-permute-start.11 = (bf16[16,4,3584]{2,1,0:T(4,128)(2,1)S(1)}, bf16[16,4,3584]{2,1,0:T(4,128)(2,1)S(1)}, u32[]{:S(2)}, u32[]{:S(2)}) collective-permute-start(bf16[16,4,3584]{2,1,0:T(4,128)(2,1)S(1)} %constant_dynamic-update-slice_fusion.near_ref), channel_id=1, source_target_pairs={{0,32},{1,33},{2,34},{3,35},{4,36},{5,37},{6,38},{7,39},{8,40},{9,... | collective-permute-start | bytes 1376264 | tf_op jit(solution)/shard_map/ppermute | solution.py:62
  43.4 24.5 %all-to-all-start = ((bf16[16,4,3456]{2,1,0:T(4,128)(2,1)}), bf16[16,4,3456]{2,1,0:T(4,128)(2,1)S(1)}, u32[]{:S(2)}, u32[]{:S(2)}) async-start(bf16[16,4,3456]{2,1,0:T(4,128)(2,1)} %shard_map.55), calls=%async_computation | async-start | bytes 884736 | tf_op jit(solution)/shard_map/all_to_all | solution.py:69
  68.8 15.1 %all-to-all-start.1 = ((bf16[8,4,3456]{2,1,0:T(4,128)(2,1)}), bf16[8,4,3456]{2,1,0:T(4,128)(2,1)S(1)}, u32[]{:S(2)}, u32[]{:S(2)}) async-start(bf16[8,4,3456]{2,1,0:T(4,128)(2,1)} %shard_map.57), calls=%async_computation.1 | async-start | bytes 442368 | tf_op jit(solution)/shard_map/all_to_all | solution.py:69
  74.9 1.6 %copy-start.5 = (bf16[10,18,16,384]{3,2,1,0:T(8,128)(2,1)S(1)}, bf16[10,18,16,384]{3,2,1,0:T(8,128)(2,1)}, u32[]{:S(2)}) copy-start(bf16[10,18,16,384]{3,2,1,0:T(8,128)(2,1)} %copy-done.4) | copy-start | bytes 6635524
  84.0 18.1 %collective-permute-start.12 = (f32[4,3456]{1,0:T(4,128)S(1)}, f32[4,3456]{1,0:T(4,128)S(1)}, u32[]{:S(2)}, u32[]{:S(2)}) collective-permute-start(f32[4,3456]{1,0:T(4,128)S(1)} %get-tuple-element.42), channel_id=1, source_target_pairs={{0,0},{1,64},{2,128},{3,192},{4,4},{5,68},{6,132},{7,196},{8,8},{9... | collective-permute-start | bytes 165896 | tf_op jit(solution)/shard_map/ppermute | solution.py:62

commit v3 on v1

--- a/solution.py
+++ b/solution.py
@@ -61,6 +61,13 @@
             pairs.append((self.index(s), self.index(t)))
         return lax.ppermute(array, AXES, pairs)
 
+    def pass_on(self, array, step):
+        pairs = []
+        for s in self.spots():
+            if s["x"] == s["zl"]:
+                pairs.append((self.index(s), self.index(dict(s, x=(s["x"] + step) % self.x))))
+        return lax.ppermute(array, AXES, pairs)
+
     def exchange(self, array, fixed, order):
         groups = {}
         for s in self.spots():
@@ -69,13 +76,18 @@
         return lax.all_to_all(array, AXES, 0, 0, tiled=True, axis_index_groups=groups)
 
 
-def shift(array, axis, step):
+def swapped(first, second, axis):
     count = lax.axis_size(axis)
-    if step > 0:
-        pairs = [(i, i + 1) for i in range(count - 1)]
-    else:
-        pairs = [(i + 1, i) for i in range(count - 1)]
-    return lax.ppermute(array, axis, pairs)
+
+    def pairs(start):
+        ends = [(i, i + 1) for i in range(start, count - 1, 2)]
+        return ends + [(j, i) for i, j in ends]
+
+    return lax.ppermute(first, axis, pairs(0)), lax.ppermute(second, axis, pairs(1))
+
+
+def is_odd(axis):
+    return lax.axis_index(axis) % 2 == 1
 
 
 def wide(row, taps=TAPS):
@@ -87,6 +99,45 @@
     for t in range(1, values.shape[1] // ch):
         total = total + values[:, t * ch : (t + 1) * ch]
     return jnp.sum(total, axis=0, keepdims=True)
+
+
+def picked(odd, first, second):
+    return jnp.where(odd, first, second), jnp.where(odd, second, first)
+
+
+def width_kernel(mid_ref, first_ref, second_ref):
+    nx, _, nz, _ = mid_ref.shape
+    odd = is_odd("gz")
+    for k in range(nx):
+        mid = mid_ref[k].astype(jnp.float32)
+        low, high = mid[:, 0], mid[:, nz - 1]
+        first_ref[k] = jnp.where(odd, low, high).astype(jnp.bfloat16)
+        second_ref[k] = jnp.where(odd, high, low).astype(jnp.bfloat16)
+
+
+def height_kernel(mid_ref, za_ref, zb_ref, first_ref, second_ref):
+    nx, ny, nz, _ = mid_ref.shape
+    odd = is_odd("gy")
+    low, high = picked(is_odd("gz"), za_ref[...].astype(jnp.float32), zb_ref[...].astype(jnp.float32))
+    ends = [jnp.concatenate([low[:, None, j], high[:, None, j]], axis=1) for j in (0, ny - 1)]
+    first_end, last_end = (e.astype(jnp.bfloat16) for e in ends)
+    for k in range(nx):
+        first_ref[k, :nz] = mid_ref[k, jnp.where(odd, 0, ny - 1)]
+        second_ref[k, :nz] = mid_ref[k, jnp.where(odd, ny - 1, 0)]
+    first_ref[:, nz:] = jnp.where(odd, first_end, last_end)
+    second_ref[:, nz:] = jnp.where(odd, last_end, first_end)
+
+
+def depth_kernel(mid_ref, za_ref, zb_ref, ya_ref, yb_ref, first_ref, second_ref):
+    nx, ny, nz, _ = mid_ref.shape
+    z_odd, y_odd, odd = is_odd("gz"), is_odd("gy"), is_odd("gx")
+    for out_ref, k in ((first_ref, jnp.where(odd, 0, nx - 1)), (second_ref, jnp.where(odd, nx - 1, 0))):
+        low, high = picked(z_odd, za_ref[k].astype(jnp.float32), zb_ref[k].astype(jnp.float32))
+        out_ref[1 : ny + 1, :nz] = mid_ref[k]
+        out_ref[1 : ny + 1, nz:] = jnp.concatenate([low[:, None], high[:, None]], axis=1).astype(jnp.bfloat16)
+        low, high = picked(y_odd, ya_ref[k], yb_ref[k])
+        out_ref[0] = low
+        out_ref[ny + 1] = high
 
 
 def base_kernel(raw_ref, held_ref):
@@ -102,32 +153,42 @@
     held_ref[0, :, taps * ch :] = both.astype(jnp.bfloat16)
 
 
-def filter_kernel(mid_ref, xl_ref, xh_ref, yl_ref, yh_ref, zl_ref, zh_ref, in_ref, taps_ref, keep_ref, send_ref):
+def join_kernel(*refs):
+    place = 0
+    for piece in refs[:-1]:
+        refs[-1][place : place + piece.shape[0]] = piece[...]
+        place += piece.shape[0]
+
+
+def filter_kernel(mid_ref, za_ref, zb_ref, ya_ref, yb_ref, xa_ref, xb_ref, in_ref, taps_ref, keep_ref, send_ref):
     nx, ny, nz, ch = mid_ref.shape
-
-    def fill(k, rows, j, n):
+    x_odd, y_odd, z_odd = is_odd("gx"), is_odd("gy"), is_odd("gz")
+
+    def fill(k, j, rows, low, high):
+        n = rows.shape[0]
         mid = rows.astype(jnp.float32)
-        low = zl_ref[k, j : j + n].astype(jnp.float32)[:, None, :]
-        high = zh_ref[k, j : j + n].astype(jnp.float32)[:, None, :]
         up = jnp.concatenate([mid[:, 1:], high], axis=1)
         down = jnp.concatenate([low, mid[:, :-1]], axis=1)
         taps_ref[k, j : j + n, :, 0:ch] = up.astype(jnp.bfloat16)
         taps_ref[k, j : j + n, :, ch : 2 * ch] = rows
         taps_ref[k, j : j + n, :, 2 * ch : 3 * ch] = down.astype(jnp.bfloat16)
 
+    def fill_face(k, j, rows):
+        ends = rows[:, nz:].astype(jnp.float32)
+        fill(k, j, rows[:, :nz], ends[:, 0:1], ends[:, 1:2])
+
     def plane(k, carry):
-        fill(k, yl_ref[k][None], 0, 1)
-        fill(k, yh_ref[k][None], ny + 1, 1)
+        low, high = picked(z_odd, za_ref[k].astype(jnp.float32), zb_ref[k].astype(jnp.float32))
+        fill(k + 1, 1, mid_ref[k], low[:, None], high[:, None])
+        low, high = picked(y_odd, ya_ref[k], yb_ref[k])
+        fill_face(k + 1, 0, low[None])
+        fill_face(k + 1, ny + 1, high[None])
         return carry
 
-    def middle(k, carry):
-        fill(k + 1, mid_ref[k], 1, ny)
-        return carry
-
-    lax.fori_loop(0, nx, middle, 0)
-    fill(0, xl_ref[0], 1, ny)
-    fill(nx + 1, xh_ref[0], 1, ny)
-    lax.fori_loop(0, nx + 2, plane, 0)
+    lax.fori_loop(0, nx, plane, 0)
+    low, high = picked(x_odd, xa_ref[...], xb_ref[...])
+    fill_face(0, 0, low)
+    fill_face(nx + 1, 0, high)
     cells = nx * ny * nz
     flat = in_ref[...].T
     core = lax.axis_index("gx") % CORES
@@ -219,8 +280,14 @@
     block_ref[...] = (values + wide(base - mean)) * inv_wide
 
 
-def last_kernel(fan_count, grad_ref, raw_ref, mean_ref, inv_ref, sums_ref, out_ref):
+def last_kernel(fan_count, x_count, own_ref, *refs):
+    *got_refs, raw_ref, mean_ref, inv_ref, sums_ref, out_ref = refs
     taps, _, ch = raw_ref.shape
+    grad = got_refs[0][...]
+    for got_ref in got_refs[1:]:
+        grad = grad + got_ref[...]
+    holder = lax.axis_index("gz") % x_count == lax.axis_index("gx") // CORES
+    grad = jnp.where(holder, own_ref[...], grad)
     sums = jnp.sum(sums_ref[...], axis=0)
     sum_grad, sum_cross, sum_square = sums[:, :ch], sums[:, ch : 2 * ch], sums[:, 2 * ch :]
     mean, inv = mean_ref[...], inv_ref[...]
@@ -234,7 +301,7 @@
     factor = inv * scale
     for t in range(taps):
         std = (raw_ref[t] - mean) * inv
-        out_ref[t] = factor * (grad_ref[:, t * ch : (t + 1) * ch] - mean_grad - std * mean_cross)
+        out_ref[t] = factor * (grad[:, t * ch : (t + 1) * ch] - mean_grad - std * mean_cross)
 
 
 def on_device(where, raw_weight, inputs, cotangent):
@@ -244,35 +311,34 @@
     bf16, f32 = jnp.bfloat16, jnp.float32
     raw = jnp.transpose(raw_weight, (1, 0, 2))
 
-    def joined(held, got):
-        return jnp.concatenate([held, got], 0)
-
-    x_low = shift(cotangent[-1:], "gx", 1)
-    x_high = shift(cotangent[:1], "gx", -1)
-    held = call(base_kernel, of((1, rows, width + ch), bf16), (raw,))
-    held = joined(held, where.send(held, lambda s: dict(y=s["y"] ^ 1)))
-    y_low = shift(jnp.concatenate([a[:, -1] for a in (x_low, cotangent, x_high)], 0), "gy", 1)
-    y_high = shift(jnp.concatenate([a[:, 0] for a in (x_low, cotangent, x_high)], 0), "gy", -1)
-    held = joined(held, where.send(held, lambda s: dict(y=s["y"] ^ 2)))
-
-    def face(k):
-        deep = jnp.concatenate([a[:, :, k] for a in (x_low, cotangent, x_high)], 0)
-        return jnp.concatenate([y_low[:, None, k], deep, y_high[:, None, k]], 1)
-
-    z_low = shift(face(nz - 1), "gz", 1)
-    z_high = shift(face(0), "gz", -1)
-    held = joined(held, where.send(held, lambda s: dict(zl=s["zl"] ^ 1)))
+    def joined(held):
+        return jnp.concatenate(held, 0)
+
+    def both(shape):
+        return (of(shape, bf16), of(shape, bf16))
+
+    faces = call(width_kernel, both((nx, ny, ch)), (cotangent,))
+    z_halo = swapped(*faces, "gz")
+    held = [call(base_kernel, of((1, rows, width + ch), bf16), (raw,))]
+    held.append(where.send(held[0], lambda s: dict(y=s["y"] ^ 1)))
+    held.append(where.send(joined(held), lambda s: dict(y=s["y"] ^ 2)))
+    faces = call(height_kernel, both((nx, nz + 2, ch)), (cotangent, *z_halo))
+    y_halo = swapped(*faces, "gy")
+    held.append(where.send(joined(held), lambda s: dict(zl=s["zl"] ^ 1)))
+    faces = call(depth_kernel, both((ny + 2, nz + 2, ch)), (cotangent, *z_halo, *y_halo))
+    x_halo = swapped(*faces, "gx")
+    held.append(where.send(joined(held), lambda s: dict(zl=s["zl"] ^ 2)))
 
     flops = 2 * nx * ny * nz * ch * width
     tap_views, keep, send = call(
         filter_kernel,
         (of((nx + 2, ny + 2, nz, 3 * ch), bf16), of((ch // 2, width), f32), of((ch // 2, width), bf16)),
-        (cotangent, x_low, x_high, y_low, y_high, z_low, z_high, inputs.reshape(-1, ch)),
+        (cotangent, *z_halo, *y_halo, *x_halo, inputs.reshape(-1, ch)),
         vmem=16,
         flops=2 * flops,
     )
     other = where.send(send, lambda s: dict(core=1 - s["core"]))
-    held = joined(held, where.send(held, lambda s: dict(zl=s["zl"] ^ 2)))
+    held = call(join_kernel, of((16, rows, width + ch), bf16), held)
     peers = where.x * where.gy
     half = call(pair_kernel, of((peers, rows, width), bf16), (keep, other))
     parts = where.exchange(half, ("core", "zl", "zh"), lambda s: (s["x"], s["y"]))
@@ -290,10 +356,10 @@
     parts, input_grad = lax.optimization_barrier((parts, input_grad))
     everyone = CORES * where.x * where.gy
     block_grad, local = call(block_kernel, (of((rows, width), f32), of((everyone, 1, 3 * ch), f32)), (parts, block_std))
-    filter_grad = where.send(block_grad, lambda s: dict(x=s["zl"], zl=s["x"]))
+    passed = [where.pass_on(block_grad, k) for k in range(1, where.x)]
     sums = where.exchange(local, ("zl", "zh"), lambda s: (s["core"], s["x"], s["y"]))
 
-    grad = call(functools.partial(last_kernel, float(ch * taps)), of((taps, rows, ch), f32), (filter_grad, raw, mean_out, inv_std, sums))
+    grad = call(functools.partial(last_kernel, float(ch * taps), where.x), of((taps, rows, ch), f32), (block_grad, *passed, raw, mean_out, inv_std, sums))
     return (input_grad, jnp.transpose(grad, (1, 0, 2)))
 
 

time: 114 us -> 95.1 us (0.83)
  waiting for transfers between devices: 30.4 us -> 20 us
  blocking collectives: 17.4 us -> 13.7 us
  local copies, waits for them, and re-layouts: 4.19 us -> 1.51 us
  starting transfers between devices: 47.8 us -> 46.2 us
    ppermute x6 -> x9, waiting for transfers between devices: 5.61 us -> 0.07 us  [the longest x3 0.05 us: swapped(): lax.ppermute(second, axis, pairs(1))]
    ppermute x7 -> x6, waiting for transfers between devices: 12.8 us -> 7.79 us  [send(): return lax.ppermute(array, AXES, pairs)]
    all_to_all x1, blocking collectives: 17.4 us -> 13.7 us  [exchange(): lax.all_to_all(array, AXES, 0, 0, tiled=True, axis_index_groups=groups)]
    ppermute x7 -> x6, starting transfers between devices: 14.6 us -> 11.1 us  [send(): return lax.ppermute(array, AXES, pairs)]
    all_to_all x2, starting transfers between devices: 18.4 us -> 21.3 us  [exchange(): lax.all_to_all(array, AXES, 0, 0, tiled=True, axis_index_groups=groups)]
    unnamed x24 -> x16, local copies, waits for them, and re-layouts: 2.97 us -> 1.51 us
    ppermute x6 -> x9, starting transfers between devices: 14.9 us -> 13.8 us  [the longest x3 5.09 us: pass_on(): return lax.ppermute(array, AXES, pairs)]
    pallas_call x8 -> x12, Pallas kernels: 11.7 us -> 12 us  [call(): pl.pallas_call(kernel, out_shape=out_shape, in_specs=[pl.BlockSpec(memory...]
  transfers between devices with their start and end apart: 15 -> 17, of which waited for: 6 -> 4; matrix products, arithmetic and copies ran while one was open for 1% -> 0% of each run, Pallas kernels for 9% -> 11%
where the time goes in v3:
time: 95.1 us; the launch traced here: 94.6 us
  starting transfers between devices  46.2 us (49%)
  waiting for transfers between devices  20 us (21%)
  blocking collectives  13.7 us (14%)
  Pallas kernels  12 us (13%)
  local copies, waits for them, and re-layouts  1.51 us (2%)
    all_to_all x2, starting transfers between devices, exchange(): lax.all_to_all(array, AXES, 0, 0, tiled=True, axis_index_groups=groups)  21.3 us
    all_to_all x1, blocking collectives, exchange(): lax.all_to_all(array, AXES, 0, 0, tiled=True, axis_index_groups=groups)  13.7 us
    all_to_all x2, waiting for transfers between devices, exchange(): lax.all_to_all(array, AXES, 0, 0, tiled=True, axis_index_groups=groups)  12.2 us
    pallas_call x12, Pallas kernels, call(): pl.pallas_call(kernel, out_shape=out_shape, in_specs=[pl.BlockSpec(memory...  12 us
    ppermute x6, starting transfers between devices, send(): return lax.ppermute(array, AXES, pairs)  11.1 us
    ppermute x6, waiting for transfers between devices, send(): return lax.ppermute(array, AXES, pairs)  7.79 us
    ppermute x3, starting transfers between devices, pass_on(): return lax.ppermute(array, AXES, pairs)  5.09 us
    ppermute x3, starting transfers between devices, swapped(): lax.ppermute(second, axis, pairs(1))  4.44 us
  transfers between devices with their start and end apart: 17, of which 4 were waited for; matrix products, arithmetic and copies ran while one was open for 0% of the time, Pallas kernels for 11%

profile of v3, /device:TPU:1, one launch (start us, length us, event | category | flops | bytes accessed | tf_op | source)
XLA Modules:
  0.0 94.6 jit_solution(14688118559306966922)
XLA Ops:
  0.6 0.0 copy-start.2
  0.7 0.9 copy-done.2
  1.5 0.1 shard_map.55.refs_0_
  1.6 2.2 %collective-permute-start.7 = (bf16[1,4,3584]{2,1,0:T(4,128)(2,1)S(1)}, bf16[1,4,3584]{2,1,0:T(4,128)(2,1)S(1)}, u32[]{:S(2)}, u32[]{:S(2)}) collective-permute-start(bf16[1,4,3584]{2,1,0:T(4,128)(2,1)S(1)} %shard_map.55.refs_0_), channel_id=1, source_target_pairs={{0,8},{1,9},{2,10},{3,11},{4,12},{5,13},{6,14},{7,15},{8,0},{9,1},... | collective-permute-start | bytes 86024 | tf_op jit(solution)/shard_map/ppermute | solution.py:62
  3.8 0.3 shard_map.50
  4.0 1.3 %collective-permute-start = (bf16[8,16,128]{2,1,0:T(8,128)(2,1)S(1)}, bf16[8,16,128]{2,1,0:T(8,128)(2,1)S(1)}, u32[]{:S(2)}, u32[]{:S(2)}) collective-permute-start(bf16[8,16,128]{2,1,0:T(8,128)(2,1)S(1)} %get-tuple-element.21), channel_id=1, source_target_pairs={{0,1},{2,3},{4,5},{6,7},{1,0},{3,2},{5,4},{7,6},{8,9},{10,11},{12,... | collective-permute-start | bytes 98312 | tf_op jit(solution)/shard_map/ppermute | solution.py:86
  5.3 0.7 collective-permute-start.1
  6.0 0.0 collective-permute-done.7.refs_1_
  6.1 2.7 %collective-permute-start.8 = (bf16[2,4,3584]{2,1,0:T(4,128)(2,1)S(1)}, bf16[2,4,3584]{2,1,0:T(4,128)(2,1)S(1)}, u32[]{:S(2)}, u32[]{:S(2)}) collective-permute-start(bf16[2,4,3584]{2,1,0:T(4,128)(2,1)S(1)} %pad_maximum_fusion.2), channel_id=1, source_target_pairs={{0,16},{1,17},{2,18},{3,19},{4,20},{5,21},{6,22},{7,23},{8,24},{9,... | collective-permute-start | bytes 172040 | tf_op jit(solution)/shard_map/ppermute | solution.py:62
  8.8 0.0 collective-permute-done.za_ref
  8.8 0.0 copy-start.1
  8.8 0.1 collective-permute-start.2
  8.9 0.8 collective-permute-start.3
  9.7 1.0 %collective-permute-done.8.refs_2_ = bf16[2,4,3584]{2,1,0:T(4,128)(2,1)S(1)} collective-permute-done((bf16[2,4,3584]{2,1,0:T(4,128)(2,1)S(1)}, bf16[2,4,3584]{2,1,0:T(4,128)(2,1)S(1)}, u32[]{:S(2)}, u32[]{:S(2)}) %collective-permute-start.8) | collective-permute-done | bytes 57376 | tf_op jit(solution)/shard_map/ppermute | solution.py:62
  10.7 0.1 pad_maximum_fusion.1
  10.8 1.7 %collective-permute-start.9 = (bf16[4,4,3584]{2,1,0:T(4,128)(2,1)S(1)}, bf16[4,4,3584]{2,1,0:T(4,128)(2,1)S(1)}, u32[]{:S(2)}, u32[]{:S(2)}) collective-permute-start(bf16[4,4,3584]{2,1,0:T(4,128)(2,1)S(1)} %pad_maximum_fusion.1), channel_id=1, source_target_pairs={{0,64},{1,65},{2,66},{3,67},{4,68},{5,69},{6,70},{7,71},{8,72},{9,... | collective-permute-start | bytes 344072 | tf_op jit(solution)/shard_map/ppermute | solution.py:62
  12.5 0.0 collective-permute-done.2.ya_ref
  12.5 0.0 collective-permute-done.3.yb_ref
  12.5 0.1 shard_map.52
  12.6 2.9 %collective-permute-start.4 = (bf16[18,18,128]{2,1,0:T(8,128)(2,1)S(1)}, bf16[18,18,128]{2,1,0:T(8,128)(2,1)S(1)}, u32[]{:S(2)}, u32[]{:S(2)}) collective-permute-start(bf16[18,18,128]{2,1,0:T(8,128)(2,1)S(1)} %get-tuple-element.25), channel_id=1, source_target_pairs={{0,32},{64,96},{128,160},{192,224},{32,0},{96,64},{160,128},{224,1... | collective-permute-start | bytes 248840 | tf_op jit(solution)/shard_map/ppermute | solution.py:86
  15.4 3.0 %collective-permute-start.5 = (bf16[18,18,128]{2,1,0:T(8,128)(2,1)S(1)}, bf16[18,18,128]{2,1,0:T(8,128)(2,1)S(1)}, u32[]{:S(2)}, u32[]{:S(2)}) collective-permute-start(bf16[18,18,128]{2,1,0:T(8,128)(2,1)S(1)} %get-tuple-element.26), channel_id=1, source_target_pairs={{32,64},{96,128},{160,192},{64,32},{128,96},{192,160},{33,65},{97,... | collective-permute-start | bytes 248840 | tf_op jit(solution)/shard_map/ppermute | solution.py:86
  18.4 0.0 collective-permute-done.9.refs_3_
  18.4 0.2 pad_maximum_fusion
  18.6 2.8 %collective-permute-start.10 = (bf16[8,4,3584]{2,1,0:T(4,128)(2,1)S(1)}, bf16[8,4,3584]{2,1,0:T(4,128)(2,1)S(1)}, u32[]{:S(2)}, u32[]{:S(2)}) collective-permute-start(bf16[8,4,3584]{2,1,0:T(4,128)(2,1)S(1)} %pad_maximum_fusion), channel_id=1, source_target_pairs={{0,128},{1,129},{2,130},{3,131},{4,132},{5,133},{6,134},{7,135},{8... | collective-permute-start | bytes 688136 | tf_op jit(solution)/shard_map/ppermute | solution.py:62
  21.4 0.0 collective-permute-done.5.xb_ref
  21.5 3.2 %shard_map.53 = (bf16[10,18,16,384]{3,2,1,0:T(8,128)(2,1)S(1)}, f32[64,3456]{1,0:T(8,128)S(1)}, bf16[64,3456]{1,0:T(8,128)(2,1)S(1)}) custom-call(bf16[8,16,16,128]{3,2,1,0:T(8,128)(2,1)S(1)} %copy-done, bf16[8,16,128]{2,1,0:T(8,128)(2,1)S(1)} %collective-permute-done.za_ref, bf16[8,16,128]{2,1,0:T(8,128)(2,1)S(1)} %collective-permute-done.1.zb_ref, ...), custom_call_target="tpu_custom_call" | custom-call | flops 3623878656 | bytes 1000000 | tf_op jit(solution)/shard_map/pallas_call | solution.py:22
  24.7 0.3 collective-permute-start.6
  25.1 6.8 %collective-permute-done.10.refs_4_ = bf16[8,4,3584]{2,1,0:T(4,128)(2,1)S(1)} collective-permute-done((bf16[8,4,3584]{2,1,0:T(4,128)(2,1)S(1)}, bf16[8,4,3584]{2,1,0:T(4,128)(2,1)S(1)}, u32[]{:S(2)}, u32[]{:S(2)}) %collective-permute-start.10) | collective-permute-done | bytes 229408 | tf_op jit(solution)/shard_map/ppermute | solution.py:62
  31.9 1.4 %collective-permute-start.11 = (bf16[16,4,3584]{2,1,0:T(4,128)(2,1)S(1)}, bf16[16,4,3584]{2,1,0:T(4,128)(2,1)S(1)}, u32[]{:S(2)}, u32[]{:S(2)}) collective-permute-start(bf16[16,4,3584]{2,1,0:T(4,128)(2,1)S(1)} %shard_map.56.near_ref), channel_id=1, source_target_pairs={{0,32},{1,33},{2,34},{3,35},{4,36},{5,37},{6,38},{7,39},{8,40},{9,... | collective-permute-start | bytes 1376264 | tf_op jit(solution)/shard_map/ppermute | solution.py:62
  33.3 0.0 collective-permute-done.6.other_ref
  33.3 0.9 shard_map.54
  34.2 15.4 %all-to-all-start = ((bf16[16,4,3456]{2,1,0:T(4,128)(2,1)}), bf16[16,4,3456]{2,1,0:T(4,128)(2,1)S(1)}, u32[]{:S(2)}, u32[]{:S(2)}) async-start(bf16[16,4,3456]{2,1,0:T(4,128)(2,1)} %shard_map.54), calls=%async_computation | async-start | bytes 884736 | tf_op jit(solution)/shard_map/all_to_all | solution.py:76
  49.6 0.0 collective-permute-done.11.far_ref
  49.6 1.1 %shard_map.57 = (bf16[128,3456]{1,0:T(8,128)(2,1)S(1)}, f32[1,128]{1,0:T(1,128)S(1)}, f32[1,128]{1,0:T(1,128)S(1)}, f32[4,3456]{1,0:T(4,128)S(1)}) custom-call(bf16[16,4,3584]{2,1,0:T(4,128)(2,1)S(1)} %shard_map.56.near_ref, bf16[16,4,3584]{2,1,0:T(4,128)(2,1)S(1)} %collective-permute-done.11.far_ref), custom_call_target="tpu_custom_call" | custom-call | flops 3000000000 | bytes 1000000 | tf_op jit(solution)/shard_map/pallas_call | solution.py:22
  50.7 0.0 copy-start.6
  50.7 0.6 copy-done.6
  51.3 7.8 %all-to-all-done.parts_ref = bf16[16,4,3456]{2,1,0:T(4,128)(2,1)S(1)} async-done(((bf16[16,4,3456]{2,1,0:T(4,128)(2,1)}), bf16[16,4,3456]{2,1,0:T(4,128)(2,1)S(1)}, u32[]{:S(2)}, u32[]{:S(2)}) %all-to-all-start) | async-done | bytes 442400 | tf_op jit(solution)/shard_map/all_to_all | solution.py:76
  59.1 0.9 shard_map.58
  60.0 5.9 %all-to-all-start.1 = ((bf16[8,4,3456]{2,1,0:T(4,128)(2,1)}), bf16[8,4,3456]{2,1,0:T(4,128)(2,1)S(1)}, u32[]{:S(2)}, u32[]{:S(2)}) async-start(bf16[8,4,3456]{2,1,0:T(4,128)(2,1)} %shard_map.58), calls=%async_computation.1 | async-start | bytes 442368 | tf_op jit(solution)/shard_map/all_to_all | solution.py:76
  65.9 0.0 copy-start.7
  65.9 4.6 %shard_map.59 = bf16[8,16,16,128]{3,2,1,0:T(8,128)(2,1)} custom-call(bf16[10,18,16,384]{3,2,1,0:T(8,128)(2,1)S(1)} %copy-done.5, bf16[128,3456]{1,0:T(8,128)(2,1)S(1)} %get-tuple-element.32.std_ref), custom_call_target="tpu_custom_call" | custom-call | flops 3623878656 | bytes 1000000 | tf_op jit(solution)/shard_map/pallas_call | solution.py:22
  70.5 4.4 %all-to-all-done.1.parts_ref = bf16[8,4,3456]{2,1,0:T(4,128)(2,1)S(1)} async-done(((bf16[8,4,3456]{2,1,0:T(4,128)(2,1)}), bf16[8,4,3456]{2,1,0:T(4,128)(2,1)S(1)}, u32[]{:S(2)}, u32[]{:S(2)}) %all-to-all-start.1) | async-done | bytes 221216 | tf_op jit(solution)/shard_map/all_to_all | solution.py:76
  74.9 0.1 shard_map.60
  75.0 1.7 %collective-permute-start.12 = (f32[4,3456]{1,0:T(4,128)S(1)}, f32[4,3456]{1,0:T(4,128)S(1)}, u32[]{:S(2)}, u32[]{:S(2)}) collective-permute-start(f32[4,3456]{1,0:T(4,128)S(1)} %get-tuple-element.36.own_ref), channel_id=1, source_target_pairs={{0,1},{4,5},{8,9},{12,13},{16,17},{20,21},{24,25},{28,29},{32,33},... | collective-permute-start | bytes 165896 | tf_op jit(solution)/shard_map/ppermute | solution.py:69
  76.7 2.1 %collective-permute-start.13 = (f32[4,3456]{1,0:T(4,128)S(1)}, f32[4,3456]{1,0:T(4,128)S(1)}, u32[]{:S(2)}, u32[]{:S(2)}) collective-permute-start(f32[4,3456]{1,0:T(4,128)S(1)} %get-tuple-element.36.own_ref), channel_id=1, source_target_pairs={{0,2},{4,6},{8,10},{12,14},{16,18},{20,22},{24,26},{28,30},{32,34}... | collective-permute-start | bytes 165896 | tf_op jit(solution)/shard_map/ppermute | solution.py:69
  78.8 1.3 %collective-permute-start.14 = (f32[4,3456]{1,0:T(4,128)S(1)}, f32[4,3456]{1,0:T(4,128)S(1)}, u32[]{:S(2)}, u32[]{:S(2)}) collective-permute-start(f32[4,3456]{1,0:T(4,128)S(1)} %get-tuple-element.36.own_ref), channel_id=1, source_target_pairs={{0,3},{4,7},{8,11},{12,15},{16,19},{20,23},{24,27},{28,31},{32,35}... | collective-permute-start | bytes 165896 | tf_op jit(solution)/shard_map/ppermute | solution.py:69
  80.1 13.7 %all_to_all.15.refs_6_ = f32[32,1,384]{2,1,0:T(1,128)S(1)} all-to-all(f32[32,1,384]{2,1,0:T(1,128)S(1)} %get-tuple-element.39), channel_id=1, replica_groups={{0,8,16,24,1,9,17,25,2,10,18,26,3,11,19,27,32,40,48,56,33,41,49,57,34,4..., dimensions={0} | all-to-all | bytes 98304 | tf_op jit(solution)/shard_map/all_to_all | solution.py:76
  93.8 0.8 shard_map.61
  (18 shorter events, 0.1 us)
Async XLA Ops:
  0.6 3.1 %copy-start = (bf16[8,16,16,128]{3,2,1,0:T(8,128)(2,1)S(1)}, bf16[8,16,16,128]{3,2,1,0:T(8,128)(2,1)}, u32[]{:S(2)}) copy-start(bf16[8,16,16,128]{3,2,1,0:T(8,128)(2,1)} %mid_ref.7) | copy-start | bytes 1572868
  0.6 0.9 copy-start.2
  1.6 4.4 %collective-permute-start.7 = (bf16[1,4,3584]{2,1,0:T(4,128)(2,1)S(1)}, bf16[1,4,3584]{2,1,0:T(4,128)(2,1)S(1)}, u32[]{:S(2)}, u32[]{:S(2)}) collective-permute-start(bf16[1,4,3584]{2,1,0:T(4,128)(2,1)S(1)} %shard_map.55.refs_0_), channel_id=1, source_target_pairs={{0,8},{1,9},{2,10},{3,11},{4,12},{5,13},{6,14},{7,15},{8,0},{9,1},... | collective-permute-start | bytes 86024 | tf_op jit(solution)/shard_map/ppermute | solution.py:62
  4.0 4.7 %collective-permute-start = (bf16[8,16,128]{2,1,0:T(8,128)(2,1)S(1)}, bf16[8,16,128]{2,1,0:T(8,128)(2,1)S(1)}, u32[]{:S(2)}, u32[]{:S(2)}) collective-permute-start(bf16[8,16,128]{2,1,0:T(8,128)(2,1)S(1)} %get-tuple-element.21), channel_id=1, source_target_pairs={{0,1},{2,3},{4,5},{6,7},{1,0},{3,2},{5,4},{7,6},{8,9},{10,11},{12,... | collective-permute-start | bytes 98312 | tf_op jit(solution)/shard_map/ppermute | solution.py:86
  5.3 3.4 %collective-permute-start.1 = (bf16[8,16,128]{2,1,0:T(8,128)(2,1)S(1)}, bf16[8,16,128]{2,1,0:T(8,128)(2,1)S(1)}, u32[]{:S(2)}, u32[]{:S(2)}) collective-permute-start(bf16[8,16,128]{2,1,0:T(8,128)(2,1)S(1)} %get-tuple-element.22), channel_id=1, source_target_pairs={{1,2},{3,4},{5,6},{2,1},{4,3},{6,5},{9,10},{11,12},{13,14},{10,9},... | collective-permute-start | bytes 98312 | tf_op jit(solution)/shard_map/ppermute | solution.py:86
  6.1 4.6 %collective-permute-start.8 = (bf16[2,4,3584]{2,1,0:T(4,128)(2,1)S(1)}, bf16[2,4,3584]{2,1,0:T(4,128)(2,1)S(1)}, u32[]{:S(2)}, u32[]{:S(2)}) collective-permute-start(bf16[2,4,3584]{2,1,0:T(4,128)(2,1)S(1)} %pad_maximum_fusion.2), channel_id=1, source_target_pairs={{0,16},{1,17},{2,18},{3,19},{4,20},{5,21},{6,22},{7,23},{8,24},{9,... | collective-permute-start | bytes 172040 | tf_op jit(solution)/shard_map/ppermute | solution.py:62
  8.8 12.7 %copy-start.1 = (bf16[8,16,16,128]{3,2,1,0:T(8,128)(2,1)S(1)}, bf16[8,16,16,128]{3,2,1,0:T(8,128)(2,1)}, u32[]{:S(2)}) copy-start(bf16[8,16,16,128]{3,2,1,0:T(8,128)(2,1)} %param.4) | copy-start | bytes 1572868
  8.8 3.7 %collective-permute-start.2 = (bf16[8,18,128]{2,1,0:T(8,128)(2,1)S(1)}, bf16[8,18,128]{2,1,0:T(8,128)(2,1)S(1)}, u32[]{:S(2)}, u32[]{:S(2)}) collective-permute-start(bf16[8,18,128]{2,1,0:T(8,128)(2,1)S(1)} %get-tuple-element.23), channel_id=1, source_target_pairs={{0,8},{16,24},{8,0},{24,16},{1,9},{17,25},{9,1},{25,17},{2,10},{18... | collective-permute-start | bytes 110600 | tf_op jit(solution)/shard_map/ppermute | solution.py:86
  8.9 3.6 %collective-permute-start.3 = (bf16[8,18,128]{2,1,0:T(8,128)(2,1)S(1)}, bf16[8,18,128]{2,1,0:T(8,128)(2,1)S(1)}, u32[]{:S(2)}, u32[]{:S(2)}) collective-permute-start(bf16[8,18,128]{2,1,0:T(8,128)(2,1)S(1)} %get-tuple-element.24), channel_id=1, source_target_pairs={{8,16},{16,8},{9,17},{17,9},{10,18},{18,10},{11,19},{19,11},{12,20... | collective-permute-start | bytes 110600 | tf_op jit(solution)/shard_map/ppermute | solution.py:86
  10.8 7.7 %collective-permute-start.9 = (bf16[4,4,3584]{2,1,0:T(4,128)(2,1)S(1)}, bf16[4,4,3584]{2,1,0:T(4,128)(2,1)S(1)}, u32[]{:S(2)}, u32[]{:S(2)}) collective-permute-start(bf16[4,4,3584]{2,1,0:T(4,128)(2,1)S(1)} %pad_maximum_fusion.1), channel_id=1, source_target_pairs={{0,64},{1,65},{2,66},{3,67},{4,68},{5,69},{6,70},{7,71},{8,72},{9,... | collective-permute-start | bytes 344072 | tf_op jit(solution)/shard_map/ppermute | solution.py:62
  12.6 8.9 %collective-permute-start.4 = (bf16[18,18,128]{2,1,0:T(8,128)(2,1)S(1)}, bf16[18,18,128]{2,1,0:T(8,128)(2,1)S(1)}, u32[]{:S(2)}, u32[]{:S(2)}) collective-permute-start(bf16[18,18,128]{2,1,0:T(8,128)(2,1)S(1)} %get-tuple-element.25), channel_id=1, source_target_pairs={{0,32},{64,96},{128,160},{192,224},{32,0},{96,64},{160,128},{224,1... | collective-permute-start | bytes 248840 | tf_op jit(solution)/shard_map/ppermute | solution.py:86
  15.4 6.1 %collective-permute-start.5 = (bf16[18,18,128]{2,1,0:T(8,128)(2,1)S(1)}, bf16[18,18,128]{2,1,0:T(8,128)(2,1)S(1)}, u32[]{:S(2)}, u32[]{:S(2)}) collective-permute-start(bf16[18,18,128]{2,1,0:T(8,128)(2,1)S(1)} %get-tuple-element.26), channel_id=1, source_target_pairs={{32,64},{96,128},{160,192},{64,32},{128,96},{192,160},{33,65},{97,... | collective-permute-start | bytes 248840 | tf_op jit(solution)/shard_map/ppermute | solution.py:86
  18.6 13.3 %collective-permute-start.10 = (bf16[8,4,3584]{2,1,0:T(4,128)(2,1)S(1)}, bf16[8,4,3584]{2,1,0:T(4,128)(2,1)S(1)}, u32[]{:S(2)}, u32[]{:S(2)}) collective-permute-start(bf16[8,4,3584]{2,1,0:T(4,128)(2,1)S(1)} %pad_maximum_fusion), channel_id=1, source_target_pairs={{0,128},{1,129},{2,130},{3,131},{4,132},{5,133},{6,134},{7,135},{8... | collective-permute-start | bytes 688136 | tf_op jit(solution)/shard_map/ppermute | solution.py:62
  24.7 8.6 %copy-start.4 = (bf16[10,18,16,384]{3,2,1,0:T(8,128)(2,1)}, bf16[10,18,16,384]{3,2,1,0:T(8,128)(2,1)S(1)}, u32[]{:S(2)}) copy-start(bf16[10,18,16,384]{3,2,1,0:T(8,128)(2,1)S(1)} %get-tuple-element.31.taps_ref) | copy-start | bytes 6635524
  24.7 8.6 %collective-permute-start.6 = (bf16[64,3456]{1,0:T(8,128)(2,1)S(1)}, bf16[64,3456]{1,0:T(8,128)(2,1)S(1)}, u32[]{:S(2)}, u32[]{:S(2)}) collective-permute-start(bf16[64,3456]{1,0:T(8,128)(2,1)S(1)} %get-tuple-element.28), channel_id=1, source_target_pairs={{0,32},{1,33},{2,34},{3,35},{4,36},{5,37},{6,38},{7,39},{8,40},{9,... | collective-permute-start | bytes 1327112 | tf_op jit(solution)/shard_map/ppermute | solution.py:62
  31.9 17.7 %collective-permute-start.11 = (bf16[16,4,3584]{2,1,0:T(4,128)(2,1)S(1)}, bf16[16,4,3584]{2,1,0:T(4,128)(2,1)S(1)}, u32[]{:S(2)}, u32[]{:S(2)}) collective-permute-start(bf16[16,4,3584]{2,1,0:T(4,128)(2,1)S(1)} %shard_map.56.near_ref), channel_id=1, source_target_pairs={{0,32},{1,33},{2,34},{3,35},{4,36},{5,37},{6,38},{7,39},{8,40},{9,... | collective-permute-start | bytes 1376264 | tf_op jit(solution)/shard_map/ppermute | solution.py:62
  34.2 24.9 %all-to-all-start = ((bf16[16,4,3456]{2,1,0:T(4,128)(2,1)}), bf16[16,4,3456]{2,1,0:T(4,128)(2,1)S(1)}, u32[]{:S(2)}, u32[]{:S(2)}) async-start(bf16[16,4,3456]{2,1,0:T(4,128)(2,1)} %shard_map.54), calls=%async_computation | async-start | bytes 884736 | tf_op jit(solution)/shard_map/all_to_all | solution.py:76
  50.7 0.6 copy-start.6
  51.3 14.6 %copy-start.5 = (bf16[10,18,16,384]{3,2,1,0:T(8,128)(2,1)S(1)}, bf16[10,18,16,384]{3,2,1,0:T(8,128)(2,1)}, u32[]{:S(2)}) copy-start(bf16[10,18,16,384]{3,2,1,0:T(8,128)(2,1)} %copy-done.4) | copy-start | bytes 6635524
  60.0 14.9 %all-to-all-start.1 = ((bf16[8,4,3456]{2,1,0:T(4,128)(2,1)}), bf16[8,4,3456]{2,1,0:T(4,128)(2,1)S(1)}, u32[]{:S(2)}, u32[]{:S(2)}) async-start(bf16[8,4,3456]{2,1,0:T(4,128)(2,1)} %shard_map.58), calls=%async_computation.1 | async-start | bytes 442368 | tf_op jit(solution)/shard_map/all_to_all | solution.py:76
  65.9 9.0 %copy-start.7 = (f32[4,3456]{1,0:T(4,128)S(1)}, f32[4,3456]{1,0:T(4,128)}, u32[]{:S(2)}) copy-start(f32[4,3456]{1,0:T(4,128)} %copy-done.6) | copy-start | bytes 165892
  70.5 23.3 %copy-start.3 = (f32[4,27,128]{2,0,1:T(4,128)S(1)}, f32[4,27,128]{2,0,1:T(4,128)}, u32[]{:S(2)}) copy-start(f32[4,27,128]{2,0,1:T(4,128)} %param.3) | copy-start | bytes 165892
  75.0 18.8 %collective-permute-start.12 = (f32[4,3456]{1,0:T(4,128)S(1)}, f32[4,3456]{1,0:T(4,128)S(1)}, u32[]{:S(2)}, u32[]{:S(2)}) collective-permute-start(f32[4,3456]{1,0:T(4,128)S(1)} %get-tuple-element.36.own_ref), channel_id=1, source_target_pairs={{0,1},{4,5},{8,9},{12,13},{16,17},{20,21},{24,25},{28,29},{32,33},... | collective-permute-start | bytes 165896 | tf_op jit(solution)/shard_map/ppermute | solution.py:69
  76.7 17.1 %collective-permute-start.13 = (f32[4,3456]{1,0:T(4,128)S(1)}, f32[4,3456]{1,0:T(4,128)S(1)}, u32[]{:S(2)}, u32[]{:S(2)}) collective-permute-start(f32[4,3456]{1,0:T(4,128)S(1)} %get-tuple-element.36.own_ref), channel_id=1, source_target_pairs={{0,2},{4,6},{8,10},{12,14},{16,18},{20,22},{24,26},{28,30},{32,34}... | collective-permute-start | bytes 165896 | tf_op jit(solution)/shard_map/ppermute | solution.py:69
  78.8 15.0 %collective-permute-start.14 = (f32[4,3456]{1,0:T(4,128)S(1)}, f32[4,3456]{1,0:T(4,128)S(1)}, u32[]{:S(2)}, u32[]{:S(2)}) collective-permute-start(f32[4,3456]{1,0:T(4,128)S(1)} %get-tuple-element.36.own_ref), channel_id=1, source_target_pairs={{0,3},{4,7},{8,11},{12,15},{16,19},{20,23},{24,27},{28,31},{32,35}... | collective-permute-start | bytes 165896 | tf_op jit(solution)/shard_map/ppermute | solution.py:69

commit v4 on v2

--- a/solution.py
+++ b/solution.py
@@ -117,6 +117,13 @@
         mid = mid_ref[k].astype(jnp.float32)
         zl_ref[k] = mid[:, 0].astype(jnp.bfloat16)
         zh_ref[k] = mid[:, nz - 1].astype(jnp.bfloat16)
+
+
+def join_kernel(*refs):
+    place = 0
+    for piece in refs[:-1]:
+        refs[-1][place : place + piece.shape[0]] = piece[...]
+        place += piece.shape[0]
 
 
 def picked(odd, first, second):
@@ -295,22 +302,23 @@
     bf16, f32 = jnp.bfloat16, jnp.float32
     raw = jnp.transpose(raw_weight, (1, 0, 2))
 
-    def joined(held, got):
-        return jnp.concatenate([held, got], 0)
+    def joined(held):
+        return jnp.concatenate(held, 0)
 
     def both(shape):
         return (of(shape, bf16), of(shape, bf16))
 
     faces = call(faces_kernel, both((1, ny, nz, ch)), (cotangent,))
     x_halo = swapped(*faces, "gx")
-    held, *width_faces = call(base_kernel, (of((1, rows, width + ch), bf16), *both((nx, ny, ch))), (raw, cotangent))
-    held = joined(held, where.send(held, lambda s: dict(y=s["y"] ^ 1)))
+    block, *width_faces = call(base_kernel, (of((1, rows, width + ch), bf16), *both((nx, ny, ch))), (raw, cotangent))
+    held = [block, where.send(block, lambda s: dict(y=s["y"] ^ 1))]
     faces = call(height_kernel, both((nx + 2, nz, ch)), (cotangent, *x_halo))
     y_halo = swapped(*faces, "gy")
-    held = joined(held, where.send(held, lambda s: dict(y=s["y"] ^ 2)))
+    held.append(where.send(joined(held), lambda s: dict(y=s["y"] ^ 2)))
     faces = call(width_kernel, both((nx + 2, ny + 2, ch)), (*width_faces, *x_halo, *y_halo))
     z_halo = swapped(*faces, "gz")
-    held = joined(held, where.send(held, lambda s: dict(zl=s["zl"] ^ 1)))
+    held.append(where.send(joined(held), lambda s: dict(zl=s["zl"] ^ 1)))
+    held.append(where.send(joined(held), lambda s: dict(zl=s["zl"] ^ 2)))
 
     flops = 2 * nx * ny * nz * ch * width
     tap_views, keep, send = call(
@@ -321,7 +329,7 @@
         flops=2 * flops,
     )
     other = where.send(send, lambda s: dict(core=1 - s["core"]))
-    held = joined(held, where.send(held, lambda s: dict(zl=s["zl"] ^ 2)))
+    held = call(join_kernel, of((16, rows, width + ch), bf16), held)
     peers = where.x * where.gy
     half = call(pair_kernel, of((peers, rows, width), bf16), (keep, other))
     parts = where.exchange(half, ("core", "zl", "zh"), lambda s: (s["x"], s["y"]))
@@ -332,11 +340,10 @@
         (held, far),
         flops=3_000_000_000,
     )
-    parts, inv_std = lax.optimization_barrier((parts, inv_std))
+    input_grad = call(input_kernel, of(inputs.shape, bf16), (tap_views, std_half), vmem=16, flops=2 * flops)
+    parts, input_grad = lax.optimization_barrier((parts, input_grad))
     copies = call(peers_kernel, of((where.zl * where.zh, rows, width), bf16), (parts,))
     parts = where.exchange(copies, ("core", "x", "y"), lambda s: (s["zh"], s["zl"]))
-    input_grad = call(input_kernel, of(inputs.shape, bf16), (tap_views, std_half), vmem=16, flops=2 * flops)
-    parts, input_grad = lax.optimization_barrier((parts, input_grad))
     everyone = CORES * where.x * where.gy
     block_grad, local = call(block_kernel, (of((rows, width), f32), of((everyone, 1, 3 * ch), f32)), (parts, block_std))
     filter_grad = where.send(block_grad, lambda s: dict(x=s["zl"], zl=s["x"]))

time: 103 us -> 89.4 us (0.87)
  waiting for transfers between devices: 26.2 us -> 10.6 us
  blocking collectives: 17.4 us -> 28.7 us
  starting transfers between devices: 41.9 us -> 34.7 us
  local copies, waits for them, and re-layouts: 4.26 us -> 2.38 us
    all_to_all x1 -> x2, blocking collectives: 17.4 us -> 28.7 us  [exchange(): lax.all_to_all(array, AXES, 0, 0, tiled=True, axis_index_groups=groups)]
    all_to_all x2 -> x1, starting transfers between devices: 21.2 us -> 13 us  [exchange(): lax.all_to_all(array, AXES, 0, 0, tiled=True, axis_index_groups=groups)]
    all_to_all x2 -> x1, waiting for transfers between devices: 11.1 us -> 3.19 us  [exchange(): lax.all_to_all(array, AXES, 0, 0, tiled=True, axis_index_groups=groups)]
    ppermute x7, waiting for transfers between devices: 14.2 us -> 7.38 us  [send(): return lax.ppermute(array, AXES, pairs)]
    ppermute x3, starting transfers between devices: 5.82 us -> 3.79 us  [swapped(): lax.ppermute(first, axis, pairs(0))]
    unnamed x16 -> x14, local copies, waits for them, and re-layouts: 4.17 us -> 2.38 us
    ppermute x7, starting transfers between devices: 11.6 us -> 13.3 us  [send(): return lax.ppermute(array, AXES, pairs)]
    ppermute x3, starting transfers between devices: 3.21 us -> 4.58 us  [swapped(): lax.ppermute(second, axis, pairs(1))]
  transfers between devices with their start and end apart: 15 -> 14, of which waited for: 6 -> 3; matrix products, arithmetic and copies ran while one was open for 0% -> 0% of each run, Pallas kernels for 10% -> 11%
where the time goes in v4:
time: 89.4 us; the launch traced here: 88.9 us
  starting transfers between devices  34.7 us (39%)
  blocking collectives  28.7 us (32%)
  Pallas kernels  11.4 us (13%)
  waiting for transfers between devices  10.6 us (12%)
  local copies, waits for them, and re-layouts  2.38 us (3%)
    all_to_all x2, blocking collectives, exchange(): lax.all_to_all(array, AXES, 0, 0, tiled=True, axis_index_groups=groups)  28.7 us
    ppermute x7, starting transfers between devices, send(): return lax.ppermute(array, AXES, pairs)  13.3 us
    all_to_all x1, starting transfers between devices, exchange(): lax.all_to_all(array, AXES, 0, 0, tiled=True, axis_index_groups=groups)  13 us
    pallas_call x12, Pallas kernels, call(): pl.pallas_call(kernel, out_shape=out_shape, in_specs=[pl.BlockSpec(memory...  11.4 us
    ppermute x7, waiting for transfers between devices, send(): return lax.ppermute(array, AXES, pairs)  7.38 us
    ppermute x3, starting transfers between devices, swapped(): lax.ppermute(second, axis, pairs(1))  4.58 us
    ppermute x3, starting transfers between devices, swapped(): lax.ppermute(first, axis, pairs(0))  3.79 us
    all_to_all x1, waiting for transfers between devices, exchange(): lax.all_to_all(array, AXES, 0, 0, tiled=True, axis_index_groups=groups)  3.19 us
  transfers between devices with their start and end apart: 14, of which 3 were waited for; matrix products, arithmetic and copies ran while one was open for 0% of the time, Pallas kernels for 11%

profile of v4, /device:TPU:1, one launch (start us, length us, event | category | flops | bytes accessed | tf_op | source)
XLA Modules:
  0.0 88.9 jit_solution(5376828700436465636)
XLA Ops:
  0.6 0.0 copy-start
  0.6 1.0 %copy-done = bf16[8,16,16,128]{3,2,1,0:T(8,128)(2,1)S(1)} copy-done((bf16[8,16,16,128]{3,2,1,0:T(8,128)(2,1)S(1)}, bf16[8,16,16,128]{3,2,1,0:T(8,128)(2,1)}, u32[]{:S(2)}) %copy-start) | copy-done | bytes 524312
  1.7 0.8 copy-done.3
  2.5 0.1 shard_map.52
  2.6 0.0 copy-start.1
  2.6 2.2 %collective-permute-start.7 = (bf16[1,4,3584]{2,1,0:T(4,128)(2,1)S(1)}, bf16[1,4,3584]{2,1,0:T(4,128)(2,1)S(1)}, u32[]{:S(2)}, u32[]{:S(2)}) collective-permute-start(bf16[1,4,3584]{2,1,0:T(4,128)(2,1)S(1)} %get-tuple-element.33.refs_0_), channel_id=1, source_target_pairs={{0,8},{1,9},{2,10},{3,11},{4,12},{5,13},{6,14},{7,15},{8,0},{9,1},... | collective-permute-start | bytes 86024 | tf_op jit(solution)/shard_map/ppermute | solution.py:62
  4.8 1.2 %collective-permute-start = (bf16[1,16,16,128]{3,2,1,0:T(8,128)(2,1)S(1)}, bf16[1,16,16,128]{3,2,1,0:T(8,128)(2,1)S(1)}, u32[]{:S(2)}, u32[]{:S(2)}) collective-permute-start(bf16[1,16,16,128]{3,2,1,0:T(8,128)(2,1)S(1)} %get-tuple-element.22), channel_id=1, source_target_pairs={{0,32},{64,96},{128,160},{192,224},{32,0},{96,64},{160,128},{224,1... | collective-permute-start | bytes 196616 | tf_op jit(solution)/shard_map/ppermute | solution.py:79
  6.1 3.3 %collective-permute-start.1 = (bf16[1,16,16,128]{3,2,1,0:T(8,128)(2,1)S(1)}, bf16[1,16,16,128]{3,2,1,0:T(8,128)(2,1)S(1)}, u32[]{:S(2)}, u32[]{:S(2)}) collective-permute-start(bf16[1,16,16,128]{3,2,1,0:T(8,128)(2,1)S(1)} %get-tuple-element.23), channel_id=1, source_target_pairs={{32,64},{96,128},{160,192},{64,32},{128,96},{192,160},{33,65},{97,... | collective-permute-start | bytes 196616 | tf_op jit(solution)/shard_map/ppermute | solution.py:79
  9.3 0.0 collective-permute-done.7.refs_1_
  9.4 2.7 %collective-permute-start.8 = (bf16[2,4,3584]{2,1,0:T(4,128)(2,1)S(1)}, bf16[2,4,3584]{2,1,0:T(4,128)(2,1)S(1)}, u32[]{:S(2)}, u32[]{:S(2)}) collective-permute-start(bf16[2,4,3584]{2,1,0:T(4,128)(2,1)S(1)} %pad_maximum_fusion.2), channel_id=1, source_target_pairs={{0,16},{1,17},{2,18},{3,19},{4,20},{5,21},{6,22},{7,23},{8,24},{9,... | collective-permute-start | bytes 172040 | tf_op jit(solution)/shard_map/ppermute | solution.py:62
  12.1 0.0 collective-permute-done.xa_ref
  12.1 0.0 collective-permute-done.1.xb_ref
  12.2 0.0 copy-start.2
  12.2 1.3 %collective-permute-start.2 = (bf16[10,16,128]{2,1,0:T(8,128)(2,1)S(1)}, bf16[10,16,128]{2,1,0:T(8,128)(2,1)S(1)}, u32[]{:S(2)}, u32[]{:S(2)}) collective-permute-start(bf16[10,16,128]{2,1,0:T(8,128)(2,1)S(1)} %get-tuple-element.24), channel_id=1, source_target_pairs={{0,8},{16,24},{8,0},{24,16},{1,9},{17,25},{9,1},{25,17},{2,10},{18... | collective-permute-start | bytes 122888 | tf_op jit(solution)/shard_map/ppermute | solution.py:79
  13.5 0.7 collective-permute-start.3
  14.1 0.0 collective-permute-done.8.refs_2_
  14.1 0.1 pad_maximum_fusion.1
  14.2 1.6 %collective-permute-start.9 = (bf16[4,4,3584]{2,1,0:T(4,128)(2,1)S(1)}, bf16[4,4,3584]{2,1,0:T(4,128)(2,1)S(1)}, u32[]{:S(2)}, u32[]{:S(2)}) collective-permute-start(bf16[4,4,3584]{2,1,0:T(4,128)(2,1)S(1)} %pad_maximum_fusion.1), channel_id=1, source_target_pairs={{0,64},{1,65},{2,66},{3,67},{4,68},{5,69},{6,70},{7,71},{8,72},{9,... | collective-permute-start | bytes 344072 | tf_op jit(solution)/shard_map/ppermute | solution.py:62
  15.8 0.0 collective-permute-done.2.ya_ref
  15.8 0.0 collective-permute-done.3.yb_ref
  15.8 0.1 shard_map.53
  16.0 1.3 %collective-permute-start.4 = (bf16[10,18,128]{2,1,0:T(8,128)(2,1)S(1)}, bf16[10,18,128]{2,1,0:T(8,128)(2,1)S(1)}, u32[]{:S(2)}, u32[]{:S(2)}) collective-permute-start(bf16[10,18,128]{2,1,0:T(8,128)(2,1)S(1)} %get-tuple-element.28), channel_id=1, source_target_pairs={{0,1},{2,3},{4,5},{6,7},{1,0},{3,2},{5,4},{7,6},{8,9},{10,11},{12,... | collective-permute-start | bytes 138248 | tf_op jit(solution)/shard_map/ppermute | solution.py:79
  17.3 0.7 collective-permute-start.5
  17.9 0.4 collective-permute-done.9.refs_3_
  18.3 0.2 pad_maximum_fusion
  18.5 3.7 %collective-permute-start.10 = (bf16[8,4,3584]{2,1,0:T(4,128)(2,1)S(1)}, bf16[8,4,3584]{2,1,0:T(4,128)(2,1)S(1)}, u32[]{:S(2)}, u32[]{:S(2)}) collective-permute-start(bf16[8,4,3584]{2,1,0:T(4,128)(2,1)S(1)} %pad_maximum_fusion), channel_id=1, source_target_pairs={{0,128},{1,129},{2,130},{3,131},{4,132},{5,133},{6,134},{7,135},{8... | collective-permute-start | bytes 688136 | tf_op jit(solution)/shard_map/ppermute | solution.py:62
  22.2 0.0 collective-permute-done.4.za_ref
  22.2 0.0 collective-permute-done.5.zb_ref
  22.2 3.4 %shard_map.54 = (bf16[10,18,16,384]{3,2,1,0:T(8,128)(2,1)S(1)}, f32[64,3456]{1,0:T(8,128)S(1)}, bf16[64,3456]{1,0:T(8,128)(2,1)S(1)}) custom-call(bf16[8,16,16,128]{3,2,1,0:T(8,128)(2,1)S(1)} %copy-done.1, bf16[1,16,16,128]{3,2,1,0:T(8,128)(2,1)S(1)} %collective-permute-done.xa_ref, bf16[1,16,16,128]{3,2,1,0:T(8,128)(2,1)S(1)} %collective-permute-done.1.xb_ref, ...), custom_call_target="tpu_custom_call" | custom-call | flops 3623878656 | bytes 1000000 | tf_op jit(solution)/shard_map/pallas_call | solution.py:22
  25.6 1.2 %collective-permute-start.6 = (bf16[64,3456]{1,0:T(8,128)(2,1)S(1)}, bf16[64,3456]{1,0:T(8,128)(2,1)S(1)}, u32[]{:S(2)}, u32[]{:S(2)}) collective-permute-start(bf16[64,3456]{1,0:T(8,128)(2,1)S(1)} %get-tuple-element.31), channel_id=1, source_target_pairs={{0,32},{1,33},{2,34},{3,35},{4,36},{5,37},{6,38},{7,39},{8,40},{9,... | collective-permute-start | bytes 1327112 | tf_op jit(solution)/shard_map/ppermute | solution.py:62
  26.8 6.9 %collective-permute-done.10.refs_4_ = bf16[8,4,3584]{2,1,0:T(4,128)(2,1)S(1)} collective-permute-done((bf16[8,4,3584]{2,1,0:T(4,128)(2,1)S(1)}, bf16[8,4,3584]{2,1,0:T(4,128)(2,1)S(1)}, u32[]{:S(2)}, u32[]{:S(2)}) %collective-permute-start.10) | collective-permute-done | bytes 229408 | tf_op jit(solution)/shard_map/ppermute | solution.py:62
  33.8 1.3 %collective-permute-start.11 = (bf16[16,4,3584]{2,1,0:T(4,128)(2,1)S(1)}, bf16[16,4,3584]{2,1,0:T(4,128)(2,1)S(1)}, u32[]{:S(2)}, u32[]{:S(2)}) collective-permute-start(bf16[16,4,3584]{2,1,0:T(4,128)(2,1)S(1)} %shard_map.56.near_ref), channel_id=1, source_target_pairs={{0,32},{1,33},{2,34},{3,35},{4,36},{5,37},{6,38},{7,39},{8,40},{9,... | collective-permute-start | bytes 1376264 | tf_op jit(solution)/shard_map/ppermute | solution.py:62
  35.1 0.0 collective-permute-done.6.other_ref
  35.1 0.9 %shard_map.55 = bf16[16,4,3456]{2,1,0:T(4,128)(2,1)} custom-call(f32[64,3456]{1,0:T(8,128)S(1)} %get-tuple-element.30.keep_ref, bf16[64,3456]{1,0:T(8,128)(2,1)S(1)} %collective-permute-done.6.other_ref), custom_call_target="tpu_custom_call" | custom-call | flops 1000000000 | bytes 1000000 | tf_op jit(solution)/shard_map/pallas_call | solution.py:22
  36.0 13.0 %all-to-all-start = ((bf16[16,4,3456]{2,1,0:T(4,128)(2,1)}), bf16[16,4,3456]{2,1,0:T(4,128)(2,1)S(1)}, u32[]{:S(2)}, u32[]{:S(2)}) async-start(bf16[16,4,3456]{2,1,0:T(4,128)(2,1)} %shard_map.55), calls=%async_computation | async-start | bytes 884736 | tf_op jit(solution)/shard_map/all_to_all | solution.py:69
  49.0 0.0 collective-permute-done.11.far_ref
  49.0 1.1 %shard_map.57 = (bf16[128,3456]{1,0:T(8,128)(2,1)S(1)}, f32[1,128]{1,0:T(1,128)S(1)}, f32[1,128]{1,0:T(1,128)S(1)}, f32[4,3456]{1,0:T(4,128)S(1)}) custom-call(bf16[16,4,3584]{2,1,0:T(4,128)(2,1)S(1)} %shard_map.56.near_ref, bf16[16,4,3584]{2,1,0:T(4,128)(2,1)S(1)} %collective-permute-done.11.far_ref), custom_call_target="tpu_custom_call" | custom-call | flops 3000000000 | bytes 1000000 | tf_op jit(solution)/shard_map/pallas_call | solution.py:22
  50.1 0.5 copy-done.6
  50.6 4.6 %shard_map.58 = bf16[8,16,16,128]{3,2,1,0:T(8,128)(2,1)} custom-call(bf16[10,18,16,384]{3,2,1,0:T(8,128)(2,1)S(1)} %copy-done.6, bf16[128,3456]{1,0:T(8,128)(2,1)S(1)} %get-tuple-element.34.std_ref), custom_call_target="tpu_custom_call" | custom-call | flops 3623878656 | bytes 1000000 | tf_op jit(solution)/shard_map/pallas_call | solution.py:22
  55.2 3.2 %all-to-all-done.parts_ref = bf16[16,4,3456]{2,1,0:T(4,128)(2,1)S(1)} async-done(((bf16[16,4,3456]{2,1,0:T(4,128)(2,1)}), bf16[16,4,3456]{2,1,0:T(4,128)(2,1)S(1)}, u32[]{:S(2)}, u32[]{:S(2)}) %all-to-all-start) | async-done | bytes 442400 | tf_op jit(solution)/shard_map/all_to_all | solution.py:69
  58.4 0.2 shard_map.59
  58.6 0.0 copy-start.4
  58.6 11.3 %all_to_all.15.parts_ref = bf16[8,4,3456]{2,1,0:T(4,128)(2,1)S(1)} all-to-all(bf16[8,4,3456]{2,1,0:T(4,128)(2,1)S(1)} %shard_map.59), channel_id=1, replica_groups={{0,64,128,192,4,68,132,196},{1,65,129,193,5,69,133,197},{2,66,130,194,6..., dimensions={0} | all-to-all | bytes 442368 | tf_op jit(solution)/shard_map/all_to_all | solution.py:69
  69.9 0.1 shard_map.60
  70.0 0.7 collective-permute-start.12
  70.7 17.4 %all_to_all.16.sums_ref = f32[32,1,384]{2,1,0:T(1,128)S(1)} all-to-all(f32[32,1,384]{2,1,0:T(1,128)S(1)} %get-tuple-element.41), channel_id=1, replica_groups={{0,8,16,24,1,9,17,25,2,10,18,26,3,11,19,27,32,40,48,56,33,41,49,57,34,4..., dimensions={0} | all-to-all | bytes 98304 | tf_op jit(solution)/shard_map/all_to_all | solution.py:69
  88.1 0.0 collective-permute-done.12.grad_ref
  88.1 0.8 shard_map.61
  (11 shorter events, 0.1 us)
Async XLA Ops:
  0.6 1.0 %copy-start = (bf16[8,16,16,128]{3,2,1,0:T(8,128)(2,1)S(1)}, bf16[8,16,16,128]{3,2,1,0:T(8,128)(2,1)}, u32[]{:S(2)}) copy-start(bf16[8,16,16,128]{3,2,1,0:T(8,128)(2,1)} %mid_ref.7) | copy-start | bytes 1572868
  1.7 0.8 copy-start.3
  2.6 9.5 %copy-start.1 = (bf16[8,16,16,128]{3,2,1,0:T(8,128)(2,1)S(1)}, bf16[8,16,16,128]{3,2,1,0:T(8,128)(2,1)}, u32[]{:S(2)}) copy-start(bf16[8,16,16,128]{3,2,1,0:T(8,128)(2,1)} %mid_ref.7) | copy-start | bytes 1572868
  2.6 6.7 %collective-permute-start.7 = (bf16[1,4,3584]{2,1,0:T(4,128)(2,1)S(1)}, bf16[1,4,3584]{2,1,0:T(4,128)(2,1)S(1)}, u32[]{:S(2)}, u32[]{:S(2)}) collective-permute-start(bf16[1,4,3584]{2,1,0:T(4,128)(2,1)S(1)} %get-tuple-element.33.refs_0_), channel_id=1, source_target_pairs={{0,8},{1,9},{2,10},{3,11},{4,12},{5,13},{6,14},{7,15},{8,0},{9,1},... | collective-permute-start | bytes 86024 | tf_op jit(solution)/shard_map/ppermute | solution.py:62
  4.8 7.3 %collective-permute-start = (bf16[1,16,16,128]{3,2,1,0:T(8,128)(2,1)S(1)}, bf16[1,16,16,128]{3,2,1,0:T(8,128)(2,1)S(1)}, u32[]{:S(2)}, u32[]{:S(2)}) collective-permute-start(bf16[1,16,16,128]{3,2,1,0:T(8,128)(2,1)S(1)} %get-tuple-element.22), channel_id=1, source_target_pairs={{0,32},{64,96},{128,160},{192,224},{32,0},{96,64},{160,128},{224,1... | collective-permute-start | bytes 196616 | tf_op jit(solution)/shard_map/ppermute | solution.py:79
  6.1 6.1 %collective-permute-start.1 = (bf16[1,16,16,128]{3,2,1,0:T(8,128)(2,1)S(1)}, bf16[1,16,16,128]{3,2,1,0:T(8,128)(2,1)S(1)}, u32[]{:S(2)}, u32[]{:S(2)}) collective-permute-start(bf16[1,16,16,128]{3,2,1,0:T(8,128)(2,1)S(1)} %get-tuple-element.23), channel_id=1, source_target_pairs={{32,64},{96,128},{160,192},{64,32},{128,96},{192,160},{33,65},{97,... | collective-permute-start | bytes 196616 | tf_op jit(solution)/shard_map/ppermute | solution.py:79
  9.4 4.7 %collective-permute-start.8 = (bf16[2,4,3584]{2,1,0:T(4,128)(2,1)S(1)}, bf16[2,4,3584]{2,1,0:T(4,128)(2,1)S(1)}, u32[]{:S(2)}, u32[]{:S(2)}) collective-permute-start(bf16[2,4,3584]{2,1,0:T(4,128)(2,1)S(1)} %pad_maximum_fusion.2), channel_id=1, source_target_pairs={{0,16},{1,17},{2,18},{3,19},{4,20},{5,21},{6,22},{7,23},{8,24},{9,... | collective-permute-start | bytes 172040 | tf_op jit(solution)/shard_map/ppermute | solution.py:62
  12.2 10.0 %copy-start.2 = (bf16[8,16,16,128]{3,2,1,0:T(8,128)(2,1)S(1)}, bf16[8,16,16,128]{3,2,1,0:T(8,128)(2,1)}, u32[]{:S(2)}) copy-start(bf16[8,16,16,128]{3,2,1,0:T(8,128)(2,1)} %param.4) | copy-start | bytes 1572868
  12.2 3.7 %collective-permute-start.2 = (bf16[10,16,128]{2,1,0:T(8,128)(2,1)S(1)}, bf16[10,16,128]{2,1,0:T(8,128)(2,1)S(1)}, u32[]{:S(2)}, u32[]{:S(2)}) collective-permute-start(bf16[10,16,128]{2,1,0:T(8,128)(2,1)S(1)} %get-tuple-element.24), channel_id=1, source_target_pairs={{0,8},{16,24},{8,0},{24,16},{1,9},{17,25},{9,1},{25,17},{2,10},{18... | collective-permute-start | bytes 122888 | tf_op jit(solution)/shard_map/ppermute | solution.py:79
  13.5 2.4 %collective-permute-start.3 = (bf16[10,16,128]{2,1,0:T(8,128)(2,1)S(1)}, bf16[10,16,128]{2,1,0:T(8,128)(2,1)S(1)}, u32[]{:S(2)}, u32[]{:S(2)}) collective-permute-start(bf16[10,16,128]{2,1,0:T(8,128)(2,1)S(1)} %get-tuple-element.25), channel_id=1, source_target_pairs={{8,16},{16,8},{9,17},{17,9},{10,18},{18,10},{11,19},{19,11},{12,20... | collective-permute-start | bytes 122888 | tf_op jit(solution)/shard_map/ppermute | solution.py:79
  14.2 4.1 %collective-permute-start.9 = (bf16[4,4,3584]{2,1,0:T(4,128)(2,1)S(1)}, bf16[4,4,3584]{2,1,0:T(4,128)(2,1)S(1)}, u32[]{:S(2)}, u32[]{:S(2)}) collective-permute-start(bf16[4,4,3584]{2,1,0:T(4,128)(2,1)S(1)} %pad_maximum_fusion.1), channel_id=1, source_target_pairs={{0,64},{1,65},{2,66},{3,67},{4,68},{5,69},{6,70},{7,71},{8,72},{9,... | collective-permute-start | bytes 344072 | tf_op jit(solution)/shard_map/ppermute | solution.py:62
  16.0 6.2 %collective-permute-start.4 = (bf16[10,18,128]{2,1,0:T(8,128)(2,1)S(1)}, bf16[10,18,128]{2,1,0:T(8,128)(2,1)S(1)}, u32[]{:S(2)}, u32[]{:S(2)}) collective-permute-start(bf16[10,18,128]{2,1,0:T(8,128)(2,1)S(1)} %get-tuple-element.28), channel_id=1, source_target_pairs={{0,1},{2,3},{4,5},{6,7},{1,0},{3,2},{5,4},{7,6},{8,9},{10,11},{12,... | collective-permute-start | bytes 138248 | tf_op jit(solution)/shard_map/ppermute | solution.py:79
  17.3 4.9 %collective-permute-start.5 = (bf16[10,18,128]{2,1,0:T(8,128)(2,1)S(1)}, bf16[10,18,128]{2,1,0:T(8,128)(2,1)S(1)}, u32[]{:S(2)}, u32[]{:S(2)}) collective-permute-start(bf16[10,18,128]{2,1,0:T(8,128)(2,1)S(1)} %get-tuple-element.29), channel_id=1, source_target_pairs={{1,2},{3,4},{5,6},{2,1},{4,3},{6,5},{9,10},{11,12},{13,14},{10,9},... | collective-permute-start | bytes 138248 | tf_op jit(solution)/shard_map/ppermute | solution.py:79
  18.5 15.2 %collective-permute-start.10 = (bf16[8,4,3584]{2,1,0:T(4,128)(2,1)S(1)}, bf16[8,4,3584]{2,1,0:T(4,128)(2,1)S(1)}, u32[]{:S(2)}, u32[]{:S(2)}) collective-permute-start(bf16[8,4,3584]{2,1,0:T(4,128)(2,1)S(1)} %pad_maximum_fusion), channel_id=1, source_target_pairs={{0,128},{1,129},{2,130},{3,131},{4,132},{5,133},{6,134},{7,135},{8... | collective-permute-start | bytes 688136 | tf_op jit(solution)/shard_map/ppermute | solution.py:62
  25.6 9.5 %copy-start.5 = (bf16[10,18,16,384]{3,2,1,0:T(8,128)(2,1)}, bf16[10,18,16,384]{3,2,1,0:T(8,128)(2,1)S(1)}, u32[]{:S(2)}) copy-start(bf16[10,18,16,384]{3,2,1,0:T(8,128)(2,1)S(1)} %get-tuple-element.32.taps_ref) | copy-start | bytes 6635524
  25.6 9.5 %collective-permute-start.6 = (bf16[64,3456]{1,0:T(8,128)(2,1)S(1)}, bf16[64,3456]{1,0:T(8,128)(2,1)S(1)}, u32[]{:S(2)}, u32[]{:S(2)}) collective-permute-start(bf16[64,3456]{1,0:T(8,128)(2,1)S(1)} %get-tuple-element.31), channel_id=1, source_target_pairs={{0,32},{1,33},{2,34},{3,35},{4,36},{5,37},{6,38},{7,39},{8,40},{9,... | collective-permute-start | bytes 1327112 | tf_op jit(solution)/shard_map/ppermute | solution.py:62
  33.8 15.2 %collective-permute-start.11 = (bf16[16,4,3584]{2,1,0:T(4,128)(2,1)S(1)}, bf16[16,4,3584]{2,1,0:T(4,128)(2,1)S(1)}, u32[]{:S(2)}, u32[]{:S(2)}) collective-permute-start(bf16[16,4,3584]{2,1,0:T(4,128)(2,1)S(1)} %shard_map.56.near_ref), channel_id=1, source_target_pairs={{0,32},{1,33},{2,34},{3,35},{4,36},{5,37},{6,38},{7,39},{8,40},{9,... | collective-permute-start | bytes 1376264 | tf_op jit(solution)/shard_map/ppermute | solution.py:62
  36.0 22.4 %all-to-all-start = ((bf16[16,4,3456]{2,1,0:T(4,128)(2,1)}), bf16[16,4,3456]{2,1,0:T(4,128)(2,1)S(1)}, u32[]{:S(2)}, u32[]{:S(2)}) async-start(bf16[16,4,3456]{2,1,0:T(4,128)(2,1)} %shard_map.55), calls=%async_computation | async-start | bytes 884736 | tf_op jit(solution)/shard_map/all_to_all | solution.py:69
  49.0 1.6 %copy-start.6 = (bf16[10,18,16,384]{3,2,1,0:T(8,128)(2,1)S(1)}, bf16[10,18,16,384]{3,2,1,0:T(8,128)(2,1)}, u32[]{:S(2)}) copy-start(bf16[10,18,16,384]{3,2,1,0:T(8,128)(2,1)} %copy-done.5) | copy-start | bytes 6635524
  58.6 29.5 %copy-start.4 = (f32[4,27,128]{2,0,1:T(4,128)S(1)}, f32[4,27,128]{2,0,1:T(4,128)}, u32[]{:S(2)}) copy-start(f32[4,27,128]{2,0,1:T(4,128)} %param.3) | copy-start | bytes 165892
  70.0 18.1 %collective-permute-start.12 = (f32[4,3456]{1,0:T(4,128)S(1)}, f32[4,3456]{1,0:T(4,128)S(1)}, u32[]{:S(2)}, u32[]{:S(2)}) collective-permute-start(f32[4,3456]{1,0:T(4,128)S(1)} %get-tuple-element.38), channel_id=1, source_target_pairs={{0,0},{1,64},{2,128},{3,192},{4,4},{5,68},{6,132},{7,196},{8,8},{9... | collective-permute-start | bytes 165896 | tf_op jit(solution)/shard_map/ppermute | solution.py:62

commit v5 on v4

--- a/solution.py
+++ b/solution.py
@@ -17,7 +17,7 @@
 MIB = 1024 * 1024
 
 
-def call(kernel, out_shape, args, vmem=8, flops=1_000_000_000):
+def call(kernel, out_shape, args, vmem=8, flops=1_000_000_000, scratch=()):
     many = isinstance(out_shape, tuple)
     return pl.pallas_call(
         kernel,
@@ -26,6 +26,7 @@
         out_specs=tuple(pl.BlockSpec(memory_space=pltpu.VMEM) for _ in out_shape)
         if many
         else pl.BlockSpec(memory_space=pltpu.VMEM),
+        scratch_shapes=scratch,
         compiler_params=pltpu.CompilerParams(vmem_limit_bytes=vmem * MIB),
         cost_estimate=pl.CostEstimate(flops=flops, bytes_accessed=1_000_000, transcendentals=0),
     )(*args)
@@ -156,15 +157,18 @@
     second_ref[...] = jnp.where(odd, high, low).astype(jnp.bfloat16)
 
 
-def filter_kernel(mid_ref, xa_ref, xb_ref, ya_ref, yb_ref, za_ref, zb_ref, in_ref, taps_ref, keep_ref, send_ref):
-    nx, ny, nz, ch = mid_ref.shape
+def fill_taps(taps_ref, mid_ref, xa_ref, xb_ref, ya_ref, yb_ref, z_halo):
+    nx, ny, _, ch = mid_ref.shape
     x_odd, y_odd, z_odd = is_odd("gx"), is_odd("gy"), is_odd("gz")
 
     def fill(k, rows, j, n):
         mid = rows.astype(jnp.float32)
-        low, high = picked(z_odd, za_ref[k, j : j + n], zb_ref[k, j : j + n])
-        low = low.astype(jnp.float32)[:, None, :]
-        high = high.astype(jnp.float32)[:, None, :]
+        if z_halo:
+            low, high = picked(z_odd, z_halo[0][k, j : j + n], z_halo[1][k, j : j + n])
+            low = low.astype(jnp.float32)[:, None, :]
+            high = high.astype(jnp.float32)[:, None, :]
+        else:
+            low = high = jnp.zeros((n, 1, ch), jnp.float32)
         up = jnp.concatenate([mid[:, 1:], high], axis=1)
         down = jnp.concatenate([low, mid[:, :-1]], axis=1)
         taps_ref[k, j : j + n, :, 0:ch] = up.astype(jnp.bfloat16)
@@ -186,19 +190,51 @@
     fill(0, low, 1, ny)
     fill(nx + 1, high, 1, ny)
     lax.fori_loop(0, nx + 2, plane, 0)
+
+
+def filter_kernel(mid_ref, xa_ref, xb_ref, ya_ref, yb_ref, in_ref, total_ref, first_ref, last_ref, taps_ref):
+    nx, ny, nz, ch = mid_ref.shape
+    fill_taps(taps_ref, mid_ref, xa_ref, xb_ref, ya_ref, yb_ref, None)
     cells = nx * ny * nz
-    flat = in_ref[...].T
-    core = lax.axis_index("gx") % CORES
+    flat = in_ref[...].reshape(cells, ch).T
     for a in range(3):
         for b in range(3):
             view = taps_ref[2 - a : 2 - a + nx, 2 - b : 2 - b + ny].reshape(cells, 3 * ch)
-            res = jnp.dot(flat, view, preferred_element_type=jnp.float32)
             lanes = pl.ds((a * 3 + b) * 3 * ch, 3 * ch)
-            for g in range(ch // 32):
-                first = res[g * 32 : g * 32 + 16]
-                second = res[g * 32 + 16 : g * 32 + 32]
-                keep_ref[g * 16 : g * 16 + 16, lanes] = jnp.where(core == 0, first, second)
-                send_ref[g * 16 : g * 16 + 16, lanes] = jnp.where(core == 0, second, first).astype(jnp.bfloat16)
+            total_ref[:, lanes] = jnp.dot(flat, view, preferred_element_type=jnp.float32)
+    for out_ref, j in ((first_ref, 0), (last_ref, nz - 1)):
+        ends = [in_ref[k].astype(jnp.float32)[:, j] for k in range(nx)]
+        out_ref[...] = jnp.concatenate(ends, axis=0).T.astype(jnp.bfloat16)
+
+
+def finish_kernel(total_ref, first_ref, last_ref, za_ref, zb_ref, keep_ref, send_ref):
+    ch = total_ref.shape[0]
+    nx, ny = za_ref.shape[0] - 2, za_ref.shape[1] - 2
+    core = lax.axis_index("gx") % CORES
+    low, high = picked(is_odd("gz"), za_ref[...].astype(jnp.float32), zb_ref[...].astype(jnp.float32))
+
+    def shifted(face):
+        return jnp.concatenate([face[:, 2 - b : 2 - b + ny] for b in range(3)], axis=2).astype(jnp.bfloat16)
+
+    low, high = shifted(low), shifted(high)
+    for a in range(3):
+        rows = slice(2 - a, 2 - a + nx)
+        above = jnp.dot(last_ref[...], high[rows].reshape(nx * ny, 3 * ch), preferred_element_type=jnp.float32)
+        below = jnp.dot(first_ref[...], low[rows].reshape(nx * ny, 3 * ch), preferred_element_type=jnp.float32)
+        for b in range(3):
+            for c in range(3):
+                lanes = pl.ds(((a * 3 + b) * 3 + c) * ch, ch)
+                res = total_ref[:, lanes]
+                if c == 0:
+                    res = res + above[:, b * ch : (b + 1) * ch]
+                if c == 2:
+                    res = res + below[:, b * ch : (b + 1) * ch]
+                for g in range(ch // 32):
+                    first = res[g * 32 : g * 32 + 16]
+                    second = res[g * 32 + 16 : g * 32 + 32]
+                    keep_ref[g * 16 : g * 16 + 16, lanes] = jnp.where(core == 0, first, second)
+                    other = jnp.where(core == 0, second, first)
+                    send_ref[g * 16 : g * 16 + 16, lanes] = other.astype(jnp.bfloat16)
 
 
 def pair_kernel(keep_ref, other_ref, out_ref):
@@ -224,8 +260,9 @@
         sums_ref[k] = three
 
 
-def input_kernel(taps_ref, std_ref, out_ref):
+def input_kernel(mid_ref, xa_ref, xb_ref, ya_ref, yb_ref, za_ref, zb_ref, std_ref, out_ref, taps_ref):
     nx, ny, nz, ch = out_ref.shape
+    fill_taps(taps_ref, mid_ref, xa_ref, xb_ref, ya_ref, yb_ref, (za_ref, zb_ref))
     planes = 2
     std = std_ref[...]
     for x in range(0, nx, planes):
@@ -321,13 +358,16 @@
     held.append(where.send(joined(held), lambda s: dict(zl=s["zl"] ^ 2)))
 
     flops = 2 * nx * ny * nz * ch * width
-    tap_views, keep, send = call(
+    scratch = [pltpu.VMEM((nx + 2, ny + 2, nz, 3 * ch), bf16)]
+    total, *ends = call(
         filter_kernel,
-        (of((nx + 2, ny + 2, nz, 3 * ch), bf16), of((ch // 2, width), f32), of((ch // 2, width), bf16)),
-        (cotangent, *x_halo, *y_halo, *z_halo, inputs.reshape(-1, ch)),
+        (of((ch, width), f32), of((ch, nx * ny), bf16), of((ch, nx * ny), bf16)),
+        (cotangent, *x_halo, *y_halo, inputs),
         vmem=16,
         flops=2 * flops,
+        scratch=scratch,
     )
+    keep, send = call(finish_kernel, (of((ch // 2, width), f32), of((ch // 2, width), bf16)), (total, *ends, *z_halo))
     other = where.send(send, lambda s: dict(core=1 - s["core"]))
     held = call(join_kernel, of((16, rows, width + ch), bf16), held)
     peers = where.x * where.gy
@@ -340,10 +380,18 @@
         (held, far),
         flops=3_000_000_000,
     )
-    input_grad = call(input_kernel, of(inputs.shape, bf16), (tap_views, std_half), vmem=16, flops=2 * flops)
-    parts, input_grad = lax.optimization_barrier((parts, input_grad))
+    parts, inv_std = lax.optimization_barrier((parts, inv_std))
     copies = call(peers_kernel, of((where.zl * where.zh, rows, width), bf16), (parts,))
     parts = where.exchange(copies, ("core", "x", "y"), lambda s: (s["zh"], s["zl"]))
+    input_grad = call(
+        input_kernel,
+        of(inputs.shape, bf16),
+        (cotangent, *x_halo, *y_halo, *z_halo, std_half),
+        vmem=16,
+        flops=2 * flops,
+        scratch=scratch,
+    )
+    parts, input_grad = lax.optimization_barrier((parts, input_grad))
     everyone = CORES * where.x * where.gy
     block_grad, local = call(block_kernel, (of((rows, width), f32), of((everyone, 1, 3 * ch), f32)), (parts, block_std))
     filter_grad = where.send(block_grad, lambda s: dict(x=s["zl"], zl=s["x"]))

time: 89.4 us -> 90.6 us (1.013)
  blocking collectives: 28.7 us -> 17.1 us
  waiting for transfers between devices: 10.6 us -> 18.9 us
  starting transfers between devices: 34.7 us -> 38.2 us
  Pallas kernels: 11.4 us -> 12.8 us
    all_to_all x2 -> x1, blocking collectives: 28.7 us -> 17.1 us  [exchange(): lax.all_to_all(array, AXES, 0, 0, tiled=True, axis_index_groups=groups)]
    all_to_all x1 -> x2, waiting for transfers between devices: 3.19 us -> 11.6 us  [exchange(): lax.all_to_all(array, AXES, 0, 0, tiled=True, axis_index_groups=groups)]
    all_to_all x1 -> x2, starting transfers between devices: 13 us -> 16.5 us  [exchange(): lax.all_to_all(array, AXES, 0, 0, tiled=True, axis_index_groups=groups)]
    pallas_call x12 -> x13, Pallas kernels: 11.4 us -> 12.8 us  [call(): pl.pallas_call(kernel, out_shape=out_shape, in_specs=[pl.BlockSpec(memory...]
    unnamed x14 -> x10, local copies, waits for them, and re-layouts: 2.38 us -> 1.86 us
  transfers between devices with their start and end apart: 14 -> 15, of which waited for: 3 -> 4; matrix products, arithmetic and copies ran while one was open for 0% -> 0% of each run, Pallas kernels for 11% -> 12%
where the time goes in v5:
time: 90.6 us; the launch traced here: 90 us
  starting transfers between devices  38.2 us (42%)
  waiting for transfers between devices  18.9 us (21%)
  blocking collectives  17.1 us (19%)
  Pallas kernels  12.8 us (14%)
  local copies, waits for them, and re-layouts  1.86 us (2%)
    all_to_all x1, blocking collectives, exchange(): lax.all_to_all(array, AXES, 0, 0, tiled=True, axis_index_groups=groups)  17.1 us
    all_to_all x2, starting transfers between devices, exchange(): lax.all_to_all(array, AXES, 0, 0, tiled=True, axis_index_groups=groups)  16.5 us
    ppermute x7, starting transfers between devices, send(): return lax.ppermute(array, AXES, pairs)  13.3 us
    pallas_call x13, Pallas kernels, call(): pl.pallas_call(kernel, out_shape=out_shape, in_specs=[pl.BlockSpec(memory...  12.8 us
    all_to_all x2, waiting for transfers between devices, exchange(): lax.all_to_all(array, AXES, 0, 0, tiled=True, axis_index_groups=groups)  11.6 us
    ppermute x7, waiting for transfers between devices, send(): return lax.ppermute(array, AXES, pairs)  7.28 us
    ppermute x3, starting transfers between devices, swapped(): lax.ppermute(second, axis, pairs(1))  4.58 us
    ppermute x3, starting transfers between devices, swapped(): lax.ppermute(first, axis, pairs(0))  3.79 us
  transfers between devices with their start and end apart: 15, of which 4 were waited for; matrix products, arithmetic and copies ran while one was open for 0% of the time, Pallas kernels for 12%

profile of v5, /device:TPU:1, one launch (start us, length us, event | category | flops | bytes accessed | tf_op | source)
XLA Modules:
  0.0 90.0 jit_solution(13493647058583797614)
XLA Ops:
  0.6 0.0 copy-start.1
  0.6 1.0 %copy-done.1 = bf16[8,16,16,128]{3,2,1,0:T(8,128)(2,1)S(1)} copy-done((bf16[8,16,16,128]{3,2,1,0:T(8,128)(2,1)S(1)}, bf16[8,16,16,128]{3,2,1,0:T(8,128)(2,1)}, u32[]{:S(2)}) %copy-start.1) | copy-done | bytes 524312
  1.7 0.8 copy-done.3
  2.5 0.1 shard_map.53
  2.6 0.0 copy-start.2
  2.6 2.2 %collective-permute-start.7 = (bf16[1,4,3584]{2,1,0:T(4,128)(2,1)S(1)}, bf16[1,4,3584]{2,1,0:T(4,128)(2,1)S(1)}, u32[]{:S(2)}, u32[]{:S(2)}) collective-permute-start(bf16[1,4,3584]{2,1,0:T(4,128)(2,1)S(1)} %get-tuple-element.39.refs_0_), channel_id=1, source_target_pairs={{0,8},{1,9},{2,10},{3,11},{4,12},{5,13},{6,14},{7,15},{8,0},{9,1},... | collective-permute-start | bytes 86024 | tf_op jit(solution)/shard_map/ppermute | solution.py:63
  4.8 1.2 %collective-permute-start = (bf16[1,16,16,128]{3,2,1,0:T(8,128)(2,1)S(1)}, bf16[1,16,16,128]{3,2,1,0:T(8,128)(2,1)S(1)}, u32[]{:S(2)}, u32[]{:S(2)}) collective-permute-start(bf16[1,16,16,128]{3,2,1,0:T(8,128)(2,1)S(1)} %get-tuple-element.26), channel_id=1, source_target_pairs={{0,32},{64,96},{128,160},{192,224},{32,0},{96,64},{160,128},{224,1... | collective-permute-start | bytes 196616 | tf_op jit(solution)/shard_map/ppermute | solution.py:80
  6.1 3.3 %collective-permute-start.1 = (bf16[1,16,16,128]{3,2,1,0:T(8,128)(2,1)S(1)}, bf16[1,16,16,128]{3,2,1,0:T(8,128)(2,1)S(1)}, u32[]{:S(2)}, u32[]{:S(2)}) collective-permute-start(bf16[1,16,16,128]{3,2,1,0:T(8,128)(2,1)S(1)} %get-tuple-element.27), channel_id=1, source_target_pairs={{32,64},{96,128},{160,192},{64,32},{128,96},{192,160},{33,65},{97,... | collective-permute-start | bytes 196616 | tf_op jit(solution)/shard_map/ppermute | solution.py:80
  9.3 0.0 collective-permute-done.7.refs_1_
  9.4 2.7 %collective-permute-start.8 = (bf16[2,4,3584]{2,1,0:T(4,128)(2,1)S(1)}, bf16[2,4,3584]{2,1,0:T(4,128)(2,1)S(1)}, u32[]{:S(2)}, u32[]{:S(2)}) collective-permute-start(bf16[2,4,3584]{2,1,0:T(4,128)(2,1)S(1)} %pad_maximum_fusion.2), channel_id=1, source_target_pairs={{0,16},{1,17},{2,18},{3,19},{4,20},{5,21},{6,22},{7,23},{8,24},{9,... | collective-permute-start | bytes 172040 | tf_op jit(solution)/shard_map/ppermute | solution.py:63
  12.1 0.0 collective-permute-done.xa_ref
  12.1 0.0 collective-permute-done.1.xb_ref
  12.2 1.3 %collective-permute-start.2 = (bf16[10,16,128]{2,1,0:T(8,128)(2,1)S(1)}, bf16[10,16,128]{2,1,0:T(8,128)(2,1)S(1)}, u32[]{:S(2)}, u32[]{:S(2)}) collective-permute-start(bf16[10,16,128]{2,1,0:T(8,128)(2,1)S(1)} %get-tuple-element.28), channel_id=1, source_target_pairs={{0,8},{16,24},{8,0},{24,16},{1,9},{17,25},{9,1},{25,17},{2,10},{18... | collective-permute-start | bytes 122888 | tf_op jit(solution)/shard_map/ppermute | solution.py:80
  13.4 0.7 collective-permute-start.3
  14.1 0.0 collective-permute-done.8.refs_2_
  14.1 0.1 pad_maximum_fusion.1
  14.2 1.6 %collective-permute-start.9 = (bf16[4,4,3584]{2,1,0:T(4,128)(2,1)S(1)}, bf16[4,4,3584]{2,1,0:T(4,128)(2,1)S(1)}, u32[]{:S(2)}, u32[]{:S(2)}) collective-permute-start(bf16[4,4,3584]{2,1,0:T(4,128)(2,1)S(1)} %pad_maximum_fusion.1), channel_id=1, source_target_pairs={{0,64},{1,65},{2,66},{3,67},{4,68},{5,69},{6,70},{7,71},{8,72},{9,... | collective-permute-start | bytes 344072 | tf_op jit(solution)/shard_map/ppermute | solution.py:63
  15.8 0.0 collective-permute-done.2.ya_ref
  15.8 0.0 collective-permute-done.3.yb_ref
  15.8 0.1 shard_map.54
  16.0 1.3 %collective-permute-start.4 = (bf16[10,18,128]{2,1,0:T(8,128)(2,1)S(1)}, bf16[10,18,128]{2,1,0:T(8,128)(2,1)S(1)}, u32[]{:S(2)}, u32[]{:S(2)}) collective-permute-start(bf16[10,18,128]{2,1,0:T(8,128)(2,1)S(1)} %get-tuple-element.35), channel_id=1, source_target_pairs={{0,1},{2,3},{4,5},{6,7},{1,0},{3,2},{5,4},{7,6},{8,9},{10,11},{12,... | collective-permute-start | bytes 138248 | tf_op jit(solution)/shard_map/ppermute | solution.py:80
  17.3 0.7 collective-permute-start.5
  17.9 0.4 collective-permute-done.9.refs_3_
  18.3 0.2 pad_maximum_fusion
  18.5 3.7 %collective-permute-start.10 = (bf16[8,4,3584]{2,1,0:T(4,128)(2,1)S(1)}, bf16[8,4,3584]{2,1,0:T(4,128)(2,1)S(1)}, u32[]{:S(2)}, u32[]{:S(2)}) collective-permute-start(bf16[8,4,3584]{2,1,0:T(4,128)(2,1)S(1)} %pad_maximum_fusion), channel_id=1, source_target_pairs={{0,128},{1,129},{2,130},{3,131},{4,132},{5,133},{6,134},{7,135},{8... | collective-permute-start | bytes 688136 | tf_op jit(solution)/shard_map/ppermute | solution.py:63
  22.2 0.0 copy-done
  22.2 3.2 %shard_map.52 = (f32[128,3456]{1,0:T(8,128)S(1)}, bf16[128,128]{1,0:T(8,128)(2,1)S(1)}, bf16[128,128]{1,0:T(8,128)(2,1)S(1)}) custom-call(bf16[8,16,16,128]{3,2,1,0:T(8,128)(2,1)S(1)} %copy-done.2, bf16[1,16,16,128]{3,2,1,0:T(8,128)(2,1)S(1)} %collective-permute-done.xa_ref, bf16[1,16,16,128]{3,2,1,0:T(8,128)(2,1)S(1)} %collective-permute-done.1.xb_ref, ...), custom_call_target="tpu_custom_call" | custom-call | flops 3623878656 | bytes 1000000 | tf_op jit(solution)/shard_map/pallas_call | solution.py:22
  25.4 0.0 collective-permute-done.4.za_ref
  25.4 0.0 collective-permute-done.5.zb_ref
  25.4 0.3 shard_map.55
  25.7 1.2 %collective-permute-start.6 = (bf16[64,3456]{1,0:T(8,128)(2,1)S(1)}, bf16[64,3456]{1,0:T(8,128)(2,1)S(1)}, u32[]{:S(2)}, u32[]{:S(2)}) collective-permute-start(bf16[64,3456]{1,0:T(8,128)(2,1)S(1)} %get-tuple-element.38), channel_id=1, source_target_pairs={{0,32},{1,33},{2,34},{3,35},{4,36},{5,37},{6,38},{7,39},{8,40},{9,... | collective-permute-start | bytes 1327112 | tf_op jit(solution)/shard_map/ppermute | solution.py:63
  26.9 6.8 %collective-permute-done.10.refs_4_ = bf16[8,4,3584]{2,1,0:T(4,128)(2,1)S(1)} collective-permute-done((bf16[8,4,3584]{2,1,0:T(4,128)(2,1)S(1)}, bf16[8,4,3584]{2,1,0:T(4,128)(2,1)S(1)}, u32[]{:S(2)}, u32[]{:S(2)}) %collective-permute-start.10) | collective-permute-done | bytes 229408 | tf_op jit(solution)/shard_map/ppermute | solution.py:63
  33.8 1.3 %collective-permute-start.11 = (bf16[16,4,3584]{2,1,0:T(4,128)(2,1)S(1)}, bf16[16,4,3584]{2,1,0:T(4,128)(2,1)S(1)}, u32[]{:S(2)}, u32[]{:S(2)}) collective-permute-start(bf16[16,4,3584]{2,1,0:T(4,128)(2,1)S(1)} %shard_map.57.near_ref), channel_id=1, source_target_pairs={{0,32},{1,33},{2,34},{3,35},{4,36},{5,37},{6,38},{7,39},{8,40},{9,... | collective-permute-start | bytes 1376264 | tf_op jit(solution)/shard_map/ppermute | solution.py:63
  35.1 0.0 collective-permute-done.6.other_ref
  35.1 0.9 shard_map.56
  36.0 12.9 %all-to-all-start = ((bf16[16,4,3456]{2,1,0:T(4,128)(2,1)}), bf16[16,4,3456]{2,1,0:T(4,128)(2,1)S(1)}, u32[]{:S(2)}, u32[]{:S(2)}) async-start(bf16[16,4,3456]{2,1,0:T(4,128)(2,1)} %shard_map.56), calls=%async_computation | async-start | bytes 884736 | tf_op jit(solution)/shard_map/all_to_all | solution.py:70
  48.9 0.0 collective-permute-done.11.far_ref
  48.9 1.1 %shard_map.58 = (bf16[128,3456]{1,0:T(8,128)(2,1)S(1)}, f32[1,128]{1,0:T(1,128)S(1)}, f32[1,128]{1,0:T(1,128)S(1)}, f32[4,3456]{1,0:T(4,128)S(1)}) custom-call(bf16[16,4,3584]{2,1,0:T(4,128)(2,1)S(1)} %shard_map.57.near_ref, bf16[16,4,3584]{2,1,0:T(4,128)(2,1)S(1)} %collective-permute-done.11.far_ref), custom_call_target="tpu_custom_call" | custom-call | flops 3000000000 | bytes 1000000 | tf_op jit(solution)/shard_map/pallas_call | solution.py:22
  50.0 8.3 %all-to-all-done.parts_ref = bf16[16,4,3456]{2,1,0:T(4,128)(2,1)S(1)} async-done(((bf16[16,4,3456]{2,1,0:T(4,128)(2,1)}), bf16[16,4,3456]{2,1,0:T(4,128)(2,1)S(1)}, u32[]{:S(2)}, u32[]{:S(2)}) %all-to-all-start) | async-done | bytes 442400 | tf_op jit(solution)/shard_map/all_to_all | solution.py:70
  58.3 0.9 shard_map.59
  59.2 3.6 %all-to-all-start.1 = ((bf16[8,4,3456]{2,1,0:T(4,128)(2,1)}), bf16[8,4,3456]{2,1,0:T(4,128)(2,1)S(1)}, u32[]{:S(2)}, u32[]{:S(2)}) async-start(bf16[8,4,3456]{2,1,0:T(4,128)(2,1)} %shard_map.59), calls=%async_computation.1 | async-start | bytes 442368 | tf_op jit(solution)/shard_map/all_to_all | solution.py:70
  62.8 5.3 %shard_map.60 = bf16[8,16,16,128]{3,2,1,0:T(8,128)(2,1)} custom-call(bf16[8,16,16,128]{3,2,1,0:T(8,128)(2,1)S(1)} %copy-done.2, bf16[1,16,16,128]{3,2,1,0:T(8,128)(2,1)S(1)} %collective-permute-done.xa_ref, bf16[1,16,16,128]{3,2,1,0:T(8,128)(2,1)S(1)} %collective-permute-done.1.xb_ref, bf16[10,16,128]{2,1,0:T(8,128)(2,1)S(1)} %collective-permute-done.2.ya_ref, ...), custom_call_target="tpu_custom_call" | custom-call | flops 3623878656 | bytes 1000000 | tf_op jit(solution)/shard_map/pallas_call | solution.py:22
  68.1 3.2 %all-to-all-done.1.parts_ref = bf16[8,4,3456]{2,1,0:T(4,128)(2,1)S(1)} async-done(((bf16[8,4,3456]{2,1,0:T(4,128)(2,1)}), bf16[8,4,3456]{2,1,0:T(4,128)(2,1)S(1)}, u32[]{:S(2)}, u32[]{:S(2)}) %all-to-all-start.1) | async-done | bytes 221216 | tf_op jit(solution)/shard_map/all_to_all | solution.py:70
  71.3 0.1 shard_map.61
  71.4 0.7 collective-permute-start.12
  72.1 17.1 %all_to_all.15.sums_ref = f32[32,1,384]{2,1,0:T(1,128)S(1)} all-to-all(f32[32,1,384]{2,1,0:T(1,128)S(1)} %get-tuple-element.49), channel_id=1, replica_groups={{0,8,16,24,1,9,17,25,2,10,18,26,3,11,19,27,32,40,48,56,33,41,49,57,34,4..., dimensions={0} | all-to-all | bytes 98304 | tf_op jit(solution)/shard_map/all_to_all | solution.py:70
  89.3 0.0 collective-permute-done.12.grad_ref
  89.3 0.8 shard_map.62
  (9 shorter events, 0.1 us)
Async XLA Ops:
  0.6 1.0 %copy-start.1 = (bf16[8,16,16,128]{3,2,1,0:T(8,128)(2,1)S(1)}, bf16[8,16,16,128]{3,2,1,0:T(8,128)(2,1)}, u32[]{:S(2)}) copy-start(bf16[8,16,16,128]{3,2,1,0:T(8,128)(2,1)} %mid_ref.9) | copy-start | bytes 1572868
  1.7 0.8 copy-start.3
  2.6 9.5 %copy-start.2 = (bf16[8,16,16,128]{3,2,1,0:T(8,128)(2,1)S(1)}, bf16[8,16,16,128]{3,2,1,0:T(8,128)(2,1)}, u32[]{:S(2)}) copy-start(bf16[8,16,16,128]{3,2,1,0:T(8,128)(2,1)} %mid_ref.9) | copy-start | bytes 1572868
  2.6 6.7 %collective-permute-start.7 = (bf16[1,4,3584]{2,1,0:T(4,128)(2,1)S(1)}, bf16[1,4,3584]{2,1,0:T(4,128)(2,1)S(1)}, u32[]{:S(2)}, u32[]{:S(2)}) collective-permute-start(bf16[1,4,3584]{2,1,0:T(4,128)(2,1)S(1)} %get-tuple-element.39.refs_0_), channel_id=1, source_target_pairs={{0,8},{1,9},{2,10},{3,11},{4,12},{5,13},{6,14},{7,15},{8,0},{9,1},... | collective-permute-start | bytes 86024 | tf_op jit(solution)/shard_map/ppermute | solution.py:63
  4.8 7.3 %collective-permute-start = (bf16[1,16,16,128]{3,2,1,0:T(8,128)(2,1)S(1)}, bf16[1,16,16,128]{3,2,1,0:T(8,128)(2,1)S(1)}, u32[]{:S(2)}, u32[]{:S(2)}) collective-permute-start(bf16[1,16,16,128]{3,2,1,0:T(8,128)(2,1)S(1)} %get-tuple-element.26), channel_id=1, source_target_pairs={{0,32},{64,96},{128,160},{192,224},{32,0},{96,64},{160,128},{224,1... | collective-permute-start | bytes 196616 | tf_op jit(solution)/shard_map/ppermute | solution.py:80
  6.1 6.1 %collective-permute-start.1 = (bf16[1,16,16,128]{3,2,1,0:T(8,128)(2,1)S(1)}, bf16[1,16,16,128]{3,2,1,0:T(8,128)(2,1)S(1)}, u32[]{:S(2)}, u32[]{:S(2)}) collective-permute-start(bf16[1,16,16,128]{3,2,1,0:T(8,128)(2,1)S(1)} %get-tuple-element.27), channel_id=1, source_target_pairs={{32,64},{96,128},{160,192},{64,32},{128,96},{192,160},{33,65},{97,... | collective-permute-start | bytes 196616 | tf_op jit(solution)/shard_map/ppermute | solution.py:80
  9.4 4.7 %collective-permute-start.8 = (bf16[2,4,3584]{2,1,0:T(4,128)(2,1)S(1)}, bf16[2,4,3584]{2,1,0:T(4,128)(2,1)S(1)}, u32[]{:S(2)}, u32[]{:S(2)}) collective-permute-start(bf16[2,4,3584]{2,1,0:T(4,128)(2,1)S(1)} %pad_maximum_fusion.2), channel_id=1, source_target_pairs={{0,16},{1,17},{2,18},{3,19},{4,20},{5,21},{6,22},{7,23},{8,24},{9,... | collective-permute-start | bytes 172040 | tf_op jit(solution)/shard_map/ppermute | solution.py:63
  12.2 3.7 %collective-permute-start.2 = (bf16[10,16,128]{2,1,0:T(8,128)(2,1)S(1)}, bf16[10,16,128]{2,1,0:T(8,128)(2,1)S(1)}, u32[]{:S(2)}, u32[]{:S(2)}) collective-permute-start(bf16[10,16,128]{2,1,0:T(8,128)(2,1)S(1)} %get-tuple-element.28), channel_id=1, source_target_pairs={{0,8},{16,24},{8,0},{24,16},{1,9},{17,25},{9,1},{25,17},{2,10},{18... | collective-permute-start | bytes 122888 | tf_op jit(solution)/shard_map/ppermute | solution.py:80
  13.4 2.4 %collective-permute-start.3 = (bf16[10,16,128]{2,1,0:T(8,128)(2,1)S(1)}, bf16[10,16,128]{2,1,0:T(8,128)(2,1)S(1)}, u32[]{:S(2)}, u32[]{:S(2)}) collective-permute-start(bf16[10,16,128]{2,1,0:T(8,128)(2,1)S(1)} %get-tuple-element.29), channel_id=1, source_target_pairs={{8,16},{16,8},{9,17},{17,9},{10,18},{18,10},{11,19},{19,11},{12,20... | collective-permute-start | bytes 122888 | tf_op jit(solution)/shard_map/ppermute | solution.py:80
  14.2 4.1 %collective-permute-start.9 = (bf16[4,4,3584]{2,1,0:T(4,128)(2,1)S(1)}, bf16[4,4,3584]{2,1,0:T(4,128)(2,1)S(1)}, u32[]{:S(2)}, u32[]{:S(2)}) collective-permute-start(bf16[4,4,3584]{2,1,0:T(4,128)(2,1)S(1)} %pad_maximum_fusion.1), channel_id=1, source_target_pairs={{0,64},{1,65},{2,66},{3,67},{4,68},{5,69},{6,70},{7,71},{8,72},{9,... | collective-permute-start | bytes 344072 | tf_op jit(solution)/shard_map/ppermute | solution.py:63
  15.8 6.3 %copy-start = (bf16[8,16,16,128]{3,2,1,0:T(8,128)(2,1)S(1)}, bf16[8,16,16,128]{3,2,1,0:T(8,128)(2,1)}, u32[]{:S(2)}) copy-start(bf16[8,16,16,128]{3,2,1,0:T(8,128)(2,1)} %in_ref.1) | copy-start | bytes 1572868
  16.0 9.4 %collective-permute-start.4 = (bf16[10,18,128]{2,1,0:T(8,128)(2,1)S(1)}, bf16[10,18,128]{2,1,0:T(8,128)(2,1)S(1)}, u32[]{:S(2)}, u32[]{:S(2)}) collective-permute-start(bf16[10,18,128]{2,1,0:T(8,128)(2,1)S(1)} %get-tuple-element.35), channel_id=1, source_target_pairs={{0,1},{2,3},{4,5},{6,7},{1,0},{3,2},{5,4},{7,6},{8,9},{10,11},{12,... | collective-permute-start | bytes 138248 | tf_op jit(solution)/shard_map/ppermute | solution.py:80
  17.3 8.1 %collective-permute-start.5 = (bf16[10,18,128]{2,1,0:T(8,128)(2,1)S(1)}, bf16[10,18,128]{2,1,0:T(8,128)(2,1)S(1)}, u32[]{:S(2)}, u32[]{:S(2)}) collective-permute-start(bf16[10,18,128]{2,1,0:T(8,128)(2,1)S(1)} %get-tuple-element.36), channel_id=1, source_target_pairs={{1,2},{3,4},{5,6},{2,1},{4,3},{6,5},{9,10},{11,12},{13,14},{10,9},... | collective-permute-start | bytes 138248 | tf_op jit(solution)/shard_map/ppermute | solution.py:80
  18.5 15.3 %collective-permute-start.10 = (bf16[8,4,3584]{2,1,0:T(4,128)(2,1)S(1)}, bf16[8,4,3584]{2,1,0:T(4,128)(2,1)S(1)}, u32[]{:S(2)}, u32[]{:S(2)}) collective-permute-start(bf16[8,4,3584]{2,1,0:T(4,128)(2,1)S(1)} %pad_maximum_fusion), channel_id=1, source_target_pairs={{0,128},{1,129},{2,130},{3,131},{4,132},{5,133},{6,134},{7,135},{8... | collective-permute-start | bytes 688136 | tf_op jit(solution)/shard_map/ppermute | solution.py:63
  25.7 9.4 %collective-permute-start.6 = (bf16[64,3456]{1,0:T(8,128)(2,1)S(1)}, bf16[64,3456]{1,0:T(8,128)(2,1)S(1)}, u32[]{:S(2)}, u32[]{:S(2)}) collective-permute-start(bf16[64,3456]{1,0:T(8,128)(2,1)S(1)} %get-tuple-element.38), channel_id=1, source_target_pairs={{0,32},{1,33},{2,34},{3,35},{4,36},{5,37},{6,38},{7,39},{8,40},{9,... | collective-permute-start | bytes 1327112 | tf_op jit(solution)/shard_map/ppermute | solution.py:63
  33.8 15.1 %collective-permute-start.11 = (bf16[16,4,3584]{2,1,0:T(4,128)(2,1)S(1)}, bf16[16,4,3584]{2,1,0:T(4,128)(2,1)S(1)}, u32[]{:S(2)}, u32[]{:S(2)}) collective-permute-start(bf16[16,4,3584]{2,1,0:T(4,128)(2,1)S(1)} %shard_map.57.near_ref), channel_id=1, source_target_pairs={{0,32},{1,33},{2,34},{3,35},{4,36},{5,37},{6,38},{7,39},{8,40},{9,... | collective-permute-start | bytes 1376264 | tf_op jit(solution)/shard_map/ppermute | solution.py:63
  36.0 22.4 %all-to-all-start = ((bf16[16,4,3456]{2,1,0:T(4,128)(2,1)}), bf16[16,4,3456]{2,1,0:T(4,128)(2,1)S(1)}, u32[]{:S(2)}, u32[]{:S(2)}) async-start(bf16[16,4,3456]{2,1,0:T(4,128)(2,1)} %shard_map.56), calls=%async_computation | async-start | bytes 884736 | tf_op jit(solution)/shard_map/all_to_all | solution.py:70
  59.2 12.1 %all-to-all-start.1 = ((bf16[8,4,3456]{2,1,0:T(4,128)(2,1)}), bf16[8,4,3456]{2,1,0:T(4,128)(2,1)S(1)}, u32[]{:S(2)}, u32[]{:S(2)}) async-start(bf16[8,4,3456]{2,1,0:T(4,128)(2,1)} %shard_map.59), calls=%async_computation.1 | async-start | bytes 442368 | tf_op jit(solution)/shard_map/all_to_all | solution.py:70
  71.3 17.9 %copy-start.4 = (f32[4,27,128]{2,0,1:T(4,128)S(1)}, f32[4,27,128]{2,0,1:T(4,128)}, u32[]{:S(2)}) copy-start(f32[4,27,128]{2,0,1:T(4,128)} %param.3) | copy-start | bytes 165892
  71.4 17.8 %collective-permute-start.12 = (f32[4,3456]{1,0:T(4,128)S(1)}, f32[4,3456]{1,0:T(4,128)S(1)}, u32[]{:S(2)}, u32[]{:S(2)}) collective-permute-start(f32[4,3456]{1,0:T(4,128)S(1)} %get-tuple-element.46), channel_id=1, source_target_pairs={{0,0},{1,64},{2,128},{3,192},{4,4},{5,68},{6,132},{7,196},{8,8},{9... | collective-permute-start | bytes 165896 | tf_op jit(solution)/shard_map/ppermute | solution.py:63

commit v6 on v5

--- a/solution.py
+++ b/solution.py
@@ -102,7 +102,7 @@
     second_ref[0] = mid_ref[jnp.where(odd, last, 0)]
 
 
-def base_kernel(raw_ref, mid_ref, held_ref, zl_ref, zh_ref):
+def base_kernel(raw_ref, mid_ref, in_ref, held_ref, zl_ref, zh_ref, il_ref, ih_ref):
     taps, rows, ch = raw_ref.shape
     base = jnp.sum(jnp.sum(raw_ref[...], axis=0), axis=0, keepdims=True) / (taps * rows)
     high = base.astype(jnp.bfloat16)
@@ -113,11 +113,11 @@
     place = lax.broadcasted_iota(jnp.int32, (rows, ch), 0)
     both = jnp.where(place == 0, high.astype(jnp.float32), low.astype(jnp.float32))
     held_ref[0, :, taps * ch :] = both.astype(jnp.bfloat16)
-    nz = mid_ref.shape[2]
-    for k in range(mid_ref.shape[0]):
-        mid = mid_ref[k].astype(jnp.float32)
-        zl_ref[k] = mid[:, 0].astype(jnp.bfloat16)
-        zh_ref[k] = mid[:, nz - 1].astype(jnp.bfloat16)
+    for whole_ref, first_ref, last_ref in ((mid_ref, zl_ref, zh_ref), (in_ref, il_ref, ih_ref)):
+        for k in range(whole_ref.shape[0]):
+            whole = whole_ref[k].astype(jnp.float32)
+            first_ref[k] = whole[:, 0].astype(jnp.bfloat16)
+            last_ref[k] = whole[:, -1].astype(jnp.bfloat16)
 
 
 def join_kernel(*refs):
@@ -131,68 +131,93 @@
     return jnp.where(odd, first, second), jnp.where(odd, second, first)
 
 
-def height_kernel(mid_ref, xa_ref, xb_ref, first_ref, second_ref):
-    nx, ny = mid_ref.shape[:2]
+def height_kernel(mid_ref, xa_ref, xb_ref, il_ref, ih_ref, first_ref, second_ref):
+    nx, ny, nz, ch = mid_ref.shape
     x_odd, odd = is_odd("gx"), is_odd("gy")
-    for out_ref, j in ((first_ref, jnp.where(odd, 0, ny - 1)), (second_ref, jnp.where(odd, ny - 1, 0))):
+    first, last = il_ref[...].astype(jnp.float32), ih_ref[...].astype(jnp.float32)
+    ends = [jnp.concatenate([first[:, None, j], last[:, None, j]], axis=1) for j in (0, ny - 1)]
+    ends = [e.astype(jnp.bfloat16) for e in ends]
+    outs = ((first_ref, jnp.where(odd, 0, ny - 1)), (second_ref, jnp.where(odd, ny - 1, 0)))
+    for (out_ref, j), end in zip(outs, (picked(odd, *ends))):
         low, high = picked(x_odd, xa_ref[0, j], xb_ref[0, j])
-        out_ref[0] = low
-        out_ref[nx + 1] = high
+        out_ref[0, :nz] = low
+        out_ref[nx + 1, :nz] = high
+        for k in (0, nx + 1):
+            out_ref[k, nz:] = jnp.zeros((2, ch), jnp.bfloat16)
         for k in range(nx):
-            out_ref[k + 1] = mid_ref[k, j]
-
-
-def width_kernel(zl_ref, zh_ref, xa_ref, xb_ref, ya_ref, yb_ref, first_ref, second_ref):
-    nz = ya_ref.shape[1]
-    x_odd, y_odd, odd = is_odd("gx"), is_odd("gy"), is_odd("gz")
-
-    def face(k, own):
-        x_low, x_high = picked(x_odd, xa_ref[0].astype(jnp.float32)[:, k], xb_ref[0].astype(jnp.float32)[:, k])
-        y_low, y_high = picked(y_odd, ya_ref[...].astype(jnp.float32)[:, k], yb_ref[...].astype(jnp.float32)[:, k])
-        deep = jnp.concatenate([x_low[None], own.astype(jnp.float32), x_high[None]], axis=0)
-        return jnp.concatenate([y_low[:, None], deep, y_high[:, None]], axis=1)
-
-    low, high = face(0, zl_ref[...]), face(nz - 1, zh_ref[...])
-    first_ref[...] = jnp.where(odd, low, high).astype(jnp.bfloat16)
-    second_ref[...] = jnp.where(odd, high, low).astype(jnp.bfloat16)
+            out_ref[k + 1, :nz] = mid_ref[k, j]
+        out_ref[1 : nx + 1, nz:] = end
+
+
+def width_kernel(zl_ref, zh_ref, xa_ref, xb_ref, first_ref, second_ref):
+    nx = zl_ref.shape[0]
+    nz = xa_ref.shape[2]
+    x_odd, odd = is_odd("gx"), is_odd("gz")
+    low, high = picked(odd, zl_ref[...], zh_ref[...])
+    first_ref[1 : nx + 1] = low
+    second_ref[1 : nx + 1] = high
+    below, above = picked(x_odd, xa_ref[0].astype(jnp.float32), xb_ref[0].astype(jnp.float32))
+    for k, face in ((0, below), (nx + 1, above)):
+        low, high = picked(odd, face[:, 0], face[:, nz - 1])
+        first_ref[k] = low.astype(jnp.bfloat16)
+        second_ref[k] = high.astype(jnp.bfloat16)
+
+
+def corner_kernel(za_ref, zb_ref, first_ref, second_ref):
+    ny = za_ref.shape[1]
+    odd = is_odd("gy")
+    low, high = picked(is_odd("gz"), za_ref[...].astype(jnp.float32), zb_ref[...].astype(jnp.float32))
+    ends = [jnp.concatenate([low[:, None, j], high[:, None, j]], axis=1) for j in (0, ny - 1)]
+    first, second = picked(odd, *ends)
+    first_ref[...] = first.astype(jnp.bfloat16)
+    second_ref[...] = second.astype(jnp.bfloat16)
 
 
 def fill_taps(taps_ref, mid_ref, xa_ref, xb_ref, ya_ref, yb_ref, z_halo):
-    nx, ny, _, ch = mid_ref.shape
+    nx, ny, nz, ch = mid_ref.shape
     x_odd, y_odd, z_odd = is_odd("gx"), is_odd("gy"), is_odd("gz")
 
-    def fill(k, rows, j, n):
+    def fill(k, j, rows, low, high):
+        n = rows.shape[0]
         mid = rows.astype(jnp.float32)
-        if z_halo:
-            low, high = picked(z_odd, z_halo[0][k, j : j + n], z_halo[1][k, j : j + n])
-            low = low.astype(jnp.float32)[:, None, :]
-            high = high.astype(jnp.float32)[:, None, :]
-        else:
-            low = high = jnp.zeros((n, 1, ch), jnp.float32)
         up = jnp.concatenate([mid[:, 1:], high], axis=1)
         down = jnp.concatenate([low, mid[:, :-1]], axis=1)
         taps_ref[k, j : j + n, :, 0:ch] = up.astype(jnp.bfloat16)
         taps_ref[k, j : j + n, :, ch : 2 * ch] = rows
         taps_ref[k, j : j + n, :, 2 * ch : 3 * ch] = down.astype(jnp.bfloat16)
 
+    def fill_rows(k, rows):
+        if z_halo:
+            low, high = picked(z_odd, z_halo[0][k].astype(jnp.float32), z_halo[1][k].astype(jnp.float32))
+            fill(k, 1, rows, low[:, None], high[:, None])
+        else:
+            none = jnp.zeros((ny, 1, ch), jnp.float32)
+            fill(k, 1, rows, none, none)
+
     def plane(k, carry):
-        low, high = picked(y_odd, ya_ref[k], yb_ref[k])
-        fill(k, low[None], 0, 1)
-        fill(k, high[None], ny + 1, 1)
+        pairs = zip((0, ny + 1), picked(y_odd, ya_ref[k, :nz], yb_ref[k, :nz]))
+        if z_halo:
+            corners = picked(y_odd, z_halo[2][k].astype(jnp.float32), z_halo[3][k].astype(jnp.float32))
+            for (j, row), corner in zip(pairs, corners):
+                fill(k, j, row[None], corner[None, 0:1], corner[None, 1:2])
+        else:
+            none = jnp.zeros((1, 1, ch), jnp.float32)
+            for j, row in pairs:
+                fill(k, j, row[None], none, none)
         return carry
 
     def middle(k, carry):
-        fill(k + 1, mid_ref[k], 1, ny)
+        fill_rows(k + 1, mid_ref[k])
         return carry
 
     lax.fori_loop(0, nx, middle, 0)
     low, high = picked(x_odd, xa_ref[0], xb_ref[0])
-    fill(0, low, 1, ny)
-    fill(nx + 1, high, 1, ny)
+    fill_rows(0, low)
+    fill_rows(nx + 1, high)
     lax.fori_loop(0, nx + 2, plane, 0)
 
 
-def filter_kernel(mid_ref, xa_ref, xb_ref, ya_ref, yb_ref, in_ref, total_ref, first_ref, last_ref, taps_ref):
+def filter_kernel(mid_ref, xa_ref, xb_ref, ya_ref, yb_ref, in_ref, il_ref, ih_ref, total_ref, ends_ref, taps_ref):
     nx, ny, nz, ch = mid_ref.shape
     fill_taps(taps_ref, mid_ref, xa_ref, xb_ref, ya_ref, yb_ref, None)
     cells = nx * ny * nz
@@ -202,33 +227,35 @@
             view = taps_ref[2 - a : 2 - a + nx, 2 - b : 2 - b + ny].reshape(cells, 3 * ch)
             lanes = pl.ds((a * 3 + b) * 3 * ch, 3 * ch)
             total_ref[:, lanes] = jnp.dot(flat, view, preferred_element_type=jnp.float32)
-    for out_ref, j in ((first_ref, 0), (last_ref, nz - 1)):
-        ends = [in_ref[k].astype(jnp.float32)[:, j] for k in range(nx)]
-        out_ref[...] = jnp.concatenate(ends, axis=0).T.astype(jnp.bfloat16)
-
-
-def finish_kernel(total_ref, first_ref, last_ref, za_ref, zb_ref, keep_ref, send_ref):
+    below, above = picked(is_odd("gy"), ya_ref[1 : nx + 1, nz:], yb_ref[1 : nx + 1, nz:])
+    below, above = below.astype(jnp.float32), above.astype(jnp.float32)
+    for side, own_ref in enumerate((il_ref, ih_ref)):
+        own = own_ref[...].astype(jnp.float32)
+        face = jnp.concatenate([below[:, side : side + 1], own, above[:, side : side + 1]], axis=1)
+        for b in range(3):
+            ends_ref[side, b] = face[:, b : b + ny].reshape(nx * ny, ch).T.astype(jnp.bfloat16)
+
+
+def finish_kernel(total_ref, ends_ref, za_ref, zb_ref, keep_ref, send_ref):
     ch = total_ref.shape[0]
-    nx, ny = za_ref.shape[0] - 2, za_ref.shape[1] - 2
+    nx, ny = za_ref.shape[0] - 2, za_ref.shape[1]
     core = lax.axis_index("gx") % CORES
-    low, high = picked(is_odd("gz"), za_ref[...].astype(jnp.float32), zb_ref[...].astype(jnp.float32))
-
-    def shifted(face):
-        return jnp.concatenate([face[:, 2 - b : 2 - b + ny] for b in range(3)], axis=2).astype(jnp.bfloat16)
-
-    low, high = shifted(low), shifted(high)
-    for a in range(3):
-        rows = slice(2 - a, 2 - a + nx)
-        above = jnp.dot(last_ref[...], high[rows].reshape(nx * ny, 3 * ch), preferred_element_type=jnp.float32)
-        below = jnp.dot(first_ref[...], low[rows].reshape(nx * ny, 3 * ch), preferred_element_type=jnp.float32)
-        for b in range(3):
+    crossing = []
+    for halo in picked(is_odd("gz"), za_ref[...], zb_ref[...]):
+        crossing.append(
+            jnp.concatenate([halo[2 - a : 2 - a + nx].reshape(nx * ny, ch) for a in range(3)], axis=1)
+        )
+    for b in range(3):
+        below = jnp.dot(ends_ref[0, b], crossing[0], preferred_element_type=jnp.float32)
+        above = jnp.dot(ends_ref[1, b], crossing[1], preferred_element_type=jnp.float32)
+        for a in range(3):
             for c in range(3):
                 lanes = pl.ds(((a * 3 + b) * 3 + c) * ch, ch)
                 res = total_ref[:, lanes]
                 if c == 0:
-                    res = res + above[:, b * ch : (b + 1) * ch]
+                    res = res + above[:, a * ch : (a + 1) * ch]
                 if c == 2:
-                    res = res + below[:, b * ch : (b + 1) * ch]
+                    res = res + below[:, a * ch : (a + 1) * ch]
                 for g in range(ch // 32):
                     first = res[g * 32 : g * 32 + 16]
                     second = res[g * 32 + 16 : g * 32 + 32]
@@ -260,9 +287,9 @@
         sums_ref[k] = three
 
 
-def input_kernel(mid_ref, xa_ref, xb_ref, ya_ref, yb_ref, za_ref, zb_ref, std_ref, out_ref, taps_ref):
+def input_kernel(mid_ref, xa_ref, xb_ref, ya_ref, yb_ref, za_ref, zb_ref, ca_ref, cb_ref, std_ref, out_ref, taps_ref):
     nx, ny, nz, ch = out_ref.shape
-    fill_taps(taps_ref, mid_ref, xa_ref, xb_ref, ya_ref, yb_ref, (za_ref, zb_ref))
+    fill_taps(taps_ref, mid_ref, xa_ref, xb_ref, ya_ref, yb_ref, (za_ref, zb_ref, ca_ref, cb_ref))
     planes = 2
     std = std_ref[...]
     for x in range(0, nx, planes):
@@ -347,33 +374,40 @@
 
     faces = call(faces_kernel, both((1, ny, nz, ch)), (cotangent,))
     x_halo = swapped(*faces, "gx")
-    block, *width_faces = call(base_kernel, (of((1, rows, width + ch), bf16), *both((nx, ny, ch))), (raw, cotangent))
+    block, *ends = call(
+        base_kernel,
+        (of((1, rows, width + ch), bf16), *both((nx, ny, ch)), *both((nx, ny, ch))),
+        (raw, cotangent, inputs),
+    )
     held = [block, where.send(block, lambda s: dict(y=s["y"] ^ 1))]
-    faces = call(height_kernel, both((nx + 2, nz, ch)), (cotangent, *x_halo))
+    faces = call(height_kernel, both((nx + 2, nz + 2, ch)), (cotangent, *x_halo, *ends[2:]))
     y_halo = swapped(*faces, "gy")
+    faces = call(width_kernel, both((nx + 2, ny, ch)), (*ends[:2], *x_halo))
+    z_halo = swapped(*faces, "gz")
     held.append(where.send(joined(held), lambda s: dict(y=s["y"] ^ 2)))
-    faces = call(width_kernel, both((nx + 2, ny + 2, ch)), (*width_faces, *x_halo, *y_halo))
-    z_halo = swapped(*faces, "gz")
     held.append(where.send(joined(held), lambda s: dict(zl=s["zl"] ^ 1)))
     held.append(where.send(joined(held), lambda s: dict(zl=s["zl"] ^ 2)))
 
     flops = 2 * nx * ny * nz * ch * width
     scratch = [pltpu.VMEM((nx + 2, ny + 2, nz, 3 * ch), bf16)]
-    total, *ends = call(
+    total, end_rows = call(
         filter_kernel,
-        (of((ch, width), f32), of((ch, nx * ny), bf16), of((ch, nx * ny), bf16)),
-        (cotangent, *x_halo, *y_halo, inputs),
+        (of((ch, width), f32), of((2, 3, ch, nx * ny), bf16)),
+        (cotangent, *x_halo, *y_halo, inputs, *ends[2:]),
         vmem=16,
         flops=2 * flops,
         scratch=scratch,
     )
-    keep, send = call(finish_kernel, (of((ch // 2, width), f32), of((ch // 2, width), bf16)), (total, *ends, *z_halo))
+    keep, send = call(
+        finish_kernel, (of((ch // 2, width), f32), of((ch // 2, width), bf16)), (total, end_rows, *z_halo)
+    )
     other = where.send(send, lambda s: dict(core=1 - s["core"]))
     held = call(join_kernel, of((16, rows, width + ch), bf16), held)
     peers = where.x * where.gy
     half = call(pair_kernel, of((peers, rows, width), bf16), (keep, other))
     parts = where.exchange(half, ("core", "zl", "zh"), lambda s: (s["x"], s["y"]))
     far = where.send(held, lambda s: dict(core=1 - s["core"]))
+    corners = swapped(*call(corner_kernel, both((nx + 2, 2, ch)), z_halo), "gy")
     std_half, mean_out, inv_std, block_std = call(
         functools.partial(std_kernel, where.x),
         (of((ch, width), bf16), of((1, ch), f32), of((1, ch), f32), of((rows, width), f32)),
@@ -386,7 +420,7 @@
     input_grad = call(
         input_kernel,
         of(inputs.shape, bf16),
-        (cotangent, *x_halo, *y_halo, *z_halo, std_half),
+        (cotangent, *x_halo, *y_halo, *z_halo, *corners, std_half),
         vmem=16,
         flops=2 * flops,
         scratch=scratch,

time: 90.6 us -> 99.2 us (1.095)
  blocking collectives: 17.1 us -> 21.6 us
  starting transfers between devices: 38.2 us -> 41.3 us
  local copies, waits for them, and re-layouts: 1.86 us -> 2.9 us
    all_to_all x1, blocking collectives: 17.1 us -> 21.6 us  [exchange(): lax.all_to_all(array, AXES, 0, 0, tiled=True, axis_index_groups=groups)]
    all_to_all x2, waiting for transfers between devices: 11.6 us -> 9.3 us  [exchange(): lax.all_to_all(array, AXES, 0, 0, tiled=True, axis_index_groups=groups)]
    all_to_all x2, starting transfers between devices: 16.5 us -> 18.2 us  [exchange(): lax.all_to_all(array, AXES, 0, 0, tiled=True, axis_index_groups=groups)]
    ppermute x3 -> x4, waiting for transfers between devices: 0.01 us -> 1.22 us  [swapped(): lax.ppermute(first, axis, pairs(0))]
    unnamed x10 -> x12, local copies, waits for them, and re-layouts: 1.86 us -> 2.9 us
    ppermute x3 -> x4, starting transfers between devices: 4.58 us -> 5.58 us  [swapped(): lax.ppermute(second, axis, pairs(1))]
    ppermute x3 -> x4, starting transfers between devices: 3.79 us -> 4.48 us  [swapped(): lax.ppermute(first, axis, pairs(0))]
    pallas_call x13 -> x14, Pallas kernels: 12.8 us -> 12.9 us  [call(): pl.pallas_call(kernel, out_shape=out_shape, in_specs=[pl.BlockSpec(memory...]
  transfers between devices with their start and end apart: 15 -> 17, of which waited for: 4 -> 6; matrix products, arithmetic and copies ran while one was open for 0% -> 0% of each run, Pallas kernels for 12% -> 11%
where the time goes in v6:
time: 99.2 us; the launch traced here: 98.6 us
  starting transfers between devices  41.3 us (42%)
  blocking collectives  21.6 us (22%)
  waiting for transfers between devices  18.8 us (19%)
  Pallas kernels  12.9 us (13%)
  local copies, waits for them, and re-layouts  2.9 us (3%)
    all_to_all x1, blocking collectives, exchange(): lax.all_to_all(array, AXES, 0, 0, tiled=True, axis_index_groups=groups)  21.6 us
    all_to_all x2, starting transfers between devices, exchange(): lax.all_to_all(array, AXES, 0, 0, tiled=True, axis_index_groups=groups)  18.2 us
    ppermute x7, starting transfers between devices, send(): return lax.ppermute(array, AXES, pairs)  13 us
    pallas_call x14, Pallas kernels, call(): pl.pallas_call(kernel, out_shape=out_shape, in_specs=[pl.BlockSpec(memory...  12.9 us
    all_to_all x2, waiting for transfers between devices, exchange(): lax.all_to_all(array, AXES, 0, 0, tiled=True, axis_index_groups=groups)  9.3 us
    ppermute x7, waiting for transfers between devices, send(): return lax.ppermute(array, AXES, pairs)  7.95 us
    ppermute x4, starting transfers between devices, swapped(): lax.ppermute(second, axis, pairs(1))  5.58 us
    ppermute x4, starting transfers between devices, swapped(): lax.ppermute(first, axis, pairs(0))  4.48 us
  transfers between devices with their start and end apart: 17, of which 6 were waited for; matrix products, arithmetic and copies ran while one was open for 0% of the time, Pallas kernels for 11%

profile of v6, /device:TPU:1, one launch (start us, length us, event | category | flops | bytes accessed | tf_op | source)
XLA Modules:
  0.0 98.6 jit_solution(12406666028494098200)
XLA Ops:
  0.6 0.0 copy-start
  0.6 1.0 %copy-done = bf16[8,16,16,128]{3,2,1,0:T(8,128)(2,1)S(1)} copy-done((bf16[8,16,16,128]{3,2,1,0:T(8,128)(2,1)S(1)}, bf16[8,16,16,128]{3,2,1,0:T(8,128)(2,1)}, u32[]{:S(2)}) %copy-start) | copy-done | bytes 524312
  1.7 1.0 %copy-done.2 = bf16[8,16,16,128]{3,2,1,0:T(8,128)(2,1)S(1)} copy-done((bf16[8,16,16,128]{3,2,1,0:T(8,128)(2,1)S(1)}, bf16[8,16,16,128]{3,2,1,0:T(8,128)(2,1)}, u32[]{:S(2)}) %copy-start.2) | copy-done | bytes 524312
  2.7 0.8 copy-done.4
  3.5 0.2 shard_map.51
  3.8 2.2 %collective-permute-start.7 = (bf16[1,4,3584]{2,1,0:T(4,128)(2,1)S(1)}, bf16[1,4,3584]{2,1,0:T(4,128)(2,1)S(1)}, u32[]{:S(2)}, u32[]{:S(2)}) collective-permute-start(bf16[1,4,3584]{2,1,0:T(4,128)(2,1)S(1)} %get-tuple-element.43.refs_0_), channel_id=1, source_target_pairs={{0,8},{1,9},{2,10},{3,11},{4,12},{5,13},{6,14},{7,15},{8,0},{9,1},... | collective-permute-start | bytes 86024 | tf_op jit(solution)/shard_map/ppermute | solution.py:63
  6.0 1.3 %collective-permute-done.7.refs_1_ = bf16[1,4,3584]{2,1,0:T(4,128)(2,1)S(1)} collective-permute-done((bf16[1,4,3584]{2,1,0:T(4,128)(2,1)S(1)}, bf16[1,4,3584]{2,1,0:T(4,128)(2,1)S(1)}, u32[]{:S(2)}, u32[]{:S(2)}) %collective-permute-start.7) | collective-permute-done | bytes 28704 | tf_op jit(solution)/shard_map/ppermute | solution.py:63
  7.3 3.2 %collective-permute-start.8 = (bf16[2,4,3584]{2,1,0:T(4,128)(2,1)S(1)}, bf16[2,4,3584]{2,1,0:T(4,128)(2,1)S(1)}, u32[]{:S(2)}, u32[]{:S(2)}) collective-permute-start(bf16[2,4,3584]{2,1,0:T(4,128)(2,1)S(1)} %pad_maximum_fusion.2), channel_id=1, source_target_pairs={{0,16},{1,17},{2,18},{3,19},{4,20},{5,21},{6,22},{7,23},{8,24},{9,... | collective-permute-start | bytes 172040 | tf_op jit(solution)/shard_map/ppermute | solution.py:63
  10.4 2.2 %collective-permute-start = (bf16[1,16,16,128]{3,2,1,0:T(8,128)(2,1)S(1)}, bf16[1,16,16,128]{3,2,1,0:T(8,128)(2,1)S(1)}, u32[]{:S(2)}, u32[]{:S(2)}) collective-permute-start(bf16[1,16,16,128]{3,2,1,0:T(8,128)(2,1)S(1)} %get-tuple-element.29), channel_id=1, source_target_pairs={{0,32},{64,96},{128,160},{192,224},{32,0},{96,64},{160,128},{224,1... | collective-permute-start | bytes 196616 | tf_op jit(solution)/shard_map/ppermute | solution.py:80
  12.6 3.4 %collective-permute-start.1 = (bf16[1,16,16,128]{3,2,1,0:T(8,128)(2,1)S(1)}, bf16[1,16,16,128]{3,2,1,0:T(8,128)(2,1)S(1)}, u32[]{:S(2)}, u32[]{:S(2)}) collective-permute-start(bf16[1,16,16,128]{3,2,1,0:T(8,128)(2,1)S(1)} %get-tuple-element.30), channel_id=1, source_target_pairs={{32,64},{96,128},{160,192},{64,32},{128,96},{192,160},{33,65},{97,... | collective-permute-start | bytes 196616 | tf_op jit(solution)/shard_map/ppermute | solution.py:80
  16.1 0.0 collective-permute-done.8.refs_2_
  16.1 0.1 pad_maximum_fusion.1
  16.2 1.7 %collective-permute-start.9 = (bf16[4,4,3584]{2,1,0:T(4,128)(2,1)S(1)}, bf16[4,4,3584]{2,1,0:T(4,128)(2,1)S(1)}, u32[]{:S(2)}, u32[]{:S(2)}) collective-permute-start(bf16[4,4,3584]{2,1,0:T(4,128)(2,1)S(1)} %pad_maximum_fusion.1), channel_id=1, source_target_pairs={{0,64},{1,65},{2,66},{3,67},{4,68},{5,69},{6,70},{7,71},{8,72},{9,... | collective-permute-start | bytes 344072 | tf_op jit(solution)/shard_map/ppermute | solution.py:63
  17.9 0.3 collective-permute-done.1.xb_ref
  18.2 0.5 collective-permute-start.2
  18.7 0.7 collective-permute-start.3
  19.4 0.0 copy-start.1
  19.4 0.1 shard_map.54
  19.5 1.3 %collective-permute-start.4 = (bf16[10,16,128]{2,1,0:T(8,128)(2,1)S(1)}, bf16[10,16,128]{2,1,0:T(8,128)(2,1)S(1)}, u32[]{:S(2)}, u32[]{:S(2)}) collective-permute-start(bf16[10,16,128]{2,1,0:T(8,128)(2,1)S(1)} %get-tuple-element.39), channel_id=1, source_target_pairs={{0,1},{2,3},{4,5},{6,7},{1,0},{3,2},{5,4},{7,6},{8,9},{10,11},{12,... | collective-permute-start | bytes 122888 | tf_op jit(solution)/shard_map/ppermute | solution.py:80
  20.8 0.7 collective-permute-start.5
  21.5 0.2 pad_maximum_fusion
  21.7 3.1 %collective-permute-start.10 = (bf16[8,4,3584]{2,1,0:T(4,128)(2,1)S(1)}, bf16[8,4,3584]{2,1,0:T(4,128)(2,1)S(1)}, u32[]{:S(2)}, u32[]{:S(2)}) collective-permute-start(bf16[8,4,3584]{2,1,0:T(4,128)(2,1)S(1)} %pad_maximum_fusion), channel_id=1, source_target_pairs={{0,128},{1,129},{2,130},{3,131},{4,132},{5,133},{6,134},{7,135},{8... | collective-permute-start | bytes 688136 | tf_op jit(solution)/shard_map/ppermute | solution.py:63
  24.7 0.0 collective-permute-done.2.ya_ref
  24.7 0.0 collective-permute-done.3.yb_ref
  24.7 3.2 %shard_map.53 = (f32[128,3456]{1,0:T(8,128)S(1)}, bf16[2,3,128,128]{3,2,1,0:T(8,128)(2,1)S(1)}) custom-call(bf16[8,16,16,128]{3,2,1,0:T(8,128)(2,1)S(1)} %copy-done.3, bf16[1,16,16,128]{3,2,1,0:T(8,128)(2,1)S(1)} %collective-permute-done.xa_ref, bf16[1,16,16,128]{3,2,1,0:T(8,128)(2,1)S(1)} %collective-permute-done.1.xb_ref, ...), custom_call_target="tpu_custom_call" | custom-call | flops 3623878656 | bytes 1000000 | tf_op jit(solution)/shard_map/pallas_call | solution.py:22
  27.9 0.0 collective-permute-done.4.za_ref
  28.0 0.3 shard_map.55
  28.3 1.0 collective-permute-start.6
  29.3 6.7 %collective-permute-done.10.refs_4_ = bf16[8,4,3584]{2,1,0:T(4,128)(2,1)S(1)} collective-permute-done((bf16[8,4,3584]{2,1,0:T(4,128)(2,1)S(1)}, bf16[8,4,3584]{2,1,0:T(4,128)(2,1)S(1)}, u32[]{:S(2)}, u32[]{:S(2)}) %collective-permute-start.10) | collective-permute-done | bytes 229408 | tf_op jit(solution)/shard_map/ppermute | solution.py:63
  36.0 1.2 %collective-permute-start.11 = (bf16[16,4,3584]{2,1,0:T(4,128)(2,1)S(1)}, bf16[16,4,3584]{2,1,0:T(4,128)(2,1)S(1)}, u32[]{:S(2)}, u32[]{:S(2)}) collective-permute-start(bf16[16,4,3584]{2,1,0:T(4,128)(2,1)S(1)} %shard_map.57.near_ref), channel_id=1, source_target_pairs={{0,32},{1,33},{2,34},{3,35},{4,36},{5,37},{6,38},{7,39},{8,40},{9,... | collective-permute-start | bytes 1376264 | tf_op jit(solution)/shard_map/ppermute | solution.py:63
  37.2 0.0 collective-permute-done.6.other_ref
  37.2 0.9 shard_map.56
  38.1 14.8 %all-to-all-start = ((bf16[16,4,3456]{2,1,0:T(4,128)(2,1)}), bf16[16,4,3456]{2,1,0:T(4,128)(2,1)S(1)}, u32[]{:S(2)}, u32[]{:S(2)}) async-start(bf16[16,4,3456]{2,1,0:T(4,128)(2,1)} %shard_map.56), calls=%async_computation | async-start | bytes 884736 | tf_op jit(solution)/shard_map/all_to_all | solution.py:70
  52.9 0.0 collective-permute-done.11.far_ref
  52.9 1.1 %shard_map.58 = (bf16[128,3456]{1,0:T(8,128)(2,1)S(1)}, f32[1,128]{1,0:T(1,128)S(1)}, f32[1,128]{1,0:T(1,128)S(1)}, f32[4,3456]{1,0:T(4,128)S(1)}) custom-call(bf16[16,4,3584]{2,1,0:T(4,128)(2,1)S(1)} %shard_map.57.near_ref, bf16[16,4,3584]{2,1,0:T(4,128)(2,1)S(1)} %collective-permute-done.11.far_ref), custom_call_target="tpu_custom_call" | custom-call | flops 3000000000 | bytes 1000000 | tf_op jit(solution)/shard_map/pallas_call | solution.py:22
  54.0 8.4 %all-to-all-done.parts_ref = bf16[16,4,3456]{2,1,0:T(4,128)(2,1)S(1)} async-done(((bf16[16,4,3456]{2,1,0:T(4,128)(2,1)}), bf16[16,4,3456]{2,1,0:T(4,128)(2,1)S(1)}, u32[]{:S(2)}, u32[]{:S(2)}) %all-to-all-start) | async-done | bytes 442400 | tf_op jit(solution)/shard_map/all_to_all | solution.py:70
  62.4 0.9 shard_map.59
  63.3 3.4 %all-to-all-start.1 = ((bf16[8,4,3456]{2,1,0:T(4,128)(2,1)}), bf16[8,4,3456]{2,1,0:T(4,128)(2,1)S(1)}, u32[]{:S(2)}, u32[]{:S(2)}) async-start(bf16[8,4,3456]{2,1,0:T(4,128)(2,1)} %shard_map.59), calls=%async_computation.1 | async-start | bytes 442368 | tf_op jit(solution)/shard_map/all_to_all | solution.py:70
  66.7 0.5 collective-permute-start.12
  67.2 0.8 collective-permute-start.13
  68.1 1.2 %collective-permute-done.12.ca_ref = bf16[10,2,128]{2,1,0:T(2,128)(2,1)S(1)} collective-permute-done((bf16[10,2,128]{2,1,0:T(2,128)(2,1)S(1)}, bf16[10,2,128]{2,1,0:T(2,128)(2,1)S(1)}, u32[]{:S(2)}, u32[]{:S(2)}) %collective-permute-start.12) | collective-permute-done | bytes 5152 | tf_op jit(solution)/shard_map/ppermute | solution.py:80
  69.3 0.0 collective-permute-done.13.cb_ref
  69.3 5.2 %shard_map.61 = bf16[8,16,16,128]{3,2,1,0:T(8,128)(2,1)} custom-call(bf16[8,16,16,128]{3,2,1,0:T(8,128)(2,1)S(1)} %copy-done.3, bf16[1,16,16,128]{3,2,1,0:T(8,128)(2,1)S(1)} %collective-permute-done.xa_ref, bf16[1,16,16,128]{3,2,1,0:T(8,128)(2,1)S(1)} %collective-permute-done.1.xb_ref, bf16[10,18,128]{2,1,0:T(8,128)(2,1)S(1)} %collective-permute-done.2.ya_ref, ...), custom_call_target="tpu_custom_call" | custom-call | flops 3623878656 | bytes 1000000 | tf_op jit(solution)/shard_map/pallas_call | solution.py:22
  74.5 0.9 all-to-all-done.1.parts_ref
  75.4 0.1 shard_map.62
  75.5 0.7 collective-permute-start.14
  76.2 21.6 %all_to_all.15.sums_ref = f32[32,1,384]{2,1,0:T(1,128)S(1)} all-to-all(f32[32,1,384]{2,1,0:T(1,128)S(1)} %get-tuple-element.55), channel_id=1, replica_groups={{0,8,16,24,1,9,17,25,2,10,18,26,3,11,19,27,32,40,48,56,33,41,49,57,34,4..., dimensions={0} | all-to-all | bytes 98304 | tf_op jit(solution)/shard_map/all_to_all | solution.py:70
  97.8 0.8 shard_map.63
  (16 shorter events, 0.2 us)
Async XLA Ops:
  0.6 1.0 %copy-start = (bf16[8,16,16,128]{3,2,1,0:T(8,128)(2,1)S(1)}, bf16[8,16,16,128]{3,2,1,0:T(8,128)(2,1)}, u32[]{:S(2)}) copy-start(bf16[8,16,16,128]{3,2,1,0:T(8,128)(2,1)} %in_ref.3) | copy-start | bytes 1572868
  1.7 1.0 %copy-start.2 = (bf16[8,16,16,128]{3,2,1,0:T(8,128)(2,1)S(1)}, bf16[8,16,16,128]{3,2,1,0:T(8,128)(2,1)}, u32[]{:S(2)}) copy-start(bf16[8,16,16,128]{3,2,1,0:T(8,128)(2,1)} %mid_ref.9) | copy-start | bytes 1572868
  2.7 0.8 copy-start.4
  3.5 6.9 %copy-start.3 = (bf16[8,16,16,128]{3,2,1,0:T(8,128)(2,1)S(1)}, bf16[8,16,16,128]{3,2,1,0:T(8,128)(2,1)}, u32[]{:S(2)}) copy-start(bf16[8,16,16,128]{3,2,1,0:T(8,128)(2,1)} %mid_ref.9) | copy-start | bytes 1572868
  3.8 3.5 %collective-permute-start.7 = (bf16[1,4,3584]{2,1,0:T(4,128)(2,1)S(1)}, bf16[1,4,3584]{2,1,0:T(4,128)(2,1)S(1)}, u32[]{:S(2)}, u32[]{:S(2)}) collective-permute-start(bf16[1,4,3584]{2,1,0:T(4,128)(2,1)S(1)} %get-tuple-element.43.refs_0_), channel_id=1, source_target_pairs={{0,8},{1,9},{2,10},{3,11},{4,12},{5,13},{6,14},{7,15},{8,0},{9,1},... | collective-permute-start | bytes 86024 | tf_op jit(solution)/shard_map/ppermute | solution.py:63
  7.3 8.8 %collective-permute-start.8 = (bf16[2,4,3584]{2,1,0:T(4,128)(2,1)S(1)}, bf16[2,4,3584]{2,1,0:T(4,128)(2,1)S(1)}, u32[]{:S(2)}, u32[]{:S(2)}) collective-permute-start(bf16[2,4,3584]{2,1,0:T(4,128)(2,1)S(1)} %pad_maximum_fusion.2), channel_id=1, source_target_pairs={{0,16},{1,17},{2,18},{3,19},{4,20},{5,21},{6,22},{7,23},{8,24},{9,... | collective-permute-start | bytes 172040 | tf_op jit(solution)/shard_map/ppermute | solution.py:63
  10.4 7.5 %collective-permute-start = (bf16[1,16,16,128]{3,2,1,0:T(8,128)(2,1)S(1)}, bf16[1,16,16,128]{3,2,1,0:T(8,128)(2,1)S(1)}, u32[]{:S(2)}, u32[]{:S(2)}) collective-permute-start(bf16[1,16,16,128]{3,2,1,0:T(8,128)(2,1)S(1)} %get-tuple-element.29), channel_id=1, source_target_pairs={{0,32},{64,96},{128,160},{192,224},{32,0},{96,64},{160,128},{224,1... | collective-permute-start | bytes 196616 | tf_op jit(solution)/shard_map/ppermute | solution.py:80
  12.6 5.6 %collective-permute-start.1 = (bf16[1,16,16,128]{3,2,1,0:T(8,128)(2,1)S(1)}, bf16[1,16,16,128]{3,2,1,0:T(8,128)(2,1)S(1)}, u32[]{:S(2)}, u32[]{:S(2)}) collective-permute-start(bf16[1,16,16,128]{3,2,1,0:T(8,128)(2,1)S(1)} %get-tuple-element.30), channel_id=1, source_target_pairs={{32,64},{96,128},{160,192},{64,32},{128,96},{192,160},{33,65},{97,... | collective-permute-start | bytes 196616 | tf_op jit(solution)/shard_map/ppermute | solution.py:80
  16.2 5.3 %collective-permute-start.9 = (bf16[4,4,3584]{2,1,0:T(4,128)(2,1)S(1)}, bf16[4,4,3584]{2,1,0:T(4,128)(2,1)S(1)}, u32[]{:S(2)}, u32[]{:S(2)}) collective-permute-start(bf16[4,4,3584]{2,1,0:T(4,128)(2,1)S(1)} %pad_maximum_fusion.1), channel_id=1, source_target_pairs={{0,64},{1,65},{2,66},{3,67},{4,68},{5,69},{6,70},{7,71},{8,72},{9,... | collective-permute-start | bytes 344072 | tf_op jit(solution)/shard_map/ppermute | solution.py:63
  18.2 6.5 %collective-permute-start.2 = (bf16[10,18,128]{2,1,0:T(8,128)(2,1)S(1)}, bf16[10,18,128]{2,1,0:T(8,128)(2,1)S(1)}, u32[]{:S(2)}, u32[]{:S(2)}) collective-permute-start(bf16[10,18,128]{2,1,0:T(8,128)(2,1)S(1)} %get-tuple-element.33), channel_id=1, source_target_pairs={{0,8},{16,24},{8,0},{24,16},{1,9},{17,25},{9,1},{25,17},{2,10},{18... | collective-permute-start | bytes 138248 | tf_op jit(solution)/shard_map/ppermute | solution.py:80
  18.7 6.0 %collective-permute-start.3 = (bf16[10,18,128]{2,1,0:T(8,128)(2,1)S(1)}, bf16[10,18,128]{2,1,0:T(8,128)(2,1)S(1)}, u32[]{:S(2)}, u32[]{:S(2)}) collective-permute-start(bf16[10,18,128]{2,1,0:T(8,128)(2,1)S(1)} %get-tuple-element.34), channel_id=1, source_target_pairs={{8,16},{16,8},{9,17},{17,9},{10,18},{18,10},{11,19},{19,11},{12,20... | collective-permute-start | bytes 138248 | tf_op jit(solution)/shard_map/ppermute | solution.py:80
  19.4 5.4 %copy-start.1 = (bf16[8,16,16,128]{3,2,1,0:T(8,128)(2,1)S(1)}, bf16[8,16,16,128]{3,2,1,0:T(8,128)(2,1)}, u32[]{:S(2)}) copy-start(bf16[8,16,16,128]{3,2,1,0:T(8,128)(2,1)} %in_ref.3) | copy-start | bytes 1572868
  19.5 8.4 %collective-permute-start.4 = (bf16[10,16,128]{2,1,0:T(8,128)(2,1)S(1)}, bf16[10,16,128]{2,1,0:T(8,128)(2,1)S(1)}, u32[]{:S(2)}, u32[]{:S(2)}) collective-permute-start(bf16[10,16,128]{2,1,0:T(8,128)(2,1)S(1)} %get-tuple-element.39), channel_id=1, source_target_pairs={{0,1},{2,3},{4,5},{6,7},{1,0},{3,2},{5,4},{7,6},{8,9},{10,11},{12,... | collective-permute-start | bytes 122888 | tf_op jit(solution)/shard_map/ppermute | solution.py:80
  20.8 7.1 %collective-permute-start.5 = (bf16[10,16,128]{2,1,0:T(8,128)(2,1)S(1)}, bf16[10,16,128]{2,1,0:T(8,128)(2,1)S(1)}, u32[]{:S(2)}, u32[]{:S(2)}) collective-permute-start(bf16[10,16,128]{2,1,0:T(8,128)(2,1)S(1)} %get-tuple-element.40), channel_id=1, source_target_pairs={{1,2},{3,4},{5,6},{2,1},{4,3},{6,5},{9,10},{11,12},{13,14},{10,9},... | collective-permute-start | bytes 122888 | tf_op jit(solution)/shard_map/ppermute | solution.py:80
  21.7 14.3 %collective-permute-start.10 = (bf16[8,4,3584]{2,1,0:T(4,128)(2,1)S(1)}, bf16[8,4,3584]{2,1,0:T(4,128)(2,1)S(1)}, u32[]{:S(2)}, u32[]{:S(2)}) collective-permute-start(bf16[8,4,3584]{2,1,0:T(4,128)(2,1)S(1)} %pad_maximum_fusion), channel_id=1, source_target_pairs={{0,128},{1,129},{2,130},{3,131},{4,132},{5,133},{6,134},{7,135},{8... | collective-permute-start | bytes 688136 | tf_op jit(solution)/shard_map/ppermute | solution.py:63
  28.3 8.9 %collective-permute-start.6 = (bf16[64,3456]{1,0:T(8,128)(2,1)S(1)}, bf16[64,3456]{1,0:T(8,128)(2,1)S(1)}, u32[]{:S(2)}, u32[]{:S(2)}) collective-permute-start(bf16[64,3456]{1,0:T(8,128)(2,1)S(1)} %get-tuple-element.42), channel_id=1, source_target_pairs={{0,32},{1,33},{2,34},{3,35},{4,36},{5,37},{6,38},{7,39},{8,40},{9,... | collective-permute-start | bytes 1327112 | tf_op jit(solution)/shard_map/ppermute | solution.py:63
  36.0 16.9 %collective-permute-start.11 = (bf16[16,4,3584]{2,1,0:T(4,128)(2,1)S(1)}, bf16[16,4,3584]{2,1,0:T(4,128)(2,1)S(1)}, u32[]{:S(2)}, u32[]{:S(2)}) collective-permute-start(bf16[16,4,3584]{2,1,0:T(4,128)(2,1)S(1)} %shard_map.57.near_ref), channel_id=1, source_target_pairs={{0,32},{1,33},{2,34},{3,35},{4,36},{5,37},{6,38},{7,39},{8,40},{9,... | collective-permute-start | bytes 1376264 | tf_op jit(solution)/shard_map/ppermute | solution.py:63
  38.1 24.3 %all-to-all-start = ((bf16[16,4,3456]{2,1,0:T(4,128)(2,1)}), bf16[16,4,3456]{2,1,0:T(4,128)(2,1)S(1)}, u32[]{:S(2)}, u32[]{:S(2)}) async-start(bf16[16,4,3456]{2,1,0:T(4,128)(2,1)} %shard_map.56), calls=%async_computation | async-start | bytes 884736 | tf_op jit(solution)/shard_map/all_to_all | solution.py:70
  63.3 12.1 %all-to-all-start.1 = ((bf16[8,4,3456]{2,1,0:T(4,128)(2,1)}), bf16[8,4,3456]{2,1,0:T(4,128)(2,1)S(1)}, u32[]{:S(2)}, u32[]{:S(2)}) async-start(bf16[8,4,3456]{2,1,0:T(4,128)(2,1)} %shard_map.59), calls=%async_computation.1 | async-start | bytes 442368 | tf_op jit(solution)/shard_map/all_to_all | solution.py:70
  66.7 2.6 %collective-permute-start.12 = (bf16[10,2,128]{2,1,0:T(2,128)(2,1)S(1)}, bf16[10,2,128]{2,1,0:T(2,128)(2,1)S(1)}, u32[]{:S(2)}, u32[]{:S(2)}) collective-permute-start(bf16[10,2,128]{2,1,0:T(2,128)(2,1)S(1)} %get-tuple-element.46), channel_id=1, source_target_pairs={{0,8},{16,24},{8,0},{24,16},{1,9},{17,25},{9,1},{25,17},{2,10},{18... | collective-permute-start | bytes 15368 | tf_op jit(solution)/shard_map/ppermute | solution.py:80
  67.2 2.0 %collective-permute-start.13 = (bf16[10,2,128]{2,1,0:T(2,128)(2,1)S(1)}, bf16[10,2,128]{2,1,0:T(2,128)(2,1)S(1)}, u32[]{:S(2)}, u32[]{:S(2)}) collective-permute-start(bf16[10,2,128]{2,1,0:T(2,128)(2,1)S(1)} %get-tuple-element.47), channel_id=1, source_target_pairs={{8,16},{16,8},{9,17},{17,9},{10,18},{18,10},{11,19},{19,11},{12,20... | collective-permute-start | bytes 15368 | tf_op jit(solution)/shard_map/ppermute | solution.py:80
  75.4 22.4 %copy-start.5 = (f32[4,27,128]{2,0,1:T(4,128)S(1)}, f32[4,27,128]{2,0,1:T(4,128)}, u32[]{:S(2)}) copy-start(f32[4,27,128]{2,0,1:T(4,128)} %param.3) | copy-start | bytes 165892
  75.5 22.3 %collective-permute-start.14 = (f32[4,3456]{1,0:T(4,128)S(1)}, f32[4,3456]{1,0:T(4,128)S(1)}, u32[]{:S(2)}, u32[]{:S(2)}) collective-permute-start(f32[4,3456]{1,0:T(4,128)S(1)} %get-tuple-element.52), channel_id=1, source_target_pairs={{0,0},{1,64},{2,128},{3,192},{4,4},{5,68},{6,132},{7,196},{8,8},{9... | collective-permute-start | bytes 165896 | tf_op jit(solution)/shard_map/ppermute | solution.py:63

commit v7 on v6

--- a/solution.py
+++ b/solution.py
@@ -77,7 +77,9 @@
         ends = [(i, i + 1) for i in range(start, count - 1, 2)]
         return ends + [(j, i) for i, j in ends]
 
-    return lax.ppermute(first, axis, pairs(0)), lax.ppermute(second, axis, pairs(1))
+    first = lax.ppermute(first, axis, pairs(0))
+    second = lax.ppermute(second, axis, pairs(1))
+    return first, second
 
 
 def is_odd(axis):
@@ -316,7 +318,8 @@
     count = float(2 * slots * rows * taps)
 
     def parts(zl_b, core_b, y_b):
-        slot = (y_b ^ y) + 4 * (zl_b ^ zl)
+        y_off, z_off = y_b ^ y, zl_b ^ zl
+        slot = (y_off >> 1) + 2 * (y_off & 1) + 4 * (z_off >> 1) + 8 * (z_off & 1)
         data = jnp.where(core_b == core, near_ref[slot], far_ref[slot]).astype(jnp.float32)
         return data[:, :width], data[0:1, width:] + data[1:2, width:]
 
@@ -341,8 +344,13 @@
     block_ref[...] = (values + wide(base - mean)) * inv_wide
 
 
-def last_kernel(fan_count, grad_ref, raw_ref, mean_ref, inv_ref, sums_ref, out_ref):
+def last_kernel(fan_count, x_count, own_ref, *refs):
+    *got_refs, raw_ref, mean_ref, inv_ref, sums_ref, out_ref = refs
     taps, _, ch = raw_ref.shape
+    steps = (lax.axis_index("gz") - lax.axis_index("gx") // CORES) % x_count
+    grad = own_ref[...]
+    for k, got_ref in enumerate(got_refs, 1):
+        grad = jnp.where(steps == k, got_ref[...], grad)
     sums = jnp.sum(sums_ref[...], axis=0)
     sum_grad, sum_cross, sum_square = sums[:, :ch], sums[:, ch : 2 * ch], sums[:, 2 * ch :]
     mean, inv = mean_ref[...], inv_ref[...]
@@ -356,7 +364,7 @@
     factor = inv * scale
     for t in range(taps):
         std = (raw_ref[t] - mean) * inv
-        out_ref[t] = factor * (grad_ref[:, t * ch : (t + 1) * ch] - mean_grad - std * mean_cross)
+        out_ref[t] = factor * (grad[:, t * ch : (t + 1) * ch] - mean_grad - std * mean_cross)
 
 
 def on_device(where, raw_weight, inputs, cotangent):
@@ -379,14 +387,14 @@
         (of((1, rows, width + ch), bf16), *both((nx, ny, ch)), *both((nx, ny, ch))),
         (raw, cotangent, inputs),
     )
-    held = [block, where.send(block, lambda s: dict(y=s["y"] ^ 1))]
+    held = [block, where.send(block, lambda s: dict(y=s["y"] ^ 2))]
     faces = call(height_kernel, both((nx + 2, nz + 2, ch)), (cotangent, *x_halo, *ends[2:]))
     y_halo = swapped(*faces, "gy")
     faces = call(width_kernel, both((nx + 2, ny, ch)), (*ends[:2], *x_halo))
     z_halo = swapped(*faces, "gz")
-    held.append(where.send(joined(held), lambda s: dict(y=s["y"] ^ 2)))
+    held.append(where.send(joined(held), lambda s: dict(y=s["y"] ^ 1)))
+    held.append(where.send(joined(held), lambda s: dict(zl=s["zl"] ^ 2)))
     held.append(where.send(joined(held), lambda s: dict(zl=s["zl"] ^ 1)))
-    held.append(where.send(joined(held), lambda s: dict(zl=s["zl"] ^ 2)))
 
     flops = 2 * nx * ny * nz * ch * width
     scratch = [pltpu.VMEM((nx + 2, ny + 2, nz, 3 * ch), bf16)]
@@ -414,7 +422,6 @@
         (held, far),
         flops=3_000_000_000,
     )
-    parts, inv_std = lax.optimization_barrier((parts, inv_std))
     copies = call(peers_kernel, of((where.zl * where.zh, rows, width), bf16), (parts,))
     parts = where.exchange(copies, ("core", "x", "y"), lambda s: (s["zh"], s["zl"]))
     input_grad = call(
@@ -428,10 +435,10 @@
     parts, input_grad = lax.optimization_barrier((parts, input_grad))
     everyone = CORES * where.x * where.gy
     block_grad, local = call(block_kernel, (of((rows, width), f32), of((everyone, 1, 3 * ch), f32)), (parts, block_std))
-    filter_grad = where.send(block_grad, lambda s: dict(x=s["zl"], zl=s["x"]))
+    passed = [where.send(block_grad, lambda s, k=k: dict(x=(s["x"] + k) % where.x)) for k in range(1, where.x)]
     sums = where.exchange(local, ("zl", "zh"), lambda s: (s["core"], s["x"], s["y"]))
 
-    grad = call(functools.partial(last_kernel, float(ch * taps)), of((taps, rows, ch), f32), (filter_grad, raw, mean_out, inv_std, sums))
+    grad = call(functools.partial(last_kernel, float(ch * taps), where.x), of((taps, rows, ch), f32), (block_grad, *passed, raw, mean_out, inv_std, sums))
     return (input_grad, jnp.transpose(grad, (1, 0, 2)))
 
 

time: 99.2 us -> 86.2 us (0.87)
  waiting for transfers between devices: 18.8 us -> 11.5 us
  blocking collectives: 21.6 us -> 15.4 us
    ppermute x7 -> x9, waiting for transfers between devices: 7.95 us -> 0.9 us  [send(): return lax.ppermute(array, AXES, pairs)]
    all_to_all x1, blocking collectives: 21.6 us -> 15.4 us  [exchange(): lax.all_to_all(array, AXES, 0, 0, tiled=True, axis_index_groups=groups)]
    all_to_all x2, starting transfers between devices: 18.2 us -> 19.2 us  [exchange(): lax.all_to_all(array, AXES, 0, 0, tiled=True, axis_index_groups=groups)]
    ppermute x7 -> x9, starting transfers between devices: 13 us -> 12.7 us  [send(): return lax.ppermute(array, AXES, pairs)]
  transfers between devices with their start and end apart: 17 -> 19, of which waited for: 6 -> 4; matrix products, arithmetic and copies ran while one was open for 0% -> 0% of each run, Pallas kernels for 11% -> 14%
where the time goes in v7:
time: 86.2 us; the launch traced here: 85.7 us
  starting transfers between devices  41.8 us (48%)
  blocking collectives  15.4 us (18%)
  Pallas kernels  12.9 us (15%)
  waiting for transfers between devices  11.5 us (13%)
  local copies, waits for them, and re-layouts  2.91 us (3%)
  between operations  0.87 us (1%)
    all_to_all x2, starting transfers between devices, exchange(): lax.all_to_all(array, AXES, 0, 0, tiled=True, axis_index_groups=groups)  19.2 us
    all_to_all x1, blocking collectives, exchange(): lax.all_to_all(array, AXES, 0, 0, tiled=True, axis_index_groups=groups)  15.4 us
    pallas_call x14, Pallas kernels, call(): pl.pallas_call(kernel, out_shape=out_shape, in_specs=[pl.BlockSpec(memory...  12.9 us
    ppermute x9, starting transfers between devices, send(): return lax.ppermute(array, AXES, pairs)  12.7 us
    all_to_all x2, waiting for transfers between devices, exchange(): lax.all_to_all(array, AXES, 0, 0, tiled=True, axis_index_groups=groups)  9.02 us
    ppermute x4, starting transfers between devices, swapped(): second = lax.ppermute(second, axis, pairs(1))  5.4 us
    ppermute x4, starting transfers between devices, swapped(): first = lax.ppermute(first, axis, pairs(0))  4.55 us
    unnamed x12, local copies, waits for them, and re-layouts  2.91 us
  transfers between devices with their start and end apart: 19, of which 4 were waited for; matrix products, arithmetic and copies ran while one was open for 0% of the time, Pallas kernels for 14%

profile of v7, /device:TPU:1, one launch (start us, length us, event | category | flops | bytes accessed | tf_op | source)
XLA Modules:
  0.0 85.7 jit_solution(4551854186750709769)
XLA Ops:
  0.6 0.0 copy-start
  0.6 1.0 %copy-done = bf16[8,16,16,128]{3,2,1,0:T(8,128)(2,1)S(1)} copy-done((bf16[8,16,16,128]{3,2,1,0:T(8,128)(2,1)S(1)}, bf16[8,16,16,128]{3,2,1,0:T(8,128)(2,1)}, u32[]{:S(2)}) %copy-start) | copy-done | bytes 524312
  1.7 1.0 %copy-done.2 = bf16[8,16,16,128]{3,2,1,0:T(8,128)(2,1)S(1)} copy-done((bf16[8,16,16,128]{3,2,1,0:T(8,128)(2,1)S(1)}, bf16[8,16,16,128]{3,2,1,0:T(8,128)(2,1)}, u32[]{:S(2)}) %copy-start.2) | copy-done | bytes 524312
  2.7 0.8 copy-done.4
  3.5 0.2 shard_map.51
  3.8 0.0 copy-start.3
  3.8 3.8 %collective-permute-start.9 = (bf16[1,4,3584]{2,1,0:T(4,128)(2,1)S(1)}, bf16[1,4,3584]{2,1,0:T(4,128)(2,1)S(1)}, u32[]{:S(2)}, u32[]{:S(2)}) collective-permute-start(bf16[1,4,3584]{2,1,0:T(4,128)(2,1)S(1)} %get-tuple-element.43.refs_0_), channel_id=1, source_target_pairs={{0,16},{1,17},{2,18},{3,19},{4,20},{5,21},{6,22},{7,23},{8,24},{9,... | collective-permute-start | bytes 86024 | tf_op jit(solution)/shard_map/ppermute | solution.py:63
  7.6 1.0 %collective-permute-start = (bf16[1,16,16,128]{3,2,1,0:T(8,128)(2,1)S(1)}, bf16[1,16,16,128]{3,2,1,0:T(8,128)(2,1)S(1)}, u32[]{:S(2)}, u32[]{:S(2)}) collective-permute-start(bf16[1,16,16,128]{3,2,1,0:T(8,128)(2,1)S(1)} %get-tuple-element.27), channel_id=1, source_target_pairs={{0,32},{64,96},{128,160},{192,224},{32,0},{96,64},{160,128},{224,1... | collective-permute-start | bytes 196616 | tf_op jit(solution)/shard_map/ppermute | solution.py:80
  8.6 3.4 %collective-permute-start.1 = (bf16[1,16,16,128]{3,2,1,0:T(8,128)(2,1)S(1)}, bf16[1,16,16,128]{3,2,1,0:T(8,128)(2,1)S(1)}, u32[]{:S(2)}, u32[]{:S(2)}) collective-permute-start(bf16[1,16,16,128]{3,2,1,0:T(8,128)(2,1)S(1)} %get-tuple-element.28), channel_id=1, source_target_pairs={{32,64},{96,128},{160,192},{64,32},{128,96},{192,160},{33,65},{97,... | collective-permute-start | bytes 196616 | tf_op jit(solution)/shard_map/ppermute | solution.py:81
  12.1 0.0 collective-permute-done.9.refs_1_
  12.2 0.5 collective-permute-start.10
  12.6 0.0 collective-permute-done.xa_ref
  12.6 1.6 %collective-permute-done.1.xb_ref = bf16[1,16,16,128]{3,2,1,0:T(8,128)(2,1)S(1)} collective-permute-done((bf16[1,16,16,128]{3,2,1,0:T(8,128)(2,1)S(1)}, bf16[1,16,16,128]{3,2,1,0:T(8,128)(2,1)S(1)}, u32[]{:S(2)}, u32[]{:S(2)}) %collective-permute-start.1) | collective-permute-done | bytes 65568 | tf_op jit(solution)/shard_map/ppermute | solution.py:81
  14.3 0.5 collective-permute-start.2
  14.7 0.7 collective-permute-start.3
  15.4 0.0 copy-start.1
  15.4 0.1 shard_map.54
  15.5 1.3 %collective-permute-start.4 = (bf16[10,16,128]{2,1,0:T(8,128)(2,1)S(1)}, bf16[10,16,128]{2,1,0:T(8,128)(2,1)S(1)}, u32[]{:S(2)}, u32[]{:S(2)}) collective-permute-start(bf16[10,16,128]{2,1,0:T(8,128)(2,1)S(1)} %get-tuple-element.37), channel_id=1, source_target_pairs={{0,1},{2,3},{4,5},{6,7},{1,0},{3,2},{5,4},{7,6},{8,9},{10,11},{12,... | collective-permute-start | bytes 122888 | tf_op jit(solution)/shard_map/ppermute | solution.py:80
  16.8 0.7 collective-permute-start.5
  17.5 0.0 collective-permute-done.10.refs_2_
  17.5 0.1 pad_maximum_fusion.1
  17.6 3.1 %collective-permute-start.11 = (bf16[4,4,3584]{2,1,0:T(4,128)(2,1)S(1)}, bf16[4,4,3584]{2,1,0:T(4,128)(2,1)S(1)}, u32[]{:S(2)}, u32[]{:S(2)}) collective-permute-start(bf16[4,4,3584]{2,1,0:T(4,128)(2,1)S(1)} %pad_maximum_fusion.1), channel_id=1, source_target_pairs={{0,128},{1,129},{2,130},{3,131},{4,132},{5,133},{6,134},{7,135},{8... | collective-permute-start | bytes 344072 | tf_op jit(solution)/shard_map/ppermute | solution.py:63
  20.7 3.2 %shard_map.53 = (f32[128,3456]{1,0:T(8,128)S(1)}, bf16[2,3,128,128]{3,2,1,0:T(8,128)(2,1)S(1)}) custom-call(bf16[8,16,16,128]{3,2,1,0:T(8,128)(2,1)S(1)} %copy-done.3, bf16[1,16,16,128]{3,2,1,0:T(8,128)(2,1)S(1)} %collective-permute-done.xa_ref, bf16[1,16,16,128]{3,2,1,0:T(8,128)(2,1)S(1)} %collective-permute-done.1.xb_ref, ...), custom_call_target="tpu_custom_call" | custom-call | flops 3623878656 | bytes 1000000 | tf_op jit(solution)/shard_map/pallas_call | solution.py:22
  23.9 0.0 collective-permute-done.4.za_ref
  23.9 0.3 shard_map.55
  24.2 1.0 %collective-permute-start.6 = (bf16[64,3456]{1,0:T(8,128)(2,1)S(1)}, bf16[64,3456]{1,0:T(8,128)(2,1)S(1)}, u32[]{:S(2)}, u32[]{:S(2)}) collective-permute-start(bf16[64,3456]{1,0:T(8,128)(2,1)S(1)} %get-tuple-element.40), channel_id=1, source_target_pairs={{0,32},{1,33},{2,34},{3,35},{4,36},{5,37},{6,38},{7,39},{8,40},{9,... | collective-permute-start | bytes 1327112 | tf_op jit(solution)/shard_map/ppermute | solution.py:63
  25.2 0.9 %collective-permute-done.11.refs_3_ = bf16[4,4,3584]{2,1,0:T(4,128)(2,1)S(1)} collective-permute-done((bf16[4,4,3584]{2,1,0:T(4,128)(2,1)S(1)}, bf16[4,4,3584]{2,1,0:T(4,128)(2,1)S(1)}, u32[]{:S(2)}, u32[]{:S(2)}) %collective-permute-start.11) | collective-permute-done | bytes 114720 | tf_op jit(solution)/shard_map/ppermute | solution.py:63
  26.1 0.2 pad_maximum_fusion
  26.2 0.8 collective-permute-start.12
  27.1 0.9 %shard_map.56 = bf16[16,4,3456]{2,1,0:T(4,128)(2,1)} custom-call(f32[64,3456]{1,0:T(8,128)S(1)} %get-tuple-element.39.keep_ref, bf16[64,3456]{1,0:T(8,128)(2,1)S(1)} %collective-permute-done.6.other_ref), custom_call_target="tpu_custom_call" | custom-call | flops 1000000000 | bytes 1000000 | tf_op jit(solution)/shard_map/pallas_call | solution.py:22
  28.0 15.6 %all-to-all-start = ((bf16[16,4,3456]{2,1,0:T(4,128)(2,1)}), bf16[16,4,3456]{2,1,0:T(4,128)(2,1)S(1)}, u32[]{:S(2)}, u32[]{:S(2)}) async-start(bf16[16,4,3456]{2,1,0:T(4,128)(2,1)} %shard_map.56), calls=%async_computation | async-start | bytes 884736 | tf_op jit(solution)/shard_map/all_to_all | solution.py:70
  43.5 0.0 collective-permute-done.12.refs_4_
  43.6 0.8 collective-permute-start.13
  44.4 1.7 %collective-permute-start.7 = (bf16[10,2,128]{2,1,0:T(2,128)(2,1)S(1)}, bf16[10,2,128]{2,1,0:T(2,128)(2,1)S(1)}, u32[]{:S(2)}, u32[]{:S(2)}) collective-permute-start(bf16[10,2,128]{2,1,0:T(2,128)(2,1)S(1)} %get-tuple-element.41), channel_id=1, source_target_pairs={{0,8},{16,24},{8,0},{24,16},{1,9},{17,25},{9,1},{25,17},{2,10},{18... | collective-permute-start | bytes 15368 | tf_op jit(solution)/shard_map/ppermute | solution.py:80
  46.1 0.6 collective-permute-start.8
  46.8 6.5 %all-to-all-done.parts_ref = bf16[16,4,3456]{2,1,0:T(4,128)(2,1)S(1)} async-done(((bf16[16,4,3456]{2,1,0:T(4,128)(2,1)}), bf16[16,4,3456]{2,1,0:T(4,128)(2,1)S(1)}, u32[]{:S(2)}, u32[]{:S(2)}) %all-to-all-start) | async-done | bytes 442400 | tf_op jit(solution)/shard_map/all_to_all | solution.py:70
  53.3 0.9 %shard_map.57 = bf16[8,4,3456]{2,1,0:T(4,128)(2,1)} custom-call(bf16[16,4,3456]{2,1,0:T(4,128)(2,1)S(1)} %all-to-all-done.parts_ref), custom_call_target="tpu_custom_call" | custom-call | flops 1000000000 | bytes 1000000 | tf_op jit(solution)/shard_map/pallas_call | solution.py:22
  54.1 3.6 %all-to-all-start.1 = ((bf16[8,4,3456]{2,1,0:T(4,128)(2,1)}), bf16[8,4,3456]{2,1,0:T(4,128)(2,1)S(1)}, u32[]{:S(2)}, u32[]{:S(2)}) async-start(bf16[8,4,3456]{2,1,0:T(4,128)(2,1)} %shard_map.57), calls=%async_computation.1 | async-start | bytes 442368 | tf_op jit(solution)/shard_map/all_to_all | solution.py:70
  57.7 0.0 collective-permute-done.13.far_ref
  57.7 1.1 %shard_map.60 = (bf16[128,3456]{1,0:T(8,128)(2,1)S(1)}, f32[1,128]{1,0:T(1,128)S(1)}, f32[1,128]{1,0:T(1,128)S(1)}, f32[4,3456]{1,0:T(4,128)S(1)}) custom-call(bf16[16,4,3584]{2,1,0:T(4,128)(2,1)S(1)} %shard_map.59.near_ref, bf16[16,4,3584]{2,1,0:T(4,128)(2,1)S(1)} %collective-permute-done.13.far_ref), custom_call_target="tpu_custom_call" | custom-call | flops 3000000000 | bytes 1000000 | tf_op jit(solution)/shard_map/pallas_call | solution.py:22
  58.9 5.2 %shard_map.61 = bf16[8,16,16,128]{3,2,1,0:T(8,128)(2,1)} custom-call(bf16[8,16,16,128]{3,2,1,0:T(8,128)(2,1)S(1)} %copy-done.3, bf16[1,16,16,128]{3,2,1,0:T(8,128)(2,1)S(1)} %collective-permute-done.xa_ref, bf16[1,16,16,128]{3,2,1,0:T(8,128)(2,1)S(1)} %collective-permute-done.1.xb_ref, bf16[10,18,128]{2,1,0:T(8,128)(2,1)S(1)} %collective-permute-done.2.ya_ref, ...), custom_call_target="tpu_custom_call" | custom-call | flops 3623878656 | bytes 1000000 | tf_op jit(solution)/shard_map/pallas_call | solution.py:22
  64.1 2.5 %all-to-all-done.1.parts_ref = bf16[8,4,3456]{2,1,0:T(4,128)(2,1)S(1)} async-done(((bf16[8,4,3456]{2,1,0:T(4,128)(2,1)}), bf16[8,4,3456]{2,1,0:T(4,128)(2,1)S(1)}, u32[]{:S(2)}, u32[]{:S(2)}) %all-to-all-start.1) | async-done | bytes 221216 | tf_op jit(solution)/shard_map/all_to_all | solution.py:70
  66.6 0.1 shard_map.62
  66.8 0.1 collective-permute-start.14
  66.8 1.7 %collective-permute-start.15 = (f32[4,3456]{1,0:T(4,128)S(1)}, f32[4,3456]{1,0:T(4,128)S(1)}, u32[]{:S(2)}, u32[]{:S(2)}) collective-permute-start(f32[4,3456]{1,0:T(4,128)S(1)} %get-tuple-element.48.own_ref), channel_id=1, source_target_pairs={{0,2},{1,3},{2,0},{3,1},{4,6},{5,7},{6,4},{7,5},{8,10},{9,11},{10,... | collective-permute-start | bytes 165896 | tf_op jit(solution)/shard_map/ppermute | solution.py:63
  68.5 1.0 %collective-permute-start.16 = (f32[4,3456]{1,0:T(4,128)S(1)}, f32[4,3456]{1,0:T(4,128)S(1)}, u32[]{:S(2)}, u32[]{:S(2)}) collective-permute-start(f32[4,3456]{1,0:T(4,128)S(1)} %get-tuple-element.48.own_ref), channel_id=1, source_target_pairs={{0,3},{1,0},{2,1},{3,2},{4,7},{5,4},{6,5},{7,6},{8,11},{9,8},{10,9... | collective-permute-start | bytes 165896 | tf_op jit(solution)/shard_map/ppermute | solution.py:63
  69.5 15.4 %all_to_all.15.refs_6_ = f32[32,1,384]{2,1,0:T(1,128)S(1)} all-to-all(f32[32,1,384]{2,1,0:T(1,128)S(1)} %get-tuple-element.51), channel_id=1, replica_groups={{0,8,16,24,1,9,17,25,2,10,18,26,3,11,19,27,32,40,48,56,33,41,49,57,34,4..., dimensions={0} | all-to-all | bytes 98304 | tf_op jit(solution)/shard_map/all_to_all | solution.py:70
  84.9 0.8 shard_map.63
  (20 shorter events, 0.2 us)
Async XLA Ops:
  0.6 1.0 %copy-start = (bf16[8,16,16,128]{3,2,1,0:T(8,128)(2,1)S(1)}, bf16[8,16,16,128]{3,2,1,0:T(8,128)(2,1)}, u32[]{:S(2)}) copy-start(bf16[8,16,16,128]{3,2,1,0:T(8,128)(2,1)} %in_ref.3) | copy-start | bytes 1572868
  1.7 1.0 %copy-start.2 = (bf16[8,16,16,128]{3,2,1,0:T(8,128)(2,1)S(1)}, bf16[8,16,16,128]{3,2,1,0:T(8,128)(2,1)}, u32[]{:S(2)}) copy-start(bf16[8,16,16,128]{3,2,1,0:T(8,128)(2,1)} %mid_ref.9) | copy-start | bytes 1572868
  2.7 0.8 copy-start.4
  3.8 10.5 %copy-start.3 = (bf16[8,16,16,128]{3,2,1,0:T(8,128)(2,1)S(1)}, bf16[8,16,16,128]{3,2,1,0:T(8,128)(2,1)}, u32[]{:S(2)}) copy-start(bf16[8,16,16,128]{3,2,1,0:T(8,128)(2,1)} %mid_ref.9) | copy-start | bytes 1572868
  3.8 8.3 %collective-permute-start.9 = (bf16[1,4,3584]{2,1,0:T(4,128)(2,1)S(1)}, bf16[1,4,3584]{2,1,0:T(4,128)(2,1)S(1)}, u32[]{:S(2)}, u32[]{:S(2)}) collective-permute-start(bf16[1,4,3584]{2,1,0:T(4,128)(2,1)S(1)} %get-tuple-element.43.refs_0_), channel_id=1, source_target_pairs={{0,16},{1,17},{2,18},{3,19},{4,20},{5,21},{6,22},{7,23},{8,24},{9,... | collective-permute-start | bytes 86024 | tf_op jit(solution)/shard_map/ppermute | solution.py:63
  7.6 5.0 %collective-permute-start = (bf16[1,16,16,128]{3,2,1,0:T(8,128)(2,1)S(1)}, bf16[1,16,16,128]{3,2,1,0:T(8,128)(2,1)S(1)}, u32[]{:S(2)}, u32[]{:S(2)}) collective-permute-start(bf16[1,16,16,128]{3,2,1,0:T(8,128)(2,1)S(1)} %get-tuple-element.27), channel_id=1, source_target_pairs={{0,32},{64,96},{128,160},{192,224},{32,0},{96,64},{160,128},{224,1... | collective-permute-start | bytes 196616 | tf_op jit(solution)/shard_map/ppermute | solution.py:80
  8.6 5.6 %collective-permute-start.1 = (bf16[1,16,16,128]{3,2,1,0:T(8,128)(2,1)S(1)}, bf16[1,16,16,128]{3,2,1,0:T(8,128)(2,1)S(1)}, u32[]{:S(2)}, u32[]{:S(2)}) collective-permute-start(bf16[1,16,16,128]{3,2,1,0:T(8,128)(2,1)S(1)} %get-tuple-element.28), channel_id=1, source_target_pairs={{32,64},{96,128},{160,192},{64,32},{128,96},{192,160},{33,65},{97,... | collective-permute-start | bytes 196616 | tf_op jit(solution)/shard_map/ppermute | solution.py:81
  12.2 5.3 %collective-permute-start.10 = (bf16[2,4,3584]{2,1,0:T(4,128)(2,1)S(1)}, bf16[2,4,3584]{2,1,0:T(4,128)(2,1)S(1)}, u32[]{:S(2)}, u32[]{:S(2)}) collective-permute-start(bf16[2,4,3584]{2,1,0:T(4,128)(2,1)S(1)} %pad_maximum_fusion.2), channel_id=1, source_target_pairs={{0,8},{1,9},{2,10},{3,11},{4,12},{5,13},{6,14},{7,15},{8,0},{9,1},... | collective-permute-start | bytes 172040 | tf_op jit(solution)/shard_map/ppermute | solution.py:63
  14.3 6.4 %collective-permute-start.2 = (bf16[10,18,128]{2,1,0:T(8,128)(2,1)S(1)}, bf16[10,18,128]{2,1,0:T(8,128)(2,1)S(1)}, u32[]{:S(2)}, u32[]{:S(2)}) collective-permute-start(bf16[10,18,128]{2,1,0:T(8,128)(2,1)S(1)} %get-tuple-element.31), channel_id=1, source_target_pairs={{0,8},{16,24},{8,0},{24,16},{1,9},{17,25},{9,1},{25,17},{2,10},{18... | collective-permute-start | bytes 138248 | tf_op jit(solution)/shard_map/ppermute | solution.py:80
  14.7 5.9 %collective-permute-start.3 = (bf16[10,18,128]{2,1,0:T(8,128)(2,1)S(1)}, bf16[10,18,128]{2,1,0:T(8,128)(2,1)S(1)}, u32[]{:S(2)}, u32[]{:S(2)}) collective-permute-start(bf16[10,18,128]{2,1,0:T(8,128)(2,1)S(1)} %get-tuple-element.32), channel_id=1, source_target_pairs={{8,16},{16,8},{9,17},{17,9},{10,18},{18,10},{11,19},{19,11},{12,20... | collective-permute-start | bytes 138248 | tf_op jit(solution)/shard_map/ppermute | solution.py:81
  15.4 5.3 %copy-start.1 = (bf16[8,16,16,128]{3,2,1,0:T(8,128)(2,1)S(1)}, bf16[8,16,16,128]{3,2,1,0:T(8,128)(2,1)}, u32[]{:S(2)}) copy-start(bf16[8,16,16,128]{3,2,1,0:T(8,128)(2,1)} %in_ref.3) | copy-start | bytes 1572868
  15.5 8.4 %collective-permute-start.4 = (bf16[10,16,128]{2,1,0:T(8,128)(2,1)S(1)}, bf16[10,16,128]{2,1,0:T(8,128)(2,1)S(1)}, u32[]{:S(2)}, u32[]{:S(2)}) collective-permute-start(bf16[10,16,128]{2,1,0:T(8,128)(2,1)S(1)} %get-tuple-element.37), channel_id=1, source_target_pairs={{0,1},{2,3},{4,5},{6,7},{1,0},{3,2},{5,4},{7,6},{8,9},{10,11},{12,... | collective-permute-start | bytes 122888 | tf_op jit(solution)/shard_map/ppermute | solution.py:80
  16.8 7.1 %collective-permute-start.5 = (bf16[10,16,128]{2,1,0:T(8,128)(2,1)S(1)}, bf16[10,16,128]{2,1,0:T(8,128)(2,1)S(1)}, u32[]{:S(2)}, u32[]{:S(2)}) collective-permute-start(bf16[10,16,128]{2,1,0:T(8,128)(2,1)S(1)} %get-tuple-element.38), channel_id=1, source_target_pairs={{1,2},{3,4},{5,6},{2,1},{4,3},{6,5},{9,10},{11,12},{13,14},{10,9},... | collective-permute-start | bytes 122888 | tf_op jit(solution)/shard_map/ppermute | solution.py:81
  17.6 8.5 %collective-permute-start.11 = (bf16[4,4,3584]{2,1,0:T(4,128)(2,1)S(1)}, bf16[4,4,3584]{2,1,0:T(4,128)(2,1)S(1)}, u32[]{:S(2)}, u32[]{:S(2)}) collective-permute-start(bf16[4,4,3584]{2,1,0:T(4,128)(2,1)S(1)} %pad_maximum_fusion.1), channel_id=1, source_target_pairs={{0,128},{1,129},{2,130},{3,131},{4,132},{5,133},{6,134},{7,135},{8... | collective-permute-start | bytes 344072 | tf_op jit(solution)/shard_map/ppermute | solution.py:63
  24.2 2.9 %collective-permute-start.6 = (bf16[64,3456]{1,0:T(8,128)(2,1)S(1)}, bf16[64,3456]{1,0:T(8,128)(2,1)S(1)}, u32[]{:S(2)}, u32[]{:S(2)}) collective-permute-start(bf16[64,3456]{1,0:T(8,128)(2,1)S(1)} %get-tuple-element.40), channel_id=1, source_target_pairs={{0,32},{1,33},{2,34},{3,35},{4,36},{5,37},{6,38},{7,39},{8,40},{9,... | collective-permute-start | bytes 1327112 | tf_op jit(solution)/shard_map/ppermute | solution.py:63
  26.2 17.3 %collective-permute-start.12 = (bf16[8,4,3584]{2,1,0:T(4,128)(2,1)S(1)}, bf16[8,4,3584]{2,1,0:T(4,128)(2,1)S(1)}, u32[]{:S(2)}, u32[]{:S(2)}) collective-permute-start(bf16[8,4,3584]{2,1,0:T(4,128)(2,1)S(1)} %pad_maximum_fusion), channel_id=1, source_target_pairs={{0,64},{1,65},{2,66},{3,67},{4,68},{5,69},{6,70},{7,71},{8,72},{9,... | collective-permute-start | bytes 688136 | tf_op jit(solution)/shard_map/ppermute | solution.py:63
  28.0 25.3 %all-to-all-start = ((bf16[16,4,3456]{2,1,0:T(4,128)(2,1)}), bf16[16,4,3456]{2,1,0:T(4,128)(2,1)S(1)}, u32[]{:S(2)}, u32[]{:S(2)}) async-start(bf16[16,4,3456]{2,1,0:T(4,128)(2,1)} %shard_map.56), calls=%async_computation | async-start | bytes 884736 | tf_op jit(solution)/shard_map/all_to_all | solution.py:70
  43.6 14.1 %collective-permute-start.13 = (bf16[16,4,3584]{2,1,0:T(4,128)(2,1)S(1)}, bf16[16,4,3584]{2,1,0:T(4,128)(2,1)S(1)}, u32[]{:S(2)}, u32[]{:S(2)}) collective-permute-start(bf16[16,4,3584]{2,1,0:T(4,128)(2,1)S(1)} %shard_map.59.near_ref), channel_id=1, source_target_pairs={{0,32},{1,33},{2,34},{3,35},{4,36},{5,37},{6,38},{7,39},{8,40},{9,... | collective-permute-start | bytes 1376264 | tf_op jit(solution)/shard_map/ppermute | solution.py:63
  44.4 14.4 %collective-permute-start.7 = (bf16[10,2,128]{2,1,0:T(2,128)(2,1)S(1)}, bf16[10,2,128]{2,1,0:T(2,128)(2,1)S(1)}, u32[]{:S(2)}, u32[]{:S(2)}) collective-permute-start(bf16[10,2,128]{2,1,0:T(2,128)(2,1)S(1)} %get-tuple-element.41), channel_id=1, source_target_pairs={{0,8},{16,24},{8,0},{24,16},{1,9},{17,25},{9,1},{25,17},{2,10},{18... | collective-permute-start | bytes 15368 | tf_op jit(solution)/shard_map/ppermute | solution.py:80
  46.1 12.7 %collective-permute-start.8 = (bf16[10,2,128]{2,1,0:T(2,128)(2,1)S(1)}, bf16[10,2,128]{2,1,0:T(2,128)(2,1)S(1)}, u32[]{:S(2)}, u32[]{:S(2)}) collective-permute-start(bf16[10,2,128]{2,1,0:T(2,128)(2,1)S(1)} %get-tuple-element.42), channel_id=1, source_target_pairs={{8,16},{16,8},{9,17},{17,9},{10,18},{18,10},{11,19},{19,11},{12,20... | collective-permute-start | bytes 15368 | tf_op jit(solution)/shard_map/ppermute | solution.py:81
  54.1 12.5 %all-to-all-start.1 = ((bf16[8,4,3456]{2,1,0:T(4,128)(2,1)}), bf16[8,4,3456]{2,1,0:T(4,128)(2,1)S(1)}, u32[]{:S(2)}, u32[]{:S(2)}) async-start(bf16[8,4,3456]{2,1,0:T(4,128)(2,1)} %shard_map.57), calls=%async_computation.1 | async-start | bytes 442368 | tf_op jit(solution)/shard_map/all_to_all | solution.py:70
  66.6 18.3 %copy-start.5 = (f32[4,27,128]{2,0,1:T(4,128)S(1)}, f32[4,27,128]{2,0,1:T(4,128)}, u32[]{:S(2)}) copy-start(f32[4,27,128]{2,0,1:T(4,128)} %param.3) | copy-start | bytes 165892
  66.8 18.1 %collective-permute-start.14 = (f32[4,3456]{1,0:T(4,128)S(1)}, f32[4,3456]{1,0:T(4,128)S(1)}, u32[]{:S(2)}, u32[]{:S(2)}) collective-permute-start(f32[4,3456]{1,0:T(4,128)S(1)} %get-tuple-element.48.own_ref), channel_id=1, source_target_pairs={{0,1},{1,2},{2,3},{3,0},{4,5},{5,6},{6,7},{7,4},{8,9},{9,10},{10,1... | collective-permute-start | bytes 165896 | tf_op jit(solution)/shard_map/ppermute | solution.py:63
  66.8 18.1 %collective-permute-start.15 = (f32[4,3456]{1,0:T(4,128)S(1)}, f32[4,3456]{1,0:T(4,128)S(1)}, u32[]{:S(2)}, u32[]{:S(2)}) collective-permute-start(f32[4,3456]{1,0:T(4,128)S(1)} %get-tuple-element.48.own_ref), channel_id=1, source_target_pairs={{0,2},{1,3},{2,0},{3,1},{4,6},{5,7},{6,4},{7,5},{8,10},{9,11},{10,... | collective-permute-start | bytes 165896 | tf_op jit(solution)/shard_map/ppermute | solution.py:63
  68.5 16.4 %collective-permute-start.16 = (f32[4,3456]{1,0:T(4,128)S(1)}, f32[4,3456]{1,0:T(4,128)S(1)}, u32[]{:S(2)}, u32[]{:S(2)}) collective-permute-start(f32[4,3456]{1,0:T(4,128)S(1)} %get-tuple-element.48.own_ref), channel_id=1, source_target_pairs={{0,3},{1,0},{2,1},{3,2},{4,7},{5,4},{6,5},{7,6},{8,11},{9,8},{10,9... | collective-permute-start | bytes 165896 | tf_op jit(solution)/shard_map/ppermute | solution.py:63

commit v8 on v7

--- a/solution.py
+++ b/solution.py
@@ -280,13 +280,26 @@
         out_ref[k] = total
 
 
-def block_kernel(parts_ref, std_ref, grad_ref, sums_ref):
-    ch = sums_ref.shape[2] // 3
+def block_kernel(parts_ref, std_ref, out_ref):
+    rows, width = std_ref.shape
+    ch = (out_ref.shape[1] - width) // 3
     total = jnp.sum(parts_ref[...].astype(jnp.float32), axis=0)
-    grad_ref[...] = total
-    three = jnp.concatenate([fold(total, ch), fold(total * std_ref[...], ch), fold(total * total, ch)], axis=1)
-    for k in range(sums_ref.shape[0]):
-        sums_ref[k] = three
+    out_ref[:, :width] = total
+    sums = jnp.concatenate([fold(total, ch), fold(total * std_ref[...], ch), fold(total * total, ch)], axis=1)
+    place = lax.broadcasted_iota(jnp.int32, (rows, 3 * ch), 0)
+    out_ref[:, width:] = jnp.where(place == 0, sums, 0.0)
+
+
+def around_kernel(axis, count, own_ref, *refs):
+    *got_refs, out_ref, held_ref = refs
+    here = lax.axis_index(axis) % count
+    size = out_ref.shape[1]
+    for k, ref in enumerate((own_ref, *got_refs)):
+        held_ref[(here + count - k) % count] = ref[0:1, ref.shape[1] - size :]
+    total = held_ref[0]
+    for k in range(1, count):
+        total = total + held_ref[k]
+    out_ref[...] = total
 
 
 def input_kernel(mid_ref, xa_ref, xb_ref, ya_ref, yb_ref, za_ref, zb_ref, ca_ref, cb_ref, std_ref, out_ref, taps_ref):
@@ -345,13 +358,13 @@
 
 
 def last_kernel(fan_count, x_count, own_ref, *refs):
-    *got_refs, raw_ref, mean_ref, inv_ref, sums_ref, out_ref = refs
+    *got_refs, raw_ref, mean_ref, inv_ref, sums_ref, others_ref, out_ref = refs
     taps, _, ch = raw_ref.shape
     steps = (lax.axis_index("gz") - lax.axis_index("gx") // CORES) % x_count
-    grad = own_ref[...]
+    grad = own_ref[:, : taps * ch]
     for k, got_ref in enumerate(got_refs, 1):
-        grad = jnp.where(steps == k, got_ref[...], grad)
-    sums = jnp.sum(sums_ref[...], axis=0)
+        grad = jnp.where(steps == k, got_ref[:, : taps * ch], grad)
+    sums = sums_ref[...] + others_ref[...]
     sum_grad, sum_cross, sum_square = sums[:, :ch], sums[:, ch : 2 * ch], sums[:, 2 * ch :]
     mean, inv = mean_ref[...], inv_ref[...]
     mean_grad = sum_grad / fan_count
@@ -433,12 +446,23 @@
         scratch=scratch,
     )
     parts, input_grad = lax.optimization_barrier((parts, input_grad))
-    everyone = CORES * where.x * where.gy
-    block_grad, local = call(block_kernel, (of((rows, width), f32), of((everyone, 1, 3 * ch), f32)), (parts, block_std))
+    block_grad = call(block_kernel, of((rows, width + 3 * ch), f32), (parts, block_std))
     passed = [where.send(block_grad, lambda s, k=k: dict(x=(s["x"] + k) % where.x)) for k in range(1, where.x)]
-    sums = where.exchange(local, ("zl", "zh"), lambda s: (s["core"], s["x"], s["y"]))
-
-    grad = call(functools.partial(last_kernel, float(ch * taps), where.x), of((taps, rows, ch), f32), (block_grad, *passed, raw, mean_out, inv_std, sums))
+
+    def around(axis, count, arrays):
+        kernel = functools.partial(around_kernel, axis, count)
+        scratch = [pltpu.VMEM((count, 1, 3 * ch), f32)]
+        return call(kernel, of((1, 3 * ch), f32), arrays, scratch=scratch)
+
+    sums = around("gz", where.x, (block_grad, *passed))
+    rest = [where.send(sums, lambda s, k=k: dict(y=(s["y"] + k) % where.gy)) for k in range(1, where.gy)]
+    sums = around("gy", where.gy, (sums, *rest))
+    others = where.send(sums, lambda s: dict(core=1 - s["core"]))
+    grad = call(
+        functools.partial(last_kernel, float(ch * taps), where.x),
+        of((taps, rows, ch), f32),
+        (block_grad, *passed, raw, mean_out, inv_std, sums, others),
+    )
     return (input_grad, jnp.transpose(grad, (1, 0, 2)))
 
 

time: 86.2 us -> 84.7 us (0.983)
  blocking collectives: 15.4 us -> 0 us
  starting transfers between devices: 41.8 us -> 50.6 us
  waiting for transfers between devices: 11.5 us -> 16.6 us
    all_to_all x1 -> x0, blocking collectives: 15.4 us -> none  [exchange(): lax.all_to_all(array, AXES, 0, 0, tiled=True, axis_index_groups=groups)]
    ppermute x9 -> x13, starting transfers between devices: 12.7 us -> 21.5 us  [send(): return lax.ppermute(array, AXES, pairs)]
    ppermute x9 -> x13, waiting for transfers between devices: 0.9 us -> 6 us  [send(): return lax.ppermute(array, AXES, pairs)]
    pallas_call x14 -> x16, Pallas kernels: 12.9 us -> 12.9 us  [call(): pl.pallas_call(kernel, out_shape=out_shape, in_specs=[pl.BlockSpec(memory...]
  transfers between devices with their start and end apart: 19 -> 23, of which waited for: 4 -> 9; matrix products, arithmetic and copies ran while one was open for 0% -> 0% of each run, Pallas kernels for 14% -> 14%
where the time goes in v8:
time: 84.7 us; the launch traced here: 84.1 us
  starting transfers between devices  50.6 us (60%)
  waiting for transfers between devices  16.6 us (20%)
  Pallas kernels  12.9 us (15%)
  local copies, waits for them, and re-layouts  2.91 us (3%)
  between operations  0.87 us (1%)
    ppermute x13, starting transfers between devices, send(): return lax.ppermute(array, AXES, pairs)  21.5 us
    all_to_all x2, starting transfers between devices, exchange(): lax.all_to_all(array, AXES, 0, 0, tiled=True, axis_index_groups=groups)  19.2 us
    pallas_call x16, Pallas kernels, call(): pl.pallas_call(kernel, out_shape=out_shape, in_specs=[pl.BlockSpec(memory...  12.9 us
    all_to_all x2, waiting for transfers between devices, exchange(): lax.all_to_all(array, AXES, 0, 0, tiled=True, axis_index_groups=groups)  9.02 us
    ppermute x13, waiting for transfers between devices, send(): return lax.ppermute(array, AXES, pairs)  6 us
    ppermute x4, starting transfers between devices, swapped(): second = lax.ppermute(second, axis, pairs(1))  5.4 us
    ppermute x4, starting transfers between devices, swapped(): first = lax.ppermute(first, axis, pairs(0))  4.55 us
    unnamed x12, local copies, waits for them, and re-layouts  2.91 us
  transfers between devices with their start and end apart: 23, of which 9 were waited for; matrix products, arithmetic and copies ran while one was open for 0% of the time, Pallas kernels for 14%

profile of v8, /device:TPU:1, one launch (start us, length us, event | category | flops | bytes accessed | tf_op | source)
XLA Modules:
  0.0 84.1 jit_solution(16860469006357938977)
XLA Ops:
  0.6 0.0 copy-start
  0.6 1.0 %copy-done = bf16[8,16,16,128]{3,2,1,0:T(8,128)(2,1)S(1)} copy-done((bf16[8,16,16,128]{3,2,1,0:T(8,128)(2,1)S(1)}, bf16[8,16,16,128]{3,2,1,0:T(8,128)(2,1)}, u32[]{:S(2)}) %copy-start) | copy-done | bytes 524312
  1.7 1.0 %copy-done.2 = bf16[8,16,16,128]{3,2,1,0:T(8,128)(2,1)S(1)} copy-done((bf16[8,16,16,128]{3,2,1,0:T(8,128)(2,1)S(1)}, bf16[8,16,16,128]{3,2,1,0:T(8,128)(2,1)}, u32[]{:S(2)}) %copy-start.2) | copy-done | bytes 524312
  2.7 0.8 copy-done.4
  3.5 0.2 shard_map.51
  3.8 3.8 %collective-permute-start.9 = (bf16[1,4,3584]{2,1,0:T(4,128)(2,1)S(1)}, bf16[1,4,3584]{2,1,0:T(4,128)(2,1)S(1)}, u32[]{:S(2)}, u32[]{:S(2)}) collective-permute-start(bf16[1,4,3584]{2,1,0:T(4,128)(2,1)S(1)} %get-tuple-element.41.refs_0_), channel_id=1, source_target_pairs={{0,16},{1,17},{2,18},{3,19},{4,20},{5,21},{6,22},{7,23},{8,24},{9,... | collective-permute-start | bytes 86024 | tf_op jit(solution)/shard_map/ppermute | solution.py:63
  7.6 1.0 %collective-permute-start = (bf16[1,16,16,128]{3,2,1,0:T(8,128)(2,1)S(1)}, bf16[1,16,16,128]{3,2,1,0:T(8,128)(2,1)S(1)}, u32[]{:S(2)}, u32[]{:S(2)}) collective-permute-start(bf16[1,16,16,128]{3,2,1,0:T(8,128)(2,1)S(1)} %get-tuple-element.25), channel_id=1, source_target_pairs={{0,32},{64,96},{128,160},{192,224},{32,0},{96,64},{160,128},{224,1... | collective-permute-start | bytes 196616 | tf_op jit(solution)/shard_map/ppermute | solution.py:80
  8.6 3.4 %collective-permute-start.1 = (bf16[1,16,16,128]{3,2,1,0:T(8,128)(2,1)S(1)}, bf16[1,16,16,128]{3,2,1,0:T(8,128)(2,1)S(1)}, u32[]{:S(2)}, u32[]{:S(2)}) collective-permute-start(bf16[1,16,16,128]{3,2,1,0:T(8,128)(2,1)S(1)} %get-tuple-element.26), channel_id=1, source_target_pairs={{32,64},{96,128},{160,192},{64,32},{128,96},{192,160},{33,65},{97,... | collective-permute-start | bytes 196616 | tf_op jit(solution)/shard_map/ppermute | solution.py:81
  12.2 0.5 collective-permute-start.10
  12.6 1.6 %collective-permute-done.1.xb_ref = bf16[1,16,16,128]{3,2,1,0:T(8,128)(2,1)S(1)} collective-permute-done((bf16[1,16,16,128]{3,2,1,0:T(8,128)(2,1)S(1)}, bf16[1,16,16,128]{3,2,1,0:T(8,128)(2,1)S(1)}, u32[]{:S(2)}, u32[]{:S(2)}) %collective-permute-start.1) | collective-permute-done | bytes 65568 | tf_op jit(solution)/shard_map/ppermute | solution.py:81
  14.3 0.5 collective-permute-start.2
  14.7 0.7 collective-permute-start.3
  15.4 0.1 shard_map.54
  15.5 1.3 %collective-permute-start.4 = (bf16[10,16,128]{2,1,0:T(8,128)(2,1)S(1)}, bf16[10,16,128]{2,1,0:T(8,128)(2,1)S(1)}, u32[]{:S(2)}, u32[]{:S(2)}) collective-permute-start(bf16[10,16,128]{2,1,0:T(8,128)(2,1)S(1)} %get-tuple-element.35), channel_id=1, source_target_pairs={{0,1},{2,3},{4,5},{6,7},{1,0},{3,2},{5,4},{7,6},{8,9},{10,11},{12,... | collective-permute-start | bytes 122888 | tf_op jit(solution)/shard_map/ppermute | solution.py:80
  16.8 0.7 collective-permute-start.5
  17.5 0.1 pad_maximum_fusion.1
  17.6 3.1 %collective-permute-start.11 = (bf16[4,4,3584]{2,1,0:T(4,128)(2,1)S(1)}, bf16[4,4,3584]{2,1,0:T(4,128)(2,1)S(1)}, u32[]{:S(2)}, u32[]{:S(2)}) collective-permute-start(bf16[4,4,3584]{2,1,0:T(4,128)(2,1)S(1)} %pad_maximum_fusion.1), channel_id=1, source_target_pairs={{0,128},{1,129},{2,130},{3,131},{4,132},{5,133},{6,134},{7,135},{8... | collective-permute-start | bytes 344072 | tf_op jit(solution)/shard_map/ppermute | solution.py:63
  20.7 3.2 %shard_map.53 = (f32[128,3456]{1,0:T(8,128)S(1)}, bf16[2,3,128,128]{3,2,1,0:T(8,128)(2,1)S(1)}) custom-call(bf16[8,16,16,128]{3,2,1,0:T(8,128)(2,1)S(1)} %copy-done.3, bf16[1,16,16,128]{3,2,1,0:T(8,128)(2,1)S(1)} %collective-permute-done.xa_ref, bf16[1,16,16,128]{3,2,1,0:T(8,128)(2,1)S(1)} %collective-permute-done.1.xb_ref, ...), custom_call_target="tpu_custom_call" | custom-call | flops 3623878656 | bytes 1000000 | tf_op jit(solution)/shard_map/pallas_call | solution.py:22
  23.9 0.3 shard_map.55
  24.2 1.0 %collective-permute-start.6 = (bf16[64,3456]{1,0:T(8,128)(2,1)S(1)}, bf16[64,3456]{1,0:T(8,128)(2,1)S(1)}, u32[]{:S(2)}, u32[]{:S(2)}) collective-permute-start(bf16[64,3456]{1,0:T(8,128)(2,1)S(1)} %get-tuple-element.38), channel_id=1, source_target_pairs={{0,32},{1,33},{2,34},{3,35},{4,36},{5,37},{6,38},{7,39},{8,40},{9,... | collective-permute-start | bytes 1327112 | tf_op jit(solution)/shard_map/ppermute | solution.py:63
  25.2 0.9 %collective-permute-done.11.refs_3_ = bf16[4,4,3584]{2,1,0:T(4,128)(2,1)S(1)} collective-permute-done((bf16[4,4,3584]{2,1,0:T(4,128)(2,1)S(1)}, bf16[4,4,3584]{2,1,0:T(4,128)(2,1)S(1)}, u32[]{:S(2)}, u32[]{:S(2)}) %collective-permute-start.11) | collective-permute-done | bytes 114720 | tf_op jit(solution)/shard_map/ppermute | solution.py:63
  26.1 0.2 pad_maximum_fusion
  26.2 0.8 %collective-permute-start.12 = (bf16[8,4,3584]{2,1,0:T(4,128)(2,1)S(1)}, bf16[8,4,3584]{2,1,0:T(4,128)(2,1)S(1)}, u32[]{:S(2)}, u32[]{:S(2)}) collective-permute-start(bf16[8,4,3584]{2,1,0:T(4,128)(2,1)S(1)} %pad_maximum_fusion), channel_id=1, source_target_pairs={{0,64},{1,65},{2,66},{3,67},{4,68},{5,69},{6,70},{7,71},{8,72},{9,... | collective-permute-start | bytes 688136 | tf_op jit(solution)/shard_map/ppermute | solution.py:63
  27.1 0.9 %shard_map.56 = bf16[16,4,3456]{2,1,0:T(4,128)(2,1)} custom-call(f32[64,3456]{1,0:T(8,128)S(1)} %get-tuple-element.37.keep_ref, bf16[64,3456]{1,0:T(8,128)(2,1)S(1)} %collective-permute-done.6.other_ref), custom_call_target="tpu_custom_call" | custom-call | flops 1000000000 | bytes 1000000 | tf_op jit(solution)/shard_map/pallas_call | solution.py:22
  28.0 15.6 %all-to-all-start = ((bf16[16,4,3456]{2,1,0:T(4,128)(2,1)}), bf16[16,4,3456]{2,1,0:T(4,128)(2,1)S(1)}, u32[]{:S(2)}, u32[]{:S(2)}) async-start(bf16[16,4,3456]{2,1,0:T(4,128)(2,1)} %shard_map.56), calls=%async_computation | async-start | bytes 884736 | tf_op jit(solution)/shard_map/all_to_all | solution.py:70
  43.6 0.8 collective-permute-start.13
  44.4 1.7 %collective-permute-start.7 = (bf16[10,2,128]{2,1,0:T(2,128)(2,1)S(1)}, bf16[10,2,128]{2,1,0:T(2,128)(2,1)S(1)}, u32[]{:S(2)}, u32[]{:S(2)}) collective-permute-start(bf16[10,2,128]{2,1,0:T(2,128)(2,1)S(1)} %get-tuple-element.39), channel_id=1, source_target_pairs={{0,8},{16,24},{8,0},{24,16},{1,9},{17,25},{9,1},{25,17},{2,10},{18... | collective-permute-start | bytes 15368 | tf_op jit(solution)/shard_map/ppermute | solution.py:80
  46.1 0.6 collective-permute-start.8
  46.8 6.5 %all-to-all-done.parts_ref = bf16[16,4,3456]{2,1,0:T(4,128)(2,1)S(1)} async-done(((bf16[16,4,3456]{2,1,0:T(4,128)(2,1)}), bf16[16,4,3456]{2,1,0:T(4,128)(2,1)S(1)}, u32[]{:S(2)}, u32[]{:S(2)}) %all-to-all-start) | async-done | bytes 442400 | tf_op jit(solution)/shard_map/all_to_all | solution.py:70
  53.3 0.9 %shard_map.57 = bf16[8,4,3456]{2,1,0:T(4,128)(2,1)} custom-call(bf16[16,4,3456]{2,1,0:T(4,128)(2,1)S(1)} %all-to-all-done.parts_ref), custom_call_target="tpu_custom_call" | custom-call | flops 1000000000 | bytes 1000000 | tf_op jit(solution)/shard_map/pallas_call | solution.py:22
  54.1 3.6 %all-to-all-start.1 = ((bf16[8,4,3456]{2,1,0:T(4,128)(2,1)}), bf16[8,4,3456]{2,1,0:T(4,128)(2,1)S(1)}, u32[]{:S(2)}, u32[]{:S(2)}) async-start(bf16[8,4,3456]{2,1,0:T(4,128)(2,1)} %shard_map.57), calls=%async_computation.1 | async-start | bytes 442368 | tf_op jit(solution)/shard_map/all_to_all | solution.py:70
  57.7 1.1 %shard_map.60 = (bf16[128,3456]{1,0:T(8,128)(2,1)S(1)}, f32[1,128]{1,0:T(1,128)S(1)}, f32[1,128]{1,0:T(1,128)S(1)}, f32[4,3456]{1,0:T(4,128)S(1)}) custom-call(bf16[16,4,3584]{2,1,0:T(4,128)(2,1)S(1)} %shard_map.59.near_ref, bf16[16,4,3584]{2,1,0:T(4,128)(2,1)S(1)} %collective-permute-done.13.far_ref), custom_call_target="tpu_custom_call" | custom-call | flops 3000000000 | bytes 1000000 | tf_op jit(solution)/shard_map/pallas_call | solution.py:22
  58.9 5.2 %shard_map.61 = bf16[8,16,16,128]{3,2,1,0:T(8,128)(2,1)} custom-call(bf16[8,16,16,128]{3,2,1,0:T(8,128)(2,1)S(1)} %copy-done.3, bf16[1,16,16,128]{3,2,1,0:T(8,128)(2,1)S(1)} %collective-permute-done.xa_ref, bf16[1,16,16,128]{3,2,1,0:T(8,128)(2,1)S(1)} %collective-permute-done.1.xb_ref, bf16[10,18,128]{2,1,0:T(8,128)(2,1)S(1)} %collective-permute-done.2.ya_ref, ...), custom_call_target="tpu_custom_call" | custom-call | flops 3623878656 | bytes 1000000 | tf_op jit(solution)/shard_map/pallas_call | solution.py:22
  64.1 2.5 %all-to-all-done.1.parts_ref = bf16[8,4,3456]{2,1,0:T(4,128)(2,1)S(1)} async-done(((bf16[8,4,3456]{2,1,0:T(4,128)(2,1)}), bf16[8,4,3456]{2,1,0:T(4,128)(2,1)S(1)}, u32[]{:S(2)}, u32[]{:S(2)}) %all-to-all-start.1) | async-done | bytes 221216 | tf_op jit(solution)/shard_map/all_to_all | solution.py:70
  66.6 0.1 shard_map.62.own_ref
  66.7 0.1 collective-permute-start.14
  66.8 1.7 %collective-permute-start.15 = (f32[4,3840]{1,0:T(4,128)S(1)}, f32[4,3840]{1,0:T(4,128)S(1)}, u32[]{:S(2)}, u32[]{:S(2)}) collective-permute-start(f32[4,3840]{1,0:T(4,128)S(1)} %shard_map.62.own_ref), channel_id=1, source_target_pairs={{0,2},{1,3},{2,0},{3,1},{4,6},{5,7},{6,4},{7,5},{8,10},{9,11},{10,... | collective-permute-start | bytes 184328 | tf_op jit(solution)/shard_map/ppermute | solution.py:63
  68.5 1.0 %collective-permute-start.16 = (f32[4,3840]{1,0:T(4,128)S(1)}, f32[4,3840]{1,0:T(4,128)S(1)}, u32[]{:S(2)}, u32[]{:S(2)}) collective-permute-start(f32[4,3840]{1,0:T(4,128)S(1)} %shard_map.62.own_ref), channel_id=1, source_target_pairs={{0,3},{1,0},{2,1},{3,2},{4,7},{5,4},{6,5},{7,6},{8,11},{9,8},{10,9... | collective-permute-start | bytes 184328 | tf_op jit(solution)/shard_map/ppermute | solution.py:63
  69.5 2.3 %collective-permute-done.14.refs_0_ = f32[4,3840]{1,0:T(4,128)S(1)} collective-permute-done((f32[4,3840]{1,0:T(4,128)S(1)}, f32[4,3840]{1,0:T(4,128)S(1)}, u32[]{:S(2)}, u32[]{:S(2)}) %collective-permute-start.14) | collective-permute-done | bytes 61472 | tf_op jit(solution)/shard_map/ppermute | solution.py:63
  71.8 0.6 collective-permute-done.16.refs_2_
  72.4 0.5 collective-permute-start.17
  72.8 0.8 collective-permute-start.18
  73.6 1.7 %collective-permute-start.19 = (f32[1,384]{1,0:T(1,128)S(1)}, f32[1,384]{1,0:T(1,128)S(1)}, u32[]{:S(2)}, u32[]{:S(2)}) collective-permute-start(f32[1,384]{1,0:T(1,128)S(1)} %shard_map.63.own_ref), channel_id=1, source_target_pairs={{0,24},{1,25},{2,26},{3,27},{4,28},{5,29},{6,30},{7,31},{8,0},{9,1... | collective-permute-start | bytes 4616 | tf_op jit(solution)/shard_map/ppermute | solution.py:63
  75.3 0.8 collective-permute-done.17.refs_0_
  76.1 0.7 collective-permute-done.18.refs_1_
  76.8 5.8 %collective-permute-start.20 = (f32[1,384]{1,0:T(1,128)S(1)}, f32[1,384]{1,0:T(1,128)S(1)}, u32[]{:S(2)}, u32[]{:S(2)}) collective-permute-start(f32[1,384]{1,0:T(1,128)S(1)} %shard_map.64.refs_6_), channel_id=1, source_target_pairs={{0,32},{1,33},{2,34},{3,35},{4,36},{5,37},{6,38},{7,39},{8,40},{9,... | collective-permute-start | bytes 4616 | tf_op jit(solution)/shard_map/ppermute | solution.py:63
  82.6 0.8 collective-permute-done.20.refs_7_
  83.4 0.7 shard_map.65
  (29 shorter events, 0.2 us)
Async XLA Ops:
  0.6 1.0 %copy-start = (bf16[8,16,16,128]{3,2,1,0:T(8,128)(2,1)S(1)}, bf16[8,16,16,128]{3,2,1,0:T(8,128)(2,1)}, u32[]{:S(2)}) copy-start(bf16[8,16,16,128]{3,2,1,0:T(8,128)(2,1)} %in_ref.3) | copy-start | bytes 1572868
  1.7 1.0 %copy-start.2 = (bf16[8,16,16,128]{3,2,1,0:T(8,128)(2,1)S(1)}, bf16[8,16,16,128]{3,2,1,0:T(8,128)(2,1)}, u32[]{:S(2)}) copy-start(bf16[8,16,16,128]{3,2,1,0:T(8,128)(2,1)} %mid_ref.9) | copy-start | bytes 1572868
  2.7 0.8 copy-start.4
  3.8 10.5 %copy-start.3 = (bf16[8,16,16,128]{3,2,1,0:T(8,128)(2,1)S(1)}, bf16[8,16,16,128]{3,2,1,0:T(8,128)(2,1)}, u32[]{:S(2)}) copy-start(bf16[8,16,16,128]{3,2,1,0:T(8,128)(2,1)} %mid_ref.9) | copy-start | bytes 1572868
  3.8 8.3 %collective-permute-start.9 = (bf16[1,4,3584]{2,1,0:T(4,128)(2,1)S(1)}, bf16[1,4,3584]{2,1,0:T(4,128)(2,1)S(1)}, u32[]{:S(2)}, u32[]{:S(2)}) collective-permute-start(bf16[1,4,3584]{2,1,0:T(4,128)(2,1)S(1)} %get-tuple-element.41.refs_0_), channel_id=1, source_target_pairs={{0,16},{1,17},{2,18},{3,19},{4,20},{5,21},{6,22},{7,23},{8,24},{9,... | collective-permute-start | bytes 86024 | tf_op jit(solution)/shard_map/ppermute | solution.py:63
  7.6 5.0 %collective-permute-start = (bf16[1,16,16,128]{3,2,1,0:T(8,128)(2,1)S(1)}, bf16[1,16,16,128]{3,2,1,0:T(8,128)(2,1)S(1)}, u32[]{:S(2)}, u32[]{:S(2)}) collective-permute-start(bf16[1,16,16,128]{3,2,1,0:T(8,128)(2,1)S(1)} %get-tuple-element.25), channel_id=1, source_target_pairs={{0,32},{64,96},{128,160},{192,224},{32,0},{96,64},{160,128},{224,1... | collective-permute-start | bytes 196616 | tf_op jit(solution)/shard_map/ppermute | solution.py:80
  8.6 5.6 %collective-permute-start.1 = (bf16[1,16,16,128]{3,2,1,0:T(8,128)(2,1)S(1)}, bf16[1,16,16,128]{3,2,1,0:T(8,128)(2,1)S(1)}, u32[]{:S(2)}, u32[]{:S(2)}) collective-permute-start(bf16[1,16,16,128]{3,2,1,0:T(8,128)(2,1)S(1)} %get-tuple-element.26), channel_id=1, source_target_pairs={{32,64},{96,128},{160,192},{64,32},{128,96},{192,160},{33,65},{97,... | collective-permute-start | bytes 196616 | tf_op jit(solution)/shard_map/ppermute | solution.py:81
  12.2 5.3 %collective-permute-start.10 = (bf16[2,4,3584]{2,1,0:T(4,128)(2,1)S(1)}, bf16[2,4,3584]{2,1,0:T(4,128)(2,1)S(1)}, u32[]{:S(2)}, u32[]{:S(2)}) collective-permute-start(bf16[2,4,3584]{2,1,0:T(4,128)(2,1)S(1)} %pad_maximum_fusion.2), channel_id=1, source_target_pairs={{0,8},{1,9},{2,10},{3,11},{4,12},{5,13},{6,14},{7,15},{8,0},{9,1},... | collective-permute-start | bytes 172040 | tf_op jit(solution)/shard_map/ppermute | solution.py:63
  14.3 6.4 %collective-permute-start.2 = (bf16[10,18,128]{2,1,0:T(8,128)(2,1)S(1)}, bf16[10,18,128]{2,1,0:T(8,128)(2,1)S(1)}, u32[]{:S(2)}, u32[]{:S(2)}) collective-permute-start(bf16[10,18,128]{2,1,0:T(8,128)(2,1)S(1)} %get-tuple-element.29), channel_id=1, source_target_pairs={{0,8},{16,24},{8,0},{24,16},{1,9},{17,25},{9,1},{25,17},{2,10},{18... | collective-permute-start | bytes 138248 | tf_op jit(solution)/shard_map/ppermute | solution.py:80
  14.7 5.9 %collective-permute-start.3 = (bf16[10,18,128]{2,1,0:T(8,128)(2,1)S(1)}, bf16[10,18,128]{2,1,0:T(8,128)(2,1)S(1)}, u32[]{:S(2)}, u32[]{:S(2)}) collective-permute-start(bf16[10,18,128]{2,1,0:T(8,128)(2,1)S(1)} %get-tuple-element.30), channel_id=1, source_target_pairs={{8,16},{16,8},{9,17},{17,9},{10,18},{18,10},{11,19},{19,11},{12,20... | collective-permute-start | bytes 138248 | tf_op jit(solution)/shard_map/ppermute | solution.py:81
  15.4 5.3 %copy-start.1 = (bf16[8,16,16,128]{3,2,1,0:T(8,128)(2,1)S(1)}, bf16[8,16,16,128]{3,2,1,0:T(8,128)(2,1)}, u32[]{:S(2)}) copy-start(bf16[8,16,16,128]{3,2,1,0:T(8,128)(2,1)} %in_ref.3) | copy-start | bytes 1572868
  15.5 8.4 %collective-permute-start.4 = (bf16[10,16,128]{2,1,0:T(8,128)(2,1)S(1)}, bf16[10,16,128]{2,1,0:T(8,128)(2,1)S(1)}, u32[]{:S(2)}, u32[]{:S(2)}) collective-permute-start(bf16[10,16,128]{2,1,0:T(8,128)(2,1)S(1)} %get-tuple-element.35), channel_id=1, source_target_pairs={{0,1},{2,3},{4,5},{6,7},{1,0},{3,2},{5,4},{7,6},{8,9},{10,11},{12,... | collective-permute-start | bytes 122888 | tf_op jit(solution)/shard_map/ppermute | solution.py:80
  16.8 7.1 %collective-permute-start.5 = (bf16[10,16,128]{2,1,0:T(8,128)(2,1)S(1)}, bf16[10,16,128]{2,1,0:T(8,128)(2,1)S(1)}, u32[]{:S(2)}, u32[]{:S(2)}) collective-permute-start(bf16[10,16,128]{2,1,0:T(8,128)(2,1)S(1)} %get-tuple-element.36), channel_id=1, source_target_pairs={{1,2},{3,4},{5,6},{2,1},{4,3},{6,5},{9,10},{11,12},{13,14},{10,9},... | collective-permute-start | bytes 122888 | tf_op jit(solution)/shard_map/ppermute | solution.py:81
  17.6 8.5 %collective-permute-start.11 = (bf16[4,4,3584]{2,1,0:T(4,128)(2,1)S(1)}, bf16[4,4,3584]{2,1,0:T(4,128)(2,1)S(1)}, u32[]{:S(2)}, u32[]{:S(2)}) collective-permute-start(bf16[4,4,3584]{2,1,0:T(4,128)(2,1)S(1)} %pad_maximum_fusion.1), channel_id=1, source_target_pairs={{0,128},{1,129},{2,130},{3,131},{4,132},{5,133},{6,134},{7,135},{8... | collective-permute-start | bytes 344072 | tf_op jit(solution)/shard_map/ppermute | solution.py:63
  24.2 2.9 %collective-permute-start.6 = (bf16[64,3456]{1,0:T(8,128)(2,1)S(1)}, bf16[64,3456]{1,0:T(8,128)(2,1)S(1)}, u32[]{:S(2)}, u32[]{:S(2)}) collective-permute-start(bf16[64,3456]{1,0:T(8,128)(2,1)S(1)} %get-tuple-element.38), channel_id=1, source_target_pairs={{0,32},{1,33},{2,34},{3,35},{4,36},{5,37},{6,38},{7,39},{8,40},{9,... | collective-permute-start | bytes 1327112 | tf_op jit(solution)/shard_map/ppermute | solution.py:63
  26.2 17.3 %collective-permute-start.12 = (bf16[8,4,3584]{2,1,0:T(4,128)(2,1)S(1)}, bf16[8,4,3584]{2,1,0:T(4,128)(2,1)S(1)}, u32[]{:S(2)}, u32[]{:S(2)}) collective-permute-start(bf16[8,4,3584]{2,1,0:T(4,128)(2,1)S(1)} %pad_maximum_fusion), channel_id=1, source_target_pairs={{0,64},{1,65},{2,66},{3,67},{4,68},{5,69},{6,70},{7,71},{8,72},{9,... | collective-permute-start | bytes 688136 | tf_op jit(solution)/shard_map/ppermute | solution.py:63
  28.0 25.3 %all-to-all-start = ((bf16[16,4,3456]{2,1,0:T(4,128)(2,1)}), bf16[16,4,3456]{2,1,0:T(4,128)(2,1)S(1)}, u32[]{:S(2)}, u32[]{:S(2)}) async-start(bf16[16,4,3456]{2,1,0:T(4,128)(2,1)} %shard_map.56), calls=%async_computation | async-start | bytes 884736 | tf_op jit(solution)/shard_map/all_to_all | solution.py:70
  43.6 14.1 %collective-permute-start.13 = (bf16[16,4,3584]{2,1,0:T(4,128)(2,1)S(1)}, bf16[16,4,3584]{2,1,0:T(4,128)(2,1)S(1)}, u32[]{:S(2)}, u32[]{:S(2)}) collective-permute-start(bf16[16,4,3584]{2,1,0:T(4,128)(2,1)S(1)} %shard_map.59.near_ref), channel_id=1, source_target_pairs={{0,32},{1,33},{2,34},{3,35},{4,36},{5,37},{6,38},{7,39},{8,40},{9,... | collective-permute-start | bytes 1376264 | tf_op jit(solution)/shard_map/ppermute | solution.py:63
  44.4 14.5 %collective-permute-start.7 = (bf16[10,2,128]{2,1,0:T(2,128)(2,1)S(1)}, bf16[10,2,128]{2,1,0:T(2,128)(2,1)S(1)}, u32[]{:S(2)}, u32[]{:S(2)}) collective-permute-start(bf16[10,2,128]{2,1,0:T(2,128)(2,1)S(1)} %get-tuple-element.39), channel_id=1, source_target_pairs={{0,8},{16,24},{8,0},{24,16},{1,9},{17,25},{9,1},{25,17},{2,10},{18... | collective-permute-start | bytes 15368 | tf_op jit(solution)/shard_map/ppermute | solution.py:80
  46.1 12.7 %collective-permute-start.8 = (bf16[10,2,128]{2,1,0:T(2,128)(2,1)S(1)}, bf16[10,2,128]{2,1,0:T(2,128)(2,1)S(1)}, u32[]{:S(2)}, u32[]{:S(2)}) collective-permute-start(bf16[10,2,128]{2,1,0:T(2,128)(2,1)S(1)} %get-tuple-element.40), channel_id=1, source_target_pairs={{8,16},{16,8},{9,17},{17,9},{10,18},{18,10},{11,19},{19,11},{12,20... | collective-permute-start | bytes 15368 | tf_op jit(solution)/shard_map/ppermute | solution.py:81
  54.1 12.5 %all-to-all-start.1 = ((bf16[8,4,3456]{2,1,0:T(4,128)(2,1)}), bf16[8,4,3456]{2,1,0:T(4,128)(2,1)S(1)}, u32[]{:S(2)}, u32[]{:S(2)}) async-start(bf16[8,4,3456]{2,1,0:T(4,128)(2,1)} %shard_map.57), calls=%async_computation.1 | async-start | bytes 442368 | tf_op jit(solution)/shard_map/all_to_all | solution.py:70
  66.7 5.0 %collective-permute-start.14 = (f32[4,3840]{1,0:T(4,128)S(1)}, f32[4,3840]{1,0:T(4,128)S(1)}, u32[]{:S(2)}, u32[]{:S(2)}) collective-permute-start(f32[4,3840]{1,0:T(4,128)S(1)} %shard_map.62.own_ref), channel_id=1, source_target_pairs={{0,1},{1,2},{2,3},{3,0},{4,5},{5,6},{6,7},{7,4},{8,9},{9,10},{10,1... | collective-permute-start | bytes 184328 | tf_op jit(solution)/shard_map/ppermute | solution.py:63
  66.8 4.9 %collective-permute-start.15 = (f32[4,3840]{1,0:T(4,128)S(1)}, f32[4,3840]{1,0:T(4,128)S(1)}, u32[]{:S(2)}, u32[]{:S(2)}) collective-permute-start(f32[4,3840]{1,0:T(4,128)S(1)} %shard_map.62.own_ref), channel_id=1, source_target_pairs={{0,2},{1,3},{2,0},{3,1},{4,6},{5,7},{6,4},{7,5},{8,10},{9,11},{10,... | collective-permute-start | bytes 184328 | tf_op jit(solution)/shard_map/ppermute | solution.py:63
  68.5 3.8 %collective-permute-start.16 = (f32[4,3840]{1,0:T(4,128)S(1)}, f32[4,3840]{1,0:T(4,128)S(1)}, u32[]{:S(2)}, u32[]{:S(2)}) collective-permute-start(f32[4,3840]{1,0:T(4,128)S(1)} %shard_map.62.own_ref), channel_id=1, source_target_pairs={{0,3},{1,0},{2,1},{3,2},{4,7},{5,4},{6,5},{7,6},{8,11},{9,8},{10,9... | collective-permute-start | bytes 184328 | tf_op jit(solution)/shard_map/ppermute | solution.py:63
  72.4 11.1 %copy-start.5 = (f32[4,27,128]{2,0,1:T(4,128)S(1)}, f32[4,27,128]{2,0,1:T(4,128)}, u32[]{:S(2)}) copy-start(f32[4,27,128]{2,0,1:T(4,128)} %param.3) | copy-start | bytes 165892
  72.4 3.7 %collective-permute-start.17 = (f32[1,384]{1,0:T(1,128)S(1)}, f32[1,384]{1,0:T(1,128)S(1)}, u32[]{:S(2)}, u32[]{:S(2)}) collective-permute-start(f32[1,384]{1,0:T(1,128)S(1)} %shard_map.63.own_ref), channel_id=1, source_target_pairs={{0,8},{1,9},{2,10},{3,11},{4,12},{5,13},{6,14},{7,15},{8,16},{9,17... | collective-permute-start | bytes 4616 | tf_op jit(solution)/shard_map/ppermute | solution.py:63
  72.8 3.9 %collective-permute-start.18 = (f32[1,384]{1,0:T(1,128)S(1)}, f32[1,384]{1,0:T(1,128)S(1)}, u32[]{:S(2)}, u32[]{:S(2)}) collective-permute-start(f32[1,384]{1,0:T(1,128)S(1)} %shard_map.63.own_ref), channel_id=1, source_target_pairs={{0,16},{1,17},{2,18},{3,19},{4,20},{5,21},{6,22},{7,23},{8,24},{9,... | collective-permute-start | bytes 4616 | tf_op jit(solution)/shard_map/ppermute | solution.py:63
  73.6 3.2 %collective-permute-start.19 = (f32[1,384]{1,0:T(1,128)S(1)}, f32[1,384]{1,0:T(1,128)S(1)}, u32[]{:S(2)}, u32[]{:S(2)}) collective-permute-start(f32[1,384]{1,0:T(1,128)S(1)} %shard_map.63.own_ref), channel_id=1, source_target_pairs={{0,24},{1,25},{2,26},{3,27},{4,28},{5,29},{6,30},{7,31},{8,0},{9,1... | collective-permute-start | bytes 4616 | tf_op jit(solution)/shard_map/ppermute | solution.py:63
  76.8 6.6 %collective-permute-start.20 = (f32[1,384]{1,0:T(1,128)S(1)}, f32[1,384]{1,0:T(1,128)S(1)}, u32[]{:S(2)}, u32[]{:S(2)}) collective-permute-start(f32[1,384]{1,0:T(1,128)S(1)} %shard_map.64.refs_6_), channel_id=1, source_target_pairs={{0,32},{1,33},{2,34},{3,35},{4,36},{5,37},{6,38},{7,39},{8,40},{9,... | collective-permute-start | bytes 4616 | tf_op jit(solution)/shard_map/ppermute | solution.py:63

commit v9 on v7

--- a/solution.py
+++ b/solution.py
@@ -225,10 +225,9 @@
     cells = nx * ny * nz
     flat = in_ref[...].reshape(cells, ch).T
     for a in range(3):
-        for b in range(3):
-            view = taps_ref[2 - a : 2 - a + nx, 2 - b : 2 - b + ny].reshape(cells, 3 * ch)
-            lanes = pl.ds((a * 3 + b) * 3 * ch, 3 * ch)
-            total_ref[:, lanes] = jnp.dot(flat, view, preferred_element_type=jnp.float32)
+        views = [taps_ref[2 - a : 2 - a + nx, 2 - b : 2 - b + ny].reshape(cells, 3 * ch) for b in range(3)]
+        lanes = pl.ds(a * 9 * ch, 9 * ch)
+        total_ref[:, lanes] = jnp.dot(flat, jnp.concatenate(views, axis=1), preferred_element_type=jnp.float32)
     below, above = picked(is_odd("gy"), ya_ref[1 : nx + 1, nz:], yb_ref[1 : nx + 1, nz:])
     below, above = below.astype(jnp.float32), above.astype(jnp.float32)
     for side, own_ref in enumerate((il_ref, ih_ref)):

time: 86.2 us -> 86.2 us (level)
  transfers between devices with their start and end apart: 19 -> 19, of which waited for: 4 -> 4; matrix products, arithmetic and copies ran while one was open for 0% -> 0% of each run, Pallas kernels for 14% -> 13%
where the time goes in v9:
time: 86.2 us; the launch traced here: 85.7 us
  starting transfers between devices  41.8 us (48%)
  blocking collectives  15.4 us (18%)
  Pallas kernels  12.5 us (15%)
  waiting for transfers between devices  11.9 us (14%)
  local copies, waits for them, and re-layouts  2.91 us (3%)
  between operations  0.87 us (1%)
    all_to_all x2, starting transfers between devices, exchange(): lax.all_to_all(array, AXES, 0, 0, tiled=True, axis_index_groups=groups)  19.6 us
    all_to_all x1, blocking collectives, exchange(): lax.all_to_all(array, AXES, 0, 0, tiled=True, axis_index_groups=groups)  15.4 us
    pallas_call x14, Pallas kernels, call(): pl.pallas_call(kernel, out_shape=out_shape, in_specs=[pl.BlockSpec(memory...  12.5 us
    ppermute x9, starting transfers between devices, send(): return lax.ppermute(array, AXES, pairs)  12.2 us
    all_to_all x2, waiting for transfers between devices, exchange(): lax.all_to_all(array, AXES, 0, 0, tiled=True, axis_index_groups=groups)  9.02 us
    ppermute x4, starting transfers between devices, swapped(): second = lax.ppermute(second, axis, pairs(1))  5.4 us
    ppermute x4, starting transfers between devices, swapped(): first = lax.ppermute(first, axis, pairs(0))  4.55 us
    unnamed x12, local copies, waits for them, and re-layouts  2.91 us
  transfers between devices with their start and end apart: 19, of which 4 were waited for; matrix products, arithmetic and copies ran while one was open for 0% of the time, Pallas kernels for 13%

profile of v9, /device:TPU:1, one launch (start us, length us, event | category | flops | bytes accessed | tf_op | source)
XLA Modules:
  0.0 85.7 jit_solution(1209581125147483286)
XLA Ops:
  0.6 0.0 copy-start
  0.6 1.0 %copy-done = bf16[8,16,16,128]{3,2,1,0:T(8,128)(2,1)S(1)} copy-done((bf16[8,16,16,128]{3,2,1,0:T(8,128)(2,1)S(1)}, bf16[8,16,16,128]{3,2,1,0:T(8,128)(2,1)}, u32[]{:S(2)}) %copy-start) | copy-done | bytes 524312
  1.7 1.0 %copy-done.2 = bf16[8,16,16,128]{3,2,1,0:T(8,128)(2,1)S(1)} copy-done((bf16[8,16,16,128]{3,2,1,0:T(8,128)(2,1)S(1)}, bf16[8,16,16,128]{3,2,1,0:T(8,128)(2,1)}, u32[]{:S(2)}) %copy-start.2) | copy-done | bytes 524312
  2.7 0.8 copy-done.4
  3.5 0.2 shard_map.51
  3.8 0.0 copy-start.3
  3.8 3.8 %collective-permute-start.9 = (bf16[1,4,3584]{2,1,0:T(4,128)(2,1)S(1)}, bf16[1,4,3584]{2,1,0:T(4,128)(2,1)S(1)}, u32[]{:S(2)}, u32[]{:S(2)}) collective-permute-start(bf16[1,4,3584]{2,1,0:T(4,128)(2,1)S(1)} %get-tuple-element.43.refs_0_), channel_id=1, source_target_pairs={{0,16},{1,17},{2,18},{3,19},{4,20},{5,21},{6,22},{7,23},{8,24},{9,... | collective-permute-start | bytes 86024 | tf_op jit(solution)/shard_map/ppermute | solution.py:63
  7.6 1.0 %collective-permute-start = (bf16[1,16,16,128]{3,2,1,0:T(8,128)(2,1)S(1)}, bf16[1,16,16,128]{3,2,1,0:T(8,128)(2,1)S(1)}, u32[]{:S(2)}, u32[]{:S(2)}) collective-permute-start(bf16[1,16,16,128]{3,2,1,0:T(8,128)(2,1)S(1)} %get-tuple-element.27), channel_id=1, source_target_pairs={{0,32},{64,96},{128,160},{192,224},{32,0},{96,64},{160,128},{224,1... | collective-permute-start | bytes 196616 | tf_op jit(solution)/shard_map/ppermute | solution.py:80
  8.6 3.4 %collective-permute-start.1 = (bf16[1,16,16,128]{3,2,1,0:T(8,128)(2,1)S(1)}, bf16[1,16,16,128]{3,2,1,0:T(8,128)(2,1)S(1)}, u32[]{:S(2)}, u32[]{:S(2)}) collective-permute-start(bf16[1,16,16,128]{3,2,1,0:T(8,128)(2,1)S(1)} %get-tuple-element.28), channel_id=1, source_target_pairs={{32,64},{96,128},{160,192},{64,32},{128,96},{192,160},{33,65},{97,... | collective-permute-start | bytes 196616 | tf_op jit(solution)/shard_map/ppermute | solution.py:81
  12.1 0.0 collective-permute-done.9.refs_1_
  12.2 0.5 collective-permute-start.10
  12.6 0.0 collective-permute-done.xa_ref
  12.6 1.6 %collective-permute-done.1.xb_ref = bf16[1,16,16,128]{3,2,1,0:T(8,128)(2,1)S(1)} collective-permute-done((bf16[1,16,16,128]{3,2,1,0:T(8,128)(2,1)S(1)}, bf16[1,16,16,128]{3,2,1,0:T(8,128)(2,1)S(1)}, u32[]{:S(2)}, u32[]{:S(2)}) %collective-permute-start.1) | collective-permute-done | bytes 65568 | tf_op jit(solution)/shard_map/ppermute | solution.py:81
  14.3 0.5 collective-permute-start.2
  14.7 0.7 collective-permute-start.3
  15.4 0.0 copy-start.1
  15.4 0.1 shard_map.54
  15.5 1.3 %collective-permute-start.4 = (bf16[10,16,128]{2,1,0:T(8,128)(2,1)S(1)}, bf16[10,16,128]{2,1,0:T(8,128)(2,1)S(1)}, u32[]{:S(2)}, u32[]{:S(2)}) collective-permute-start(bf16[10,16,128]{2,1,0:T(8,128)(2,1)S(1)} %get-tuple-element.37), channel_id=1, source_target_pairs={{0,1},{2,3},{4,5},{6,7},{1,0},{3,2},{5,4},{7,6},{8,9},{10,11},{12,... | collective-permute-start | bytes 122888 | tf_op jit(solution)/shard_map/ppermute | solution.py:80
  16.8 0.7 collective-permute-start.5
  17.5 0.0 collective-permute-done.10.refs_2_
  17.5 0.1 pad_maximum_fusion.1
  17.6 3.1 %collective-permute-start.11 = (bf16[4,4,3584]{2,1,0:T(4,128)(2,1)S(1)}, bf16[4,4,3584]{2,1,0:T(4,128)(2,1)S(1)}, u32[]{:S(2)}, u32[]{:S(2)}) collective-permute-start(bf16[4,4,3584]{2,1,0:T(4,128)(2,1)S(1)} %pad_maximum_fusion.1), channel_id=1, source_target_pairs={{0,128},{1,129},{2,130},{3,131},{4,132},{5,133},{6,134},{7,135},{8... | collective-permute-start | bytes 344072 | tf_op jit(solution)/shard_map/ppermute | solution.py:63
  20.7 2.8 %shard_map.53 = (f32[128,3456]{1,0:T(8,128)S(1)}, bf16[2,3,128,128]{3,2,1,0:T(8,128)(2,1)S(1)}) custom-call(bf16[8,16,16,128]{3,2,1,0:T(8,128)(2,1)S(1)} %copy-done.3, bf16[1,16,16,128]{3,2,1,0:T(8,128)(2,1)S(1)} %collective-permute-done.xa_ref, bf16[1,16,16,128]{3,2,1,0:T(8,128)(2,1)S(1)} %collective-permute-done.1.xb_ref, ...), custom_call_target="tpu_custom_call" | custom-call | flops 3623878656 | bytes 1000000 | tf_op jit(solution)/shard_map/pallas_call | solution.py:22
  23.4 0.0 collective-permute-done.5.zb_ref
  23.5 0.3 shard_map.55
  23.8 0.9 %collective-permute-start.6 = (bf16[64,3456]{1,0:T(8,128)(2,1)S(1)}, bf16[64,3456]{1,0:T(8,128)(2,1)S(1)}, u32[]{:S(2)}, u32[]{:S(2)}) collective-permute-start(bf16[64,3456]{1,0:T(8,128)(2,1)S(1)} %get-tuple-element.40), channel_id=1, source_target_pairs={{0,32},{1,33},{2,34},{3,35},{4,36},{5,37},{6,38},{7,39},{8,40},{9,... | collective-permute-start | bytes 1327112 | tf_op jit(solution)/shard_map/ppermute | solution.py:63
  24.7 1.3 %collective-permute-done.11.refs_3_ = bf16[4,4,3584]{2,1,0:T(4,128)(2,1)S(1)} collective-permute-done((bf16[4,4,3584]{2,1,0:T(4,128)(2,1)S(1)}, bf16[4,4,3584]{2,1,0:T(4,128)(2,1)S(1)}, u32[]{:S(2)}, u32[]{:S(2)}) %collective-permute-start.11) | collective-permute-done | bytes 114720 | tf_op jit(solution)/shard_map/ppermute | solution.py:63
  26.1 0.2 pad_maximum_fusion
  26.2 0.4 collective-permute-start.12
  26.6 0.0 collective-permute-done.6.other_ref
  26.6 0.9 %shard_map.56 = bf16[16,4,3456]{2,1,0:T(4,128)(2,1)} custom-call(f32[64,3456]{1,0:T(8,128)S(1)} %get-tuple-element.39.keep_ref, bf16[64,3456]{1,0:T(8,128)(2,1)S(1)} %collective-permute-done.6.other_ref), custom_call_target="tpu_custom_call" | custom-call | flops 1000000000 | bytes 1000000 | tf_op jit(solution)/shard_map/pallas_call | solution.py:22
  27.5 16.0 %all-to-all-start = ((bf16[16,4,3456]{2,1,0:T(4,128)(2,1)}), bf16[16,4,3456]{2,1,0:T(4,128)(2,1)S(1)}, u32[]{:S(2)}, u32[]{:S(2)}) async-start(bf16[16,4,3456]{2,1,0:T(4,128)(2,1)} %shard_map.56), calls=%async_computation | async-start | bytes 884736 | tf_op jit(solution)/shard_map/all_to_all | solution.py:70
  43.5 0.0 collective-permute-done.12.refs_4_
  43.6 0.8 collective-permute-start.13
  44.4 1.7 %collective-permute-start.7 = (bf16[10,2,128]{2,1,0:T(2,128)(2,1)S(1)}, bf16[10,2,128]{2,1,0:T(2,128)(2,1)S(1)}, u32[]{:S(2)}, u32[]{:S(2)}) collective-permute-start(bf16[10,2,128]{2,1,0:T(2,128)(2,1)S(1)} %get-tuple-element.41), channel_id=1, source_target_pairs={{0,8},{16,24},{8,0},{24,16},{1,9},{17,25},{9,1},{25,17},{2,10},{18... | collective-permute-start | bytes 15368 | tf_op jit(solution)/shard_map/ppermute | solution.py:80
  46.1 0.6 collective-permute-start.8
  46.8 6.5 %all-to-all-done.parts_ref = bf16[16,4,3456]{2,1,0:T(4,128)(2,1)S(1)} async-done(((bf16[16,4,3456]{2,1,0:T(4,128)(2,1)}), bf16[16,4,3456]{2,1,0:T(4,128)(2,1)S(1)}, u32[]{:S(2)}, u32[]{:S(2)}) %all-to-all-start) | async-done | bytes 442400 | tf_op jit(solution)/shard_map/all_to_all | solution.py:70
  53.3 0.9 %shard_map.57 = bf16[8,4,3456]{2,1,0:T(4,128)(2,1)} custom-call(bf16[16,4,3456]{2,1,0:T(4,128)(2,1)S(1)} %all-to-all-done.parts_ref), custom_call_target="tpu_custom_call" | custom-call | flops 1000000000 | bytes 1000000 | tf_op jit(solution)/shard_map/pallas_call | solution.py:22
  54.1 3.6 %all-to-all-start.1 = ((bf16[8,4,3456]{2,1,0:T(4,128)(2,1)}), bf16[8,4,3456]{2,1,0:T(4,128)(2,1)S(1)}, u32[]{:S(2)}, u32[]{:S(2)}) async-start(bf16[8,4,3456]{2,1,0:T(4,128)(2,1)} %shard_map.57), calls=%async_computation.1 | async-start | bytes 442368 | tf_op jit(solution)/shard_map/all_to_all | solution.py:70
  57.7 1.1 %shard_map.60 = (bf16[128,3456]{1,0:T(8,128)(2,1)S(1)}, f32[1,128]{1,0:T(1,128)S(1)}, f32[1,128]{1,0:T(1,128)S(1)}, f32[4,3456]{1,0:T(4,128)S(1)}) custom-call(bf16[16,4,3584]{2,1,0:T(4,128)(2,1)S(1)} %shard_map.59.near_ref, bf16[16,4,3584]{2,1,0:T(4,128)(2,1)S(1)} %collective-permute-done.13.far_ref), custom_call_target="tpu_custom_call" | custom-call | flops 3000000000 | bytes 1000000 | tf_op jit(solution)/shard_map/pallas_call | solution.py:22
  58.9 5.2 %shard_map.61 = bf16[8,16,16,128]{3,2,1,0:T(8,128)(2,1)} custom-call(bf16[8,16,16,128]{3,2,1,0:T(8,128)(2,1)S(1)} %copy-done.3, bf16[1,16,16,128]{3,2,1,0:T(8,128)(2,1)S(1)} %collective-permute-done.xa_ref, bf16[1,16,16,128]{3,2,1,0:T(8,128)(2,1)S(1)} %collective-permute-done.1.xb_ref, bf16[10,18,128]{2,1,0:T(8,128)(2,1)S(1)} %collective-permute-done.2.ya_ref, ...), custom_call_target="tpu_custom_call" | custom-call | flops 3623878656 | bytes 1000000 | tf_op jit(solution)/shard_map/pallas_call | solution.py:22
  64.1 2.5 %all-to-all-done.1.parts_ref = bf16[8,4,3456]{2,1,0:T(4,128)(2,1)S(1)} async-done(((bf16[8,4,3456]{2,1,0:T(4,128)(2,1)}), bf16[8,4,3456]{2,1,0:T(4,128)(2,1)S(1)}, u32[]{:S(2)}, u32[]{:S(2)}) %all-to-all-start.1) | async-done | bytes 221216 | tf_op jit(solution)/shard_map/all_to_all | solution.py:70
  66.6 0.1 shard_map.62
  66.8 0.1 collective-permute-start.14
  66.8 1.7 %collective-permute-start.15 = (f32[4,3456]{1,0:T(4,128)S(1)}, f32[4,3456]{1,0:T(4,128)S(1)}, u32[]{:S(2)}, u32[]{:S(2)}) collective-permute-start(f32[4,3456]{1,0:T(4,128)S(1)} %get-tuple-element.48.own_ref), channel_id=1, source_target_pairs={{0,2},{1,3},{2,0},{3,1},{4,6},{5,7},{6,4},{7,5},{8,10},{9,11},{10,... | collective-permute-start | bytes 165896 | tf_op jit(solution)/shard_map/ppermute | solution.py:63
  68.5 1.0 %collective-permute-start.16 = (f32[4,3456]{1,0:T(4,128)S(1)}, f32[4,3456]{1,0:T(4,128)S(1)}, u32[]{:S(2)}, u32[]{:S(2)}) collective-permute-start(f32[4,3456]{1,0:T(4,128)S(1)} %get-tuple-element.48.own_ref), channel_id=1, source_target_pairs={{0,3},{1,0},{2,1},{3,2},{4,7},{5,4},{6,5},{7,6},{8,11},{9,8},{10,9... | collective-permute-start | bytes 165896 | tf_op jit(solution)/shard_map/ppermute | solution.py:63
  69.5 15.4 %all_to_all.15.refs_6_ = f32[32,1,384]{2,1,0:T(1,128)S(1)} all-to-all(f32[32,1,384]{2,1,0:T(1,128)S(1)} %get-tuple-element.51), channel_id=1, replica_groups={{0,8,16,24,1,9,17,25,2,10,18,26,3,11,19,27,32,40,48,56,33,41,49,57,34,4..., dimensions={0} | all-to-all | bytes 98304 | tf_op jit(solution)/shard_map/all_to_all | solution.py:70
  84.9 0.8 shard_map.63
  (20 shorter events, 0.2 us)
Async XLA Ops:
  0.6 1.0 %copy-start = (bf16[8,16,16,128]{3,2,1,0:T(8,128)(2,1)S(1)}, bf16[8,16,16,128]{3,2,1,0:T(8,128)(2,1)}, u32[]{:S(2)}) copy-start(bf16[8,16,16,128]{3,2,1,0:T(8,128)(2,1)} %in_ref.3) | copy-start | bytes 1572868
  1.7 1.0 %copy-start.2 = (bf16[8,16,16,128]{3,2,1,0:T(8,128)(2,1)S(1)}, bf16[8,16,16,128]{3,2,1,0:T(8,128)(2,1)}, u32[]{:S(2)}) copy-start(bf16[8,16,16,128]{3,2,1,0:T(8,128)(2,1)} %mid_ref.9) | copy-start | bytes 1572868
  2.7 0.8 copy-start.4
  3.8 10.5 %copy-start.3 = (bf16[8,16,16,128]{3,2,1,0:T(8,128)(2,1)S(1)}, bf16[8,16,16,128]{3,2,1,0:T(8,128)(2,1)}, u32[]{:S(2)}) copy-start(bf16[8,16,16,128]{3,2,1,0:T(8,128)(2,1)} %mid_ref.9) | copy-start | bytes 1572868
  3.8 8.3 %collective-permute-start.9 = (bf16[1,4,3584]{2,1,0:T(4,128)(2,1)S(1)}, bf16[1,4,3584]{2,1,0:T(4,128)(2,1)S(1)}, u32[]{:S(2)}, u32[]{:S(2)}) collective-permute-start(bf16[1,4,3584]{2,1,0:T(4,128)(2,1)S(1)} %get-tuple-element.43.refs_0_), channel_id=1, source_target_pairs={{0,16},{1,17},{2,18},{3,19},{4,20},{5,21},{6,22},{7,23},{8,24},{9,... | collective-permute-start | bytes 86024 | tf_op jit(solution)/shard_map/ppermute | solution.py:63
  7.6 5.0 %collective-permute-start = (bf16[1,16,16,128]{3,2,1,0:T(8,128)(2,1)S(1)}, bf16[1,16,16,128]{3,2,1,0:T(8,128)(2,1)S(1)}, u32[]{:S(2)}, u32[]{:S(2)}) collective-permute-start(bf16[1,16,16,128]{3,2,1,0:T(8,128)(2,1)S(1)} %get-tuple-element.27), channel_id=1, source_target_pairs={{0,32},{64,96},{128,160},{192,224},{32,0},{96,64},{160,128},{224,1... | collective-permute-start | bytes 196616 | tf_op jit(solution)/shard_map/ppermute | solution.py:80
  8.6 5.6 %collective-permute-start.1 = (bf16[1,16,16,128]{3,2,1,0:T(8,128)(2,1)S(1)}, bf16[1,16,16,128]{3,2,1,0:T(8,128)(2,1)S(1)}, u32[]{:S(2)}, u32[]{:S(2)}) collective-permute-start(bf16[1,16,16,128]{3,2,1,0:T(8,128)(2,1)S(1)} %get-tuple-element.28), channel_id=1, source_target_pairs={{32,64},{96,128},{160,192},{64,32},{128,96},{192,160},{33,65},{97,... | collective-permute-start | bytes 196616 | tf_op jit(solution)/shard_map/ppermute | solution.py:81
  12.2 5.3 %collective-permute-start.10 = (bf16[2,4,3584]{2,1,0:T(4,128)(2,1)S(1)}, bf16[2,4,3584]{2,1,0:T(4,128)(2,1)S(1)}, u32[]{:S(2)}, u32[]{:S(2)}) collective-permute-start(bf16[2,4,3584]{2,1,0:T(4,128)(2,1)S(1)} %pad_maximum_fusion.2), channel_id=1, source_target_pairs={{0,8},{1,9},{2,10},{3,11},{4,12},{5,13},{6,14},{7,15},{8,0},{9,1},... | collective-permute-start | bytes 172040 | tf_op jit(solution)/shard_map/ppermute | solution.py:63
  14.3 6.4 %collective-permute-start.2 = (bf16[10,18,128]{2,1,0:T(8,128)(2,1)S(1)}, bf16[10,18,128]{2,1,0:T(8,128)(2,1)S(1)}, u32[]{:S(2)}, u32[]{:S(2)}) collective-permute-start(bf16[10,18,128]{2,1,0:T(8,128)(2,1)S(1)} %get-tuple-element.31), channel_id=1, source_target_pairs={{0,8},{16,24},{8,0},{24,16},{1,9},{17,25},{9,1},{25,17},{2,10},{18... | collective-permute-start | bytes 138248 | tf_op jit(solution)/shard_map/ppermute | solution.py:80
  14.7 5.9 %collective-permute-start.3 = (bf16[10,18,128]{2,1,0:T(8,128)(2,1)S(1)}, bf16[10,18,128]{2,1,0:T(8,128)(2,1)S(1)}, u32[]{:S(2)}, u32[]{:S(2)}) collective-permute-start(bf16[10,18,128]{2,1,0:T(8,128)(2,1)S(1)} %get-tuple-element.32), channel_id=1, source_target_pairs={{8,16},{16,8},{9,17},{17,9},{10,18},{18,10},{11,19},{19,11},{12,20... | collective-permute-start | bytes 138248 | tf_op jit(solution)/shard_map/ppermute | solution.py:81
  15.4 5.3 %copy-start.1 = (bf16[8,16,16,128]{3,2,1,0:T(8,128)(2,1)S(1)}, bf16[8,16,16,128]{3,2,1,0:T(8,128)(2,1)}, u32[]{:S(2)}) copy-start(bf16[8,16,16,128]{3,2,1,0:T(8,128)(2,1)} %in_ref.3) | copy-start | bytes 1572868
  15.5 7.9 %collective-permute-start.4 = (bf16[10,16,128]{2,1,0:T(8,128)(2,1)S(1)}, bf16[10,16,128]{2,1,0:T(8,128)(2,1)S(1)}, u32[]{:S(2)}, u32[]{:S(2)}) collective-permute-start(bf16[10,16,128]{2,1,0:T(8,128)(2,1)S(1)} %get-tuple-element.37), channel_id=1, source_target_pairs={{0,1},{2,3},{4,5},{6,7},{1,0},{3,2},{5,4},{7,6},{8,9},{10,11},{12,... | collective-permute-start | bytes 122888 | tf_op jit(solution)/shard_map/ppermute | solution.py:80
  16.8 6.6 %collective-permute-start.5 = (bf16[10,16,128]{2,1,0:T(8,128)(2,1)S(1)}, bf16[10,16,128]{2,1,0:T(8,128)(2,1)S(1)}, u32[]{:S(2)}, u32[]{:S(2)}) collective-permute-start(bf16[10,16,128]{2,1,0:T(8,128)(2,1)S(1)} %get-tuple-element.38), channel_id=1, source_target_pairs={{1,2},{3,4},{5,6},{2,1},{4,3},{6,5},{9,10},{11,12},{13,14},{10,9},... | collective-permute-start | bytes 122888 | tf_op jit(solution)/shard_map/ppermute | solution.py:81
  17.6 8.5 %collective-permute-start.11 = (bf16[4,4,3584]{2,1,0:T(4,128)(2,1)S(1)}, bf16[4,4,3584]{2,1,0:T(4,128)(2,1)S(1)}, u32[]{:S(2)}, u32[]{:S(2)}) collective-permute-start(bf16[4,4,3584]{2,1,0:T(4,128)(2,1)S(1)} %pad_maximum_fusion.1), channel_id=1, source_target_pairs={{0,128},{1,129},{2,130},{3,131},{4,132},{5,133},{6,134},{7,135},{8... | collective-permute-start | bytes 344072 | tf_op jit(solution)/shard_map/ppermute | solution.py:63
  23.8 2.8 %collective-permute-start.6 = (bf16[64,3456]{1,0:T(8,128)(2,1)S(1)}, bf16[64,3456]{1,0:T(8,128)(2,1)S(1)}, u32[]{:S(2)}, u32[]{:S(2)}) collective-permute-start(bf16[64,3456]{1,0:T(8,128)(2,1)S(1)} %get-tuple-element.40), channel_id=1, source_target_pairs={{0,32},{1,33},{2,34},{3,35},{4,36},{5,37},{6,38},{7,39},{8,40},{9,... | collective-permute-start | bytes 1327112 | tf_op jit(solution)/shard_map/ppermute | solution.py:63
  26.2 17.3 %collective-permute-start.12 = (bf16[8,4,3584]{2,1,0:T(4,128)(2,1)S(1)}, bf16[8,4,3584]{2,1,0:T(4,128)(2,1)S(1)}, u32[]{:S(2)}, u32[]{:S(2)}) collective-permute-start(bf16[8,4,3584]{2,1,0:T(4,128)(2,1)S(1)} %pad_maximum_fusion), channel_id=1, source_target_pairs={{0,64},{1,65},{2,66},{3,67},{4,68},{5,69},{6,70},{7,71},{8,72},{9,... | collective-permute-start | bytes 688136 | tf_op jit(solution)/shard_map/ppermute | solution.py:63
  27.5 25.8 %all-to-all-start = ((bf16[16,4,3456]{2,1,0:T(4,128)(2,1)}), bf16[16,4,3456]{2,1,0:T(4,128)(2,1)S(1)}, u32[]{:S(2)}, u32[]{:S(2)}) async-start(bf16[16,4,3456]{2,1,0:T(4,128)(2,1)} %shard_map.56), calls=%async_computation | async-start | bytes 884736 | tf_op jit(solution)/shard_map/all_to_all | solution.py:70
  43.6 14.1 %collective-permute-start.13 = (bf16[16,4,3584]{2,1,0:T(4,128)(2,1)S(1)}, bf16[16,4,3584]{2,1,0:T(4,128)(2,1)S(1)}, u32[]{:S(2)}, u32[]{:S(2)}) collective-permute-start(bf16[16,4,3584]{2,1,0:T(4,128)(2,1)S(1)} %shard_map.59.near_ref), channel_id=1, source_target_pairs={{0,32},{1,33},{2,34},{3,35},{4,36},{5,37},{6,38},{7,39},{8,40},{9,... | collective-permute-start | bytes 1376264 | tf_op jit(solution)/shard_map/ppermute | solution.py:63
  44.4 14.4 %collective-permute-start.7 = (bf16[10,2,128]{2,1,0:T(2,128)(2,1)S(1)}, bf16[10,2,128]{2,1,0:T(2,128)(2,1)S(1)}, u32[]{:S(2)}, u32[]{:S(2)}) collective-permute-start(bf16[10,2,128]{2,1,0:T(2,128)(2,1)S(1)} %get-tuple-element.41), channel_id=1, source_target_pairs={{0,8},{16,24},{8,0},{24,16},{1,9},{17,25},{9,1},{25,17},{2,10},{18... | collective-permute-start | bytes 15368 | tf_op jit(solution)/shard_map/ppermute | solution.py:80
  46.1 12.7 %collective-permute-start.8 = (bf16[10,2,128]{2,1,0:T(2,128)(2,1)S(1)}, bf16[10,2,128]{2,1,0:T(2,128)(2,1)S(1)}, u32[]{:S(2)}, u32[]{:S(2)}) collective-permute-start(bf16[10,2,128]{2,1,0:T(2,128)(2,1)S(1)} %get-tuple-element.42), channel_id=1, source_target_pairs={{8,16},{16,8},{9,17},{17,9},{10,18},{18,10},{11,19},{19,11},{12,20... | collective-permute-start | bytes 15368 | tf_op jit(solution)/shard_map/ppermute | solution.py:81
  54.1 12.5 %all-to-all-start.1 = ((bf16[8,4,3456]{2,1,0:T(4,128)(2,1)}), bf16[8,4,3456]{2,1,0:T(4,128)(2,1)S(1)}, u32[]{:S(2)}, u32[]{:S(2)}) async-start(bf16[8,4,3456]{2,1,0:T(4,128)(2,1)} %shard_map.57), calls=%async_computation.1 | async-start | bytes 442368 | tf_op jit(solution)/shard_map/all_to_all | solution.py:70
  66.6 18.3 %copy-start.5 = (f32[4,27,128]{2,0,1:T(4,128)S(1)}, f32[4,27,128]{2,0,1:T(4,128)}, u32[]{:S(2)}) copy-start(f32[4,27,128]{2,0,1:T(4,128)} %param.3) | copy-start | bytes 165892
  66.8 18.1 %collective-permute-start.14 = (f32[4,3456]{1,0:T(4,128)S(1)}, f32[4,3456]{1,0:T(4,128)S(1)}, u32[]{:S(2)}, u32[]{:S(2)}) collective-permute-start(f32[4,3456]{1,0:T(4,128)S(1)} %get-tuple-element.48.own_ref), channel_id=1, source_target_pairs={{0,1},{1,2},{2,3},{3,0},{4,5},{5,6},{6,7},{7,4},{8,9},{9,10},{10,1... | collective-permute-start | bytes 165896 | tf_op jit(solution)/shard_map/ppermute | solution.py:63
  66.8 18.1 %collective-permute-start.15 = (f32[4,3456]{1,0:T(4,128)S(1)}, f32[4,3456]{1,0:T(4,128)S(1)}, u32[]{:S(2)}, u32[]{:S(2)}) collective-permute-start(f32[4,3456]{1,0:T(4,128)S(1)} %get-tuple-element.48.own_ref), channel_id=1, source_target_pairs={{0,2},{1,3},{2,0},{3,1},{4,6},{5,7},{6,4},{7,5},{8,10},{9,11},{10,... | collective-permute-start | bytes 165896 | tf_op jit(solution)/shard_map/ppermute | solution.py:63
  68.5 16.4 %collective-permute-start.16 = (f32[4,3456]{1,0:T(4,128)S(1)}, f32[4,3456]{1,0:T(4,128)S(1)}, u32[]{:S(2)}, u32[]{:S(2)}) collective-permute-start(f32[4,3456]{1,0:T(4,128)S(1)} %get-tuple-element.48.own_ref), channel_id=1, source_target_pairs={{0,3},{1,0},{2,1},{3,2},{4,7},{5,4},{6,5},{7,6},{8,11},{9,8},{10,9... | collective-permute-start | bytes 165896 | tf_op jit(solution)/shard_map/ppermute | solution.py:63
